TPU v7x, 8 devices: a whole 2x2x1 slice. The times are simulated.
8 devices in a mesh: dp: 2 (over y, z), ep: 4 (over x, core).
Axes of the slice: x: 2, y: 2, z: 1, core: 2. Of those that a mesh axis runs over, the one named last changes fastest.
Arguments:
- x: bfloat16 [2, 4, 1024, 2048], P('dp', 'ep'), parts along dimension 0
- expert: int32 [2, 4, 1024, 4], P('dp', 'ep'), parts along dimension 0
- slot: int32 [2, 4, 1024, 4], P('dp', 'ep'), parts along dimension 0
- gate: float32 [2, 4, 1024, 4], P('dp', 'ep'), parts along dimension 0
- w_gate: bfloat16 [60, 2048, 1408], P('ep')
- w_up: bfloat16 [60, 2048, 1408], P('ep')
- w_down: bfloat16 [60, 1408, 2048], P('ep')
- s_gate: bfloat16 [2048, 5632], replicated
- s_up: bfloat16 [2048, 5632], replicated
- s_down: bfloat16 [5632, 2048], replicated
Outputs:
- y: bfloat16 [2, 4, 1024, 2048], P('dp', 'ep'), parts along dimension 0
There are 2 independent parts. A program takes and returns all parts, laid end to end along the dimension named above; an argument that names none is the same for every part.
All inputs are finite; a program needn't handle non-finite values.
Results may differ from a plain program's by a relative error of at most 0.009.
Values are sent between devices in bfloat16 or wider.
A program may use at most 2 GiB of HBM per device.

v0:
```python
import functools

import jax
import jax.numpy as jnp
from jax import lax
from jax.experimental import pallas as pl
from jax.experimental.pallas import tpu as pltpu
from jax.sharding import PartitionSpec as P


MIB = 1 << 20
ROW = 16
BLK = 128
F32, BF16 = jnp.float32, jnp.bfloat16


def dot(a, b):
    return jnp.dot(a, b, preferred_element_type=F32)


def cost(flops, nbytes):
    return pl.CostEstimate(flops=int(flops), bytes_accessed=int(nbytes), transcendentals=0)


def shared_body(x_ref, g_ref, u_ref, d_ref, *rest, rows):
    init_ref, y_ref = rest if len(rest) == 2 else (None, rest[0])
    step = pl.program_id(0)
    tokens, width = x_ref.shape[0], g_ref.shape[1]
    depth = d_ref.shape[1]

    @pl.when(step == 0)
    def _():
        if init_ref is None:
            y_ref[...] = jnp.zeros_like(y_ref)
        else:
            y_ref[...] = init_ref[...]

    def one(i, _):
        r = pl.ds(pl.multiple_of(i * rows, rows), rows)
        x = x_ref[r, :]
        hs = []
        for c in range(0, width, 256):
            g = dot(x, g_ref[:, c : c + 256])
            u = dot(x, u_ref[:, c : c + 256])
            hs.append((jax.nn.silu(g) * u).astype(BF16))
        h = jnp.concatenate(hs, axis=1)
        for c in range(0, depth, 256):
            y_ref[r, c : c + 256] += dot(h, d_ref[:, c : c + 256])
        return _

    lax.fori_loop(0, tokens // rows, one, 0)


def shared_expert(x, s_gate, s_up, s_down, first, last, init=None, chunk=512, rows=256):
    tokens, d = x.shape
    once = dict(pipeline_mode=pl.Buffered(1))
    return pl.pallas_call(
        functools.partial(shared_body, rows=rows),
        grid=(last - first,),
        in_specs=[
            pl.BlockSpec((tokens, d), lambda i: (0, 0), **once),
            pl.BlockSpec((d, chunk), lambda i: (0, i + first)),
            pl.BlockSpec((d, chunk), lambda i: (0, i + first)),
            pl.BlockSpec((chunk, d), lambda i: (i + first, 0)),
        ]
        + ([] if init is None else [pl.BlockSpec((tokens, d), lambda i: (0, 0), **once)]),
        out_specs=pl.BlockSpec((tokens, d), lambda i: (0, 0), **once),
        out_shape=jax.ShapeDtypeStruct((tokens, d), F32),
        compiler_params=pltpu.CompilerParams(vmem_limit_bytes=60 * MIB),
        cost_estimate=cost(6 * tokens * d * chunk * (last - first), 6 * d * chunk * (last - first)),
        name="shared",
    )(x, s_gate, s_up, s_down, *(() if init is None else (init,)))


def dispatch_body(nblk_ref, pos_ref, x_ref, z_ref):
    b = pl.program_id(0)

    @pl.when(b < nblk_ref[0])
    def _():
        tokens = x_ref.shape[0]
        row = b * BLK + lax.broadcasted_iota(jnp.int32, (BLK, tokens), 0)
        hit = pos_ref[0:1, :] == row
        for j in range(1, pos_ref.shape[0]):
            hit = hit | (pos_ref[j : j + 1, :] == row)
        p = jnp.where(hit, 1.0, 0.0).astype(BF16)
        for c in range(0, x_ref.shape[1], 256):
            z_ref[:, c : c + 256] = dot(p, x_ref[:, c : c + 256]).astype(BF16)


def dispatch(nblk, pos, x, rows):
    tokens, d = x.shape
    last = lambda b, n: jnp.minimum(b, jnp.maximum(n[0] - 1, 0))
    return pl.pallas_call(
        dispatch_body,
        grid_spec=pltpu.PrefetchScalarGridSpec(
            num_scalar_prefetch=1,
            grid=(rows // BLK,),
            in_specs=[
                pl.BlockSpec(pos.shape, lambda b, n: (0, 0)),
                pl.BlockSpec((tokens, d), lambda b, n: (0, 0)),
            ],
            out_specs=pl.BlockSpec((BLK, d), lambda b, n: (last(b, n), 0)),
        ),
        out_shape=jax.ShapeDtypeStruct((rows, d), BF16),
        compiler_params=pltpu.CompilerParams(vmem_limit_bytes=60 * MIB),
        cost_estimate=cost(2 * tokens * d * rows // 3, 8 * MIB),
        name="dispatch",
    )(nblk, pos, x)


def rows_of(n_ref, e, sources, experts):
    total = 0
    for q in range(sources):
        total = total + n_ref[q * experts + e]
    return total


def gate_up_body(n_ref, off_ref, wg_ref, wu_ref, *rest, experts, sources):
    z_refs, h_ref, zs, sem = rest[:sources], rest[sources], rest[sources + 1], rest[sources + 2]
    e = pl.program_id(0)
    width = wg_ref.shape[1]

    def fetch(e, slot):
        at = 0
        for q in range(sources):
            n = n_ref[q * experts + e]
            off = off_ref[q * experts + e]

            def one(i, _):
                src = pl.ds(pl.multiple_of(off + i * ROW, ROW), ROW)
                dst = pl.ds(pl.multiple_of(at + i * ROW, ROW), ROW)
                pltpu.make_async_copy(z_refs[q].at[src, :], zs.at[slot, dst, :], sem.at[slot]).start()
                return _

            lax.fori_loop(0, n // ROW, one, 0)
            at = at + n

    @pl.when(e == 0)
    def _():
        fetch(0, 0)

    @pl.when(e + 1 < experts)
    def _():
        fetch(e + 1, (e + 1) % 2)

    slot = e % 2
    total = rows_of(n_ref, e, sources, experts)

    def wait(i, _):
        r = pl.ds(0, ROW)
        pltpu.make_async_copy(z_refs[0].at[r, :], zs.at[slot, r, :], sem.at[slot]).wait()
        return _

    lax.fori_loop(0, total // ROW, wait, 0)

    def block(rows):
        z = zs[slot, :rows, :]
        whole = width // 256 * 256
        for c in range(0, whole, 256):
            g = dot(z, wg_ref[:, c : c + 256])
            u = dot(z, wu_ref[:, c : c + 256])
            h_ref[:rows, c : c + 256] = (jax.nn.silu(g) * u).astype(BF16)
        if whole < width:
            left = width - whole
            gu = dot(z, jnp.concatenate([wg_ref[:, whole:], wu_ref[:, whole:]], axis=1))
            h_ref[:rows, whole:] = (jax.nn.silu(gu[:, :left]) * gu[:, left:]).astype(BF16)

    for rows in range(BLK, zs.shape[1] + 1, BLK):
        pl.when((total > rows - BLK) & (total <= rows))(functools.partial(block, rows))


def gate_up(n, off, w_gate, w_up, zs, most):
    experts, d, f = w_gate.shape
    sources = len(zs)
    return pl.pallas_call(
        functools.partial(gate_up_body, experts=experts, sources=sources),
        grid_spec=pltpu.PrefetchScalarGridSpec(
            num_scalar_prefetch=2,
            grid=(experts,),
            in_specs=[
                pl.BlockSpec((None, d, f), lambda e, *_: (e, 0, 0)),
                pl.BlockSpec((None, d, f), lambda e, *_: (e, 0, 0)),
            ]
            + [pl.BlockSpec(memory_space=pl.ANY)] * sources,
            out_specs=pl.BlockSpec((None, most, f), lambda e, *_: (e, 0, 0)),
            scratch_shapes=[
                pltpu.VMEM((2, most, d), BF16),
                pltpu.SemaphoreType.DMA((2,)),
            ],
        ),
        out_shape=jax.ShapeDtypeStruct((experts, most, f), BF16),
        compiler_params=pltpu.CompilerParams(vmem_limit_bytes=60 * MIB),
        cost_estimate=cost(4 * experts * 256 * d * f, 2 * experts * d * f * 2),
        name="gate_up",
    )(n, off, w_gate, w_up, *zs)


def down_body(n_ref, off_ref, k_ref, wd_ref, h_ref, c_ref, *rest, experts, sources, group):
    y_refs, (hb, stage, outs, cb, acc, sem, csem) = rest[:sources], rest[sources:]
    step = pl.program_id(0)

    def c_copy(q):
        return pltpu.make_async_copy(c_ref.at[q], cb.at[q % 2], csem.at[q % 2])

    def h_copy(e, b):
        r = pl.ds(pl.multiple_of(b * BLK, BLK), BLK)
        return pltpu.make_async_copy(h_ref.at[e, r, :], hb.at[e, r, :], sem.at[e])

    @pl.when(step == 0)
    def _():
        def fetch(e, _):
            def one(b, _):
                h_copy(e, b).start()
                return _

            lax.fori_loop(0, pl.cdiv(rows_of(n_ref, e, sources, experts), BLK), one, 0)
            return _

        lax.fori_loop(0, experts, fetch, 0)
        for q in range(2):
            c_copy(sources - 1 - q).start()
        outs[...] = jnp.zeros_like(outs)

    def expert(g, _):
        e = step * group + g
        total = rows_of(n_ref, e, sources, experts)
        blocks = pl.cdiv(total, BLK)

        def arrive(b, _):
            h_copy(e, b).wait()
            return _

        lax.fori_loop(0, blocks, arrive, 0)

        def compute(b, _):
            r = pl.ds(pl.multiple_of(b * BLK, BLK), BLK)
            h = hb[e, r, :]
            for c in range(0, wd_ref.shape[2], 256):
                stage[r, c : c + 256] = dot(h, wd_ref[g, :, c : c + 256]).astype(BF16)
            return _

        lax.fori_loop(0, blocks, compute, 0)

        at = 0
        for q in range(sources):
            n = n_ref[q * experts + e]
            off = off_ref[q * experts + e]

            def move(i, _):
                src = pl.ds(pl.multiple_of(at + i * ROW, ROW), ROW)
                dst = pl.ds(pl.multiple_of(off + i * ROW, ROW), ROW)
                outs[q, dst, :] = stage[src, :]
                return _

            lax.fori_loop(0, n // ROW, move, 0)
            at = at + n
        return _

    lax.fori_loop(0, group, expert, 0)

    @pl.when(step == experts // group - 1)
    def _():
        tokens, columns = acc.shape
        for q in reversed(range(sources)):
            c_copy(q).wait()
            acc[...] = jnp.zeros_like(acc)

            def part(k, _):
                r = pl.ds(pl.multiple_of(k * 256, 256), 256)
                for t in range(0, tokens, 256):
                    cm = cb[q % 2, t : t + 256, r]
                    for c in range(0, columns, 256):
                        acc[t : t + 256, c : c + 256] += dot(cm, outs[q, r, c : c + 256])
                return _

            lax.fori_loop(0, k_ref[q], part, 0)
            y_refs[q][...] = acc[...].astype(y_refs[q].dtype)
            if q >= 2:
                c_copy(q - 2).start()


def down(n, off, k, w_down, h, comb, column, columns, group=3):
    experts, f, d = w_down.shape
    sources, tokens, rows = comb.shape
    most = h.shape[1]
    once = dict(pipeline_mode=pl.Buffered(1))
    return pl.pallas_call(
        functools.partial(down_body, experts=experts, sources=sources, group=group),
        grid_spec=pltpu.PrefetchScalarGridSpec(
            num_scalar_prefetch=3,
            grid=(experts // group,),
            in_specs=[
                pl.BlockSpec((group, f, columns), lambda e, *_: (e, 0, column // columns)),
                pl.BlockSpec(memory_space=pl.ANY),
                pl.BlockSpec(memory_space=pl.ANY),
            ],
            out_specs=[pl.BlockSpec((tokens, columns), lambda e, *_: (0, 0), **once)] * sources,
            scratch_shapes=[
                pltpu.VMEM((experts, most, f), BF16),
                pltpu.VMEM((most, columns), BF16),
                pltpu.VMEM((sources, rows, columns), BF16),
                pltpu.VMEM((2, tokens, rows), BF16),
                pltpu.VMEM((tokens, columns), F32),
                pltpu.SemaphoreType.DMA((experts,)),
                pltpu.SemaphoreType.DMA((2,)),
            ],
        ),
        out_shape=[jax.ShapeDtypeStruct((tokens, columns), F32 if q % 2 == 0 else BF16) for q in range(sources)],
        compiler_params=pltpu.CompilerParams(vmem_limit_bytes=60 * MIB),
        cost_estimate=cost(2 * experts * 256 * f * columns, experts * f * columns * 2),
        name="down",
    )(n, off, k, w_down, h, comb)


def layer(x, expert, slot, gate, w_gate, w_up, w_down, s_gate, s_up, s_down, *, members, experts):
    x, expert, slot, gate = x[0, 0], expert[0, 0], slot[0, 0], gate[0, 0]
    tokens, d = x.shape
    local = w_gate.shape[0]
    slots = 5 * tokens * expert.shape[1] // (4 * experts)
    most_q = pl.cdiv(slots, ROW) * ROW
    rows = pl.cdiv(local * most_q, 256) * 256
    most = pl.cdiv(members * most_q, BLK) * BLK
    me = lax.axis_index("ep")

    def swap(v, q):
        return lax.ppermute(v, "ep", [(i, i ^ q) for i in range(members)])

    mark = (expert * 128 + jnp.minimum(slot, 127)).astype(F32)
    meta = jnp.stack([mark.T, gate.T])
    metas = [meta]
    for q in range(1, members):
        metas.append(swap(meta, q))
    metas = jnp.stack(metas)
    far = swap(x, 2)
    near = swap(x, 1)

    mark = metas[:, 0].astype(jnp.int32)
    where, s = (mark >> 7) - me * local, mark & 127
    ok = (where >= 0) & (where < local) & (s < slots)
    ids = jnp.arange(local, dtype=jnp.int32)
    is_it = (where[:, None] == ids[None, :, None, None]) & ok[:, None]
    n = jnp.max(jnp.where(is_it, s[:, None] + 1, 0), axis=(2, 3))
    n = (n + ROW - 1) // ROW * ROW
    off = jnp.sum(jnp.where(ids[None, :] < ids[:, None], n[:, None, :], 0), axis=2)
    used = jnp.sum(n, axis=1)
    pos = jnp.where(ok, jnp.sum(jnp.where(is_it, off[:, :, None, None], 0), axis=1) + s, -1)
    weight = metas[:, 1].astype(BF16)
    at = jnp.arange(rows, dtype=jnp.int32)
    comb = jnp.zeros((members, tokens, rows), BF16)
    for j in range(pos.shape[1]):
        comb = jnp.where(pos[:, j, :, None] == at, weight[:, j, :, None], comb)

    nf, of = n.reshape(-1), off.reshape(-1)
    nblk = (used + BLK - 1) // BLK
    k = (used + 255) // 256

    def send(q, v):
        return dispatch(nblk[q : q + 1], pos[q], v, rows)

    chunks = s_gate.shape[1] // 512
    cut = chunks * 2 // 3
    y_shared = shared_expert(x, s_gate, s_up, s_down, 0, cut)
    z = [send(0, x), send(1, near)]
    far_near = swap(far, 1)
    z += [send(2, far), send(3, far_near)]
    h = gate_up(nf, of, w_gate, w_up, z, most)

    columns = 512
    own, side, back = [], [], []
    for c in range(0, d, columns):
        y0, y1, y2, y3 = down(nf, of, k, w_down, h, comb, c, columns)
        mine = y2 + swap(y3, 1).astype(F32)
        back.append(swap(mine.astype(BF16), 2))
        side.append(swap(y1, 1))
        own.append(y0)
    y_shared = shared_expert(x, s_gate, s_up, s_down, cut, chunks, y_shared)
    out = [
        (y_shared[:, i * columns : (i + 1) * columns] + own[i] + side[i].astype(F32) + back[i].astype(F32)).astype(BF16)
        for i in range(len(own))
    ]
    return jnp.concatenate(out, axis=1)[None, None]


def solution(mesh):
    members = mesh.shape["ep"]
    tok = P("dp", "ep", None, None)
    w = P("ep", None, None)
    rep = P(None, None)

    def step(x, expert, slot, gate, w_gate, w_up, w_down, s_gate, s_up, s_down):
        body = functools.partial(layer, members=members, experts=w_gate.shape[0])
        return jax.shard_map(
            body,
            mesh=mesh,
            in_specs=(tok, tok, tok, tok, w, w, w, rep, rep, rep),
            out_specs=tok,
            check_vma=False,
        )(x, expert, slot, gate, w_gate, w_up, w_down, s_gate, s_up, s_down)

    return step
```

profile of v0, /device:TPU:0, one launch (start us, length us, event | category | flops | bytes accessed | tf_op | source)
XLA Modules:
  0.0 526.2 jit_solution(10372340713502581487)
XLA Ops:
  0.0 3.3 collective-permute-start.4
  3.3 0.7 convert_bitcast_fusion
  4.1 0.7 fusion.26
  4.9 1.8 collective-permute-start.2
  6.7 0.3 collective-permute-start.3
  7.0 88.1 %collective-permute-done.1 = f32[2,4,1024]{2,1,0:T(4,128)S(1)} collective-permute-done((f32[2,4,1024]{2,1,0:T(4,128)S(1)}, f32[2,4,1024]{2,1,0:T(4,128)S(1)}, u32[]{:S(2)}, u32[]{:S(2)}) %collective-permute-start.1) | collective-permute-done | bytes 32800 | tf_op jit(solution)/shard_map/ppermute | solution.py:326
  95.2 0.1 and_bitcast_fusion
  95.3 1.2 select_reduce_fusion.1
  96.5 0.1 fusion.27
  96.6 0.4 select_reduce_fusion.2
  97.0 0.1 copy.20
  97.1 0.7 reshape.54.off_ref
  97.7 0.1 sub.43
  97.8 0.5 and_select_fusion
  98.3 0.6 fusion.31
  99.0 0.5 select_reduce_fusion
  99.5 0.1 fusion.17
  99.6 0.6 slice_bitcast_fusion
  100.2 8.1 %dispatch.4.rest_0_ = bf16[1536,2048]{1,0:T(8,128)(2,1)} custom-call(s32[1]{0:T(128)} %get-tuple-element.65.nblk_ref, s32[4,1024]{1,0:T(4,128)} %get-tuple-element.54.pos_ref, bf16[1024,2048]{1,0:T(8,128)(2,1)} %bitcast.70), custom_call_target="tpu_custom_call" | custom-call | flops 2147483648 | bytes 8388608 | tf_op jit(solution)/shard_map/dispatch/pallas_call | solution.py:93
  108.3 0.6 fusion.25.n_ref
  108.9 0.1 fusion.30
  109.1 1.8 collective-permute-start.5
  110.9 16.2 %fusion.c_ref = bf16[4,1024,1536]{2,1,0:T(8,128)(2,1)} fusion(s32[4,1024]{1,0:T(4,128)S(1)} %get-tuple-element.68, s32[4,1024]{1,0:T(4,128)S(1)} %get-tuple-element.69, s32[4,1024]{1,0:T(4,128)S(1)} %get-tuple-element.70, s32[4,1024]{1,0:T(4,128)S(1)} %get-tuple-element.71, bf16[4,1024]{1,0:T(4,128)(2,1)S(1)} %get-tuple-element.72, ...), kind=kLoop, calls=%fused_computation.4 | loop fusion | flops 50331648 | bytes 12681216 | tf_op jit(solution)/shard_map/jit(_where)/select_n | solution.py:351
  127.0 8.8 %dispatch.6.rest_2_ = bf16[1536,2048]{1,0:T(8,128)(2,1)} custom-call(s32[1]{0:T(128)} %get-tuple-element.63.nblk_ref, s32[4,1024]{1,0:T(4,128)} %get-tuple-element.52.pos_ref, bf16[1024,2048]{1,0:T(8,128)(2,1)} %collective-permute-done.4.x_ref), custom_call_target="tpu_custom_call" | custom-call | flops 2147483648 | bytes 8388608 | tf_op jit(solution)/shard_map/dispatch/pallas_call | solution.py:93
  135.8 8.0 %dispatch.5.rest_1_ = bf16[1536,2048]{1,0:T(8,128)(2,1)} custom-call(s32[1]{0:T(128)} %get-tuple-element.64.nblk_ref, s32[4,1024]{1,0:T(4,128)} %get-tuple-element.53.pos_ref, bf16[1024,2048]{1,0:T(8,128)(2,1)} %collective-permute-done.3.x_ref), custom_call_target="tpu_custom_call" | custom-call | flops 2147483648 | bytes 8388608 | tf_op jit(solution)/shard_map/dispatch/pallas_call | solution.py:93
  143.8 8.8 %dispatch.7.rest_3_ = bf16[1536,2048]{1,0:T(8,128)(2,1)} custom-call(s32[1]{0:T(128)} %get-tuple-element.62.nblk_ref, s32[4,1024]{1,0:T(4,128)} %get-tuple-element.51.pos_ref, bf16[1024,2048]{1,0:T(8,128)(2,1)} %collective-permute-done.5.x_ref), custom_call_target="tpu_custom_call" | custom-call | flops 2147483648 | bytes 8388608 | tf_op jit(solution)/shard_map/dispatch/pallas_call | solution.py:93
  152.6 73.5 %gate_up.1.h_ref = bf16[15,384,1408]{2,1,0:T(8,128)(2,1)} custom-call(s32[60]{0:T(128)} %fusion.25.n_ref, s32[60]{0:T(128)} %reshape.54.off_ref, bf16[15,2048,1408]{2,1,0:T(8,128)(2,1)} %wg_ref.1, bf16[15,2048,1408]{2,1,0:T(8,128)(2,1)} %wu_ref.1, bf16[1536,2048]{1,0:T(8,128)(2,1)} %dispatch.4.rest_0_, bf16[1536,2048]{1,0:T(8,128)(2,1)} %dispatch.5.rest_1_, ...), custom_call_target="tpu_custom_call" | custom-call | flops 44291850240 | bytes 173015040 | tf_op jit(solution)/shard_map/gate_up/pallas_call | solution.py:175
  226.0 27.3 %down.5 = (f32[1024,512]{1,0:T(8,128)}, bf16[1024,512]{1,0:T(8,128)(2,1)}, f32[1024,512]{1,0:T(8,128)}, bf16[1024,512]{1,0:T(8,128)(2,1)}) custom-call(s32[60]{0:T(128)} %fusion.25.n_ref, s32[60]{0:T(128)} %reshape.54.off_ref, s32[4]{0:T(128)} %get-tuple-element.67.k_ref, bf16[15,1408,2048]{2,1,0:T(8,128)(2,1)} %wd_ref.7, ...), custom_call_target="tpu_custom_call" | custom-call | flops 5536481280 | bytes 21626880 | tf_op jit(solution)/shard_map/down/pallas_call | solution.py:287
  253.4 27.0 %down.6 = (f32[1024,512]{1,0:T(8,128)}, bf16[1024,512]{1,0:T(8,128)(2,1)}, f32[1024,512]{1,0:T(8,128)}, bf16[1024,512]{1,0:T(8,128)(2,1)}) custom-call(s32[60]{0:T(128)} %fusion.25.n_ref, s32[60]{0:T(128)} %reshape.54.off_ref, s32[4]{0:T(128)} %get-tuple-element.67.k_ref, bf16[15,1408,2048]{2,1,0:T(8,128)(2,1)} %wd_ref.7, ...), custom_call_target="tpu_custom_call" | custom-call | flops 5536481280 | bytes 21626880 | tf_op jit(solution)/shard_map/down/pallas_call | solution.py:287
  280.4 27.0 %down.7 = (f32[1024,512]{1,0:T(8,128)}, bf16[1024,512]{1,0:T(8,128)(2,1)}, f32[1024,512]{1,0:T(8,128)}, bf16[1024,512]{1,0:T(8,128)(2,1)}) custom-call(s32[60]{0:T(128)} %fusion.25.n_ref, s32[60]{0:T(128)} %reshape.54.off_ref, s32[4]{0:T(128)} %get-tuple-element.67.k_ref, bf16[15,1408,2048]{2,1,0:T(8,128)(2,1)} %wd_ref.7, ...), custom_call_target="tpu_custom_call" | custom-call | flops 5536481280 | bytes 21626880 | tf_op jit(solution)/shard_map/down/pallas_call | solution.py:287
  307.4 27.3 %down.4 = (f32[1024,512]{1,0:T(8,128)}, bf16[1024,512]{1,0:T(8,128)(2,1)}, f32[1024,512]{1,0:T(8,128)}, bf16[1024,512]{1,0:T(8,128)(2,1)}) custom-call(s32[60]{0:T(128)} %fusion.25.n_ref, s32[60]{0:T(128)} %reshape.54.off_ref, s32[4]{0:T(128)} %get-tuple-element.67.k_ref, bf16[15,1408,2048]{2,1,0:T(8,128)(2,1)} %wd_ref.7, ...), custom_call_target="tpu_custom_call" | custom-call | flops 5536481280 | bytes 21626880 | tf_op jit(solution)/shard_map/down/pallas_call | solution.py:287
  334.7 18.4 %collective-permute-start.10 = (bf16[1024,512]{1,0:T(8,128)(2,1)}, bf16[1024,512]{1,0:T(8,128)(2,1)}, u32[]{:S(2)}, u32[]{:S(2)}) collective-permute-start(bf16[1024,512]{1,0:T(8,128)(2,1)} %get-tuple-element.28), channel_id=1, source_target_pairs={{0,1},{1,0},{2,3},{3,2},{4,5},{5,4},{6,7},{7,6}} | collective-permute-start | bytes 3145736 | tf_op jit(solution)/shard_map/ppermute | solution.py:326
  353.1 0.5 collective-permute-start.16
  353.6 59.1 %shared.2.rest_0_ = f32[1024,2048]{1,0:T(8,128)} custom-call(bf16[1024,2048]{1,0:T(8,128)(2,1)} %bitcast.71, bf16[2048,5632]{1,0:T(8,128)(2,1)} %g_ref.3, bf16[2048,5632]{1,0:T(8,128)(2,1)} %u_ref.3, bf16[5632,2048]{1,0:T(8,128)(2,1)} %d_ref.3), custom_call_target="tpu_custom_call" | custom-call | flops 45097156608 | bytes 44040192 | tf_op jit(solution)/shard_map/shared/pallas_call | solution.py:57
  412.8 0.5 collective-permute-start.12
  413.3 0.5 collective-permute-start.9
  413.8 2.7 add_convert_fusion.2
  416.5 2.7 add_convert_fusion.1
  419.2 2.6 add_convert_fusion
  421.8 2.6 add_convert_fusion.3
  424.4 2.0 collective-permute-start.14
  426.5 2.0 collective-permute-start.8
  428.5 39.7 %shared.3 = f32[1024,2048]{1,0:T(8,128)} custom-call(bf16[1024,2048]{1,0:T(8,128)(2,1)} %bitcast.72, bf16[2048,5632]{1,0:T(8,128)(2,1)} %g_ref.3, bf16[2048,5632]{1,0:T(8,128)(2,1)} %u_ref.3, bf16[5632,2048]{1,0:T(8,128)(2,1)} %d_ref.3, f32[1024,2048]{1,0:T(8,128)} %shared.2.rest_0_), custom_call_target="tpu_custom_call" | custom-call | flops 25769803776 | bytes 25165824 | tf_op jit(solution)/shard_map/shared/pallas_call | solution.py:57
  468.2 2.4 collective-permute-done.14
  470.6 22.5 %collective-permute-done.17 = bf16[1024,512]{1,0:T(8,128)(2,1)} collective-permute-done((bf16[1024,512]{1,0:T(8,128)(2,1)}, bf16[1024,512]{1,0:T(8,128)(2,1)}, u32[]{:S(2)}, u32[]{:S(2)}) %collective-permute-start.17) | collective-permute-done | bytes 1048608 | tf_op jit(solution)/shard_map/ppermute | solution.py:326
  493.1 22.0 %collective-permute-done.8 = bf16[1024,512]{1,0:T(8,128)(2,1)} collective-permute-done((bf16[1024,512]{1,0:T(8,128)(2,1)}, bf16[1024,512]{1,0:T(8,128)(2,1)}, u32[]{:S(2)}, u32[]{:S(2)}) %collective-permute-start.8) | collective-permute-done | bytes 1048608 | tf_op jit(solution)/shard_map/ppermute | solution.py:326
  515.1 8.7 %fusion.15 = (bf16[1024,512]{1,0:T(8,128)(2,1)S(1)}, bf16[1024,512]{1,0:T(8,128)(2,1)S(1)}, bf16[1024,512]{1,0:T(8,128)(2,1)S(1)}, bf16[1024,512]{1,0:T(8,128)(2,1)S(1)}) fusion(f32[1024,512]{1,0:T(8,128)} %get-tuple-element.21, f32[1024,2048]{1,0:T(8,128)} %shared.3, bf16[1024,512]{1,0:T(8,128)(2,1)} %collective-permute-done.8, ...), kind=kLoop, calls=%fused_computation.24 | loop fusion | flops 12582912 | bytes 29360128 | tf_op jit(solution)/shard_map/convert_element_type | solution.py:378
  523.8 2.3 maximum_bitcast_fusion
  (41 shorter events, 0.5 us)
Async XLA Ops:
  0.0 109.1 %collective-permute-start.4 = (bf16[1024,2048]{1,0:T(8,128)(2,1)}, bf16[1024,2048]{1,0:T(8,128)(2,1)}, u32[]{:S(2)}, u32[]{:S(2)}) collective-permute-start(bf16[1024,2048]{1,0:T(8,128)(2,1)} %bitcast.68), channel_id=1, source_target_pairs={{0,2},{1,3},{2,0},{3,1},{4,6},{5,7},{6,4},{7,5}} | collective-permute-start | bytes 12582920 | tf_op jit(solution)/shard_map/ppermute | solution.py:326
  4.8 2.2 collective-permute-start
  4.8 90.3 %collective-permute-start.1 = (f32[2,4,1024]{2,1,0:T(4,128)S(1)}, f32[2,4,1024]{2,1,0:T(4,128)S(1)}, u32[]{:S(2)}, u32[]{:S(2)}) collective-permute-start(f32[2,4,1024]{2,1,0:T(4,128)S(1)} %get-tuple-element.60), channel_id=1, source_target_pairs={{0,2},{1,3},{2,0},{3,1},{4,6},{5,7},{6,4},{7,5}} | collective-permute-start | bytes 98312 | tf_op jit(solution)/shard_map/ppermute | solution.py:326
  4.9 90.3 %collective-permute-start.2 = (f32[2,4,1024]{2,1,0:T(4,128)S(1)}, f32[2,4,1024]{2,1,0:T(4,128)S(1)}, u32[]{:S(2)}, u32[]{:S(2)}) collective-permute-start(f32[2,4,1024]{2,1,0:T(4,128)S(1)} %get-tuple-element.60), channel_id=1, source_target_pairs={{0,3},{1,2},{2,1},{3,0},{4,7},{5,6},{6,5},{7,4}} | collective-permute-start | bytes 98312 | tf_op jit(solution)/shard_map/ppermute | solution.py:326
  6.7 129.1 %collective-permute-start.3 = (bf16[1024,2048]{1,0:T(8,128)(2,1)}, bf16[1024,2048]{1,0:T(8,128)(2,1)}, u32[]{:S(2)}, u32[]{:S(2)}) collective-permute-start(bf16[1024,2048]{1,0:T(8,128)(2,1)} %bitcast.69), channel_id=1, source_target_pairs={{0,1},{1,0},{2,3},{3,2},{4,5},{5,4},{6,7},{7,6}} | collective-permute-start | bytes 12582920 | tf_op jit(solution)/shard_map/ppermute | solution.py:326
  109.1 34.7 %collective-permute-start.5 = (bf16[1024,2048]{1,0:T(8,128)(2,1)}, bf16[1024,2048]{1,0:T(8,128)(2,1)}, u32[]{:S(2)}, u32[]{:S(2)}) collective-permute-start(bf16[1024,2048]{1,0:T(8,128)(2,1)} %collective-permute-done.4.x_ref), channel_id=1, source_target_pairs={{0,1},{1,0},{2,3},{3,2},{4,5},{5,4},{6,7},{7,6}} | collective-permute-start | bytes 12582920 | tf_op jit(solution)/shard_map/ppermute | solution.py:326
  334.7 78.5 %collective-permute-start.10 = (bf16[1024,512]{1,0:T(8,128)(2,1)}, bf16[1024,512]{1,0:T(8,128)(2,1)}, u32[]{:S(2)}, u32[]{:S(2)}) collective-permute-start(bf16[1024,512]{1,0:T(8,128)(2,1)} %get-tuple-element.28), channel_id=1, source_target_pairs={{0,1},{1,0},{2,3},{3,2},{4,5},{5,4},{6,7},{7,6}} | collective-permute-start | bytes 3145736 | tf_op jit(solution)/shard_map/ppermute | solution.py:326
  353.1 60.2 %collective-permute-start.13 = (bf16[1024,512]{1,0:T(8,128)(2,1)}, bf16[1024,512]{1,0:T(8,128)(2,1)}, u32[]{:S(2)}, u32[]{:S(2)}) collective-permute-start(bf16[1024,512]{1,0:T(8,128)(2,1)} %get-tuple-element.32), channel_id=1, source_target_pairs={{0,1},{1,0},{2,3},{3,2},{4,5},{5,4},{6,7},{7,6}} | collective-permute-start | bytes 3145736 | tf_op jit(solution)/shard_map/ppermute | solution.py:326
  353.1 66.0 %collective-permute-start.16 = (bf16[1024,512]{1,0:T(8,128)(2,1)}, bf16[1024,512]{1,0:T(8,128)(2,1)}, u32[]{:S(2)}, u32[]{:S(2)}) collective-permute-start(bf16[1024,512]{1,0:T(8,128)(2,1)} %get-tuple-element.36), channel_id=1, source_target_pairs={{0,1},{1,0},{2,3},{3,2},{4,5},{5,4},{6,7},{7,6}} | collective-permute-start | bytes 3145736 | tf_op jit(solution)/shard_map/ppermute | solution.py:326
  353.6 60.2 %copy-start.3 = (f32[1024,512]{1,0:T(8,128)S(1)}, f32[1024,512]{1,0:T(8,128)}, u32[]{:S(2)}) copy-start(f32[1024,512]{1,0:T(8,128)} %get-tuple-element.27) | copy-start | bytes 6291460
  353.6 68.2 %collective-permute-start.7 = (bf16[1024,512]{1,0:T(8,128)(2,1)}, bf16[1024,512]{1,0:T(8,128)(2,1)}, u32[]{:S(2)}, u32[]{:S(2)}) collective-permute-start(bf16[1024,512]{1,0:T(8,128)(2,1)} %get-tuple-element.24), channel_id=1, source_target_pairs={{0,1},{1,0},{2,3},{3,2},{4,5},{5,4},{6,7},{7,6}} | collective-permute-start | bytes 3145736 | tf_op jit(solution)/shard_map/ppermute | solution.py:326
  412.8 3.7 copy-start.4
  412.8 11.6 %collective-permute-start.12 = (bf16[1024,512]{1,0:T(8,128)(2,1)}, bf16[1024,512]{1,0:T(8,128)(2,1)S(1)}, u32[]{:S(2)}, u32[]{:S(2)}) collective-permute-start(bf16[1024,512]{1,0:T(8,128)(2,1)} %get-tuple-element.30), channel_id=1, source_target_pairs={{0,1},{1,0},{2,3},{3,2},{4,5},{5,4},{6,7},{7,6}} | collective-permute-start | bytes 3145736 | tf_op jit(solution)/shard_map/ppermute | solution.py:326
  413.2 13.2 %collective-permute-start.15 = (bf16[1024,512]{1,0:T(8,128)(2,1)}, bf16[1024,512]{1,0:T(8,128)(2,1)}, u32[]{:S(2)}, u32[]{:S(2)}) collective-permute-start(bf16[1024,512]{1,0:T(8,128)(2,1)} %get-tuple-element.34), channel_id=1, source_target_pairs={{0,1},{1,0},{2,3},{3,2},{4,5},{5,4},{6,7},{7,6}} | collective-permute-start | bytes 3145736 | tf_op jit(solution)/shard_map/ppermute | solution.py:326
  413.3 13.2 %collective-permute-start.9 = (bf16[1024,512]{1,0:T(8,128)(2,1)}, bf16[1024,512]{1,0:T(8,128)(2,1)}, u32[]{:S(2)}, u32[]{:S(2)}) collective-permute-start(bf16[1024,512]{1,0:T(8,128)(2,1)} %get-tuple-element.26), channel_id=1, source_target_pairs={{0,1},{1,0},{2,3},{3,2},{4,5},{5,4},{6,7},{7,6}} | collective-permute-start | bytes 3145736 | tf_op jit(solution)/shard_map/ppermute | solution.py:326
  413.8 5.4 %copy-start.2 = (f32[1024,512]{1,0:T(8,128)S(1)}, f32[1024,512]{1,0:T(8,128)}, u32[]{:S(2)}) copy-start(f32[1024,512]{1,0:T(8,128)} %get-tuple-element.35) | copy-start | bytes 6291460
  416.5 5.3 %copy-start.1 = (f32[1024,512]{1,0:T(8,128)S(1)}, f32[1024,512]{1,0:T(8,128)}, u32[]{:S(2)}) copy-start(f32[1024,512]{1,0:T(8,128)} %get-tuple-element.23) | copy-start | bytes 6291460
  419.2 49.0 %collective-permute-start.6 = (bf16[1024,512]{1,0:T(8,128)(2,1)}, bf16[1024,512]{1,0:T(8,128)(2,1)}, u32[]{:S(2)}, u32[]{:S(2)}) collective-permute-start(bf16[1024,512]{1,0:T(8,128)(2,1)} %get-tuple-element.22), channel_id=1, source_target_pairs={{0,1},{1,0},{2,3},{3,2},{4,5},{5,4},{6,7},{7,6}} | collective-permute-start | bytes 3145736 | tf_op jit(solution)/shard_map/ppermute | solution.py:326
  421.8 46.4 %collective-permute-start.11 = (bf16[1024,512]{1,0:T(8,128)(2,1)}, bf16[1024,512]{1,0:T(8,128)(2,1)}, u32[]{:S(2)}, u32[]{:S(2)}) collective-permute-start(bf16[1024,512]{1,0:T(8,128)(2,1)} %add_convert_fusion.2), channel_id=1, source_target_pairs={{0,2},{1,3},{2,0},{3,1},{4,6},{5,7},{6,4},{7,5}} | collective-permute-start | bytes 3145736 | tf_op jit(solution)/shard_map/ppermute | solution.py:326
  424.4 90.7 %copy-start = (f32[1024,512]{1,0:T(8,128)S(1)}, f32[1024,512]{1,0:T(8,128)}, u32[]{:S(2)}) copy-start(f32[1024,512]{1,0:T(8,128)} %get-tuple-element.25) | copy-start | bytes 6291460
  424.4 46.2 %collective-permute-start.14 = (bf16[1024,512]{1,0:T(8,128)(2,1)}, bf16[1024,512]{1,0:T(8,128)(2,1)}, u32[]{:S(2)}, u32[]{:S(2)}) collective-permute-start(bf16[1024,512]{1,0:T(8,128)(2,1)} %add_convert_fusion.1), channel_id=1, source_target_pairs={{0,2},{1,3},{2,0},{3,1},{4,6},{5,7},{6,4},{7,5}} | collective-permute-start | bytes 3145736 | tf_op jit(solution)/shard_map/ppermute | solution.py:326
  426.4 66.7 %collective-permute-start.17 = (bf16[1024,512]{1,0:T(8,128)(2,1)}, bf16[1024,512]{1,0:T(8,128)(2,1)}, u32[]{:S(2)}, u32[]{:S(2)}) collective-permute-start(bf16[1024,512]{1,0:T(8,128)(2,1)} %add_convert_fusion), channel_id=1, source_target_pairs={{0,2},{1,3},{2,0},{3,1},{4,6},{5,7},{6,4},{7,5}} | collective-permute-start | bytes 3145736 | tf_op jit(solution)/shard_map/ppermute | solution.py:326
  426.5 88.6 %collective-permute-start.8 = (bf16[1024,512]{1,0:T(8,128)(2,1)}, bf16[1024,512]{1,0:T(8,128)(2,1)}, u32[]{:S(2)}, u32[]{:S(2)}) collective-permute-start(bf16[1024,512]{1,0:T(8,128)(2,1)} %add_convert_fusion.3), channel_id=1, source_target_pairs={{0,2},{1,3},{2,0},{3,1},{4,6},{5,7},{6,4},{7,5}} | collective-permute-start | bytes 3145736 | tf_op jit(solution)/shard_map/ppermute | solution.py:326
where the time goes:
time: 527 us; the launch traced here: 526 us
  Pallas kernels  315 us (60%)
  waiting for transfers between devices  135 us (26%)
  other arithmetic  42.8 us (8%)
  starting transfers between devices  31.3 us (6%)
    ppermute x18, waiting for transfers between devices, swap(): return lax.ppermute(v, 'ep', [(i, i ^ q) for i in range(members)])  135 us
    pallas_call x4, Pallas kernels, down(): pl.pallas_call(functools.partial(down_body, experts=experts, sources=sour...  109 us
    pallas_call x2, Pallas kernels, shared_expert(): pl.pallas_call(functools.partial(shared_body, rows=rows), grid=(last - fi...  98.9 us
    pallas_call x1, Pallas kernels, gate_up(): pl.pallas_call(functools.partial(gate_up_body, experts=experts, sources=s...  73.5 us
    pallas_call x4, Pallas kernels, dispatch(): pl.pallas_call(dispatch_body, grid_spec=pltpu.PrefetchScalarGridSpec(num_...  33.6 us
    ppermute x18, starting transfers between devices, swap(): return lax.ppermute(v, 'ep', [(i, i ^ q) for i in range(members)])  31.3 us
    select_n x1, other arithmetic, layer(): comb = jnp.where(pos[:, j, :, None] == at, weight[:, j, :, None], comb)  16.2 us
    convert_element_type x4, other arithmetic, layer(): back.append(swap(mine.astype(BF16), 2))  10.6 us
  transfers between devices with their start and end apart: 18, of which 4 were waited for; matrix products, arithmetic and copies ran while one was open for 6% of the time, Pallas kernels for 24%

commit v1 on v0

--- a/solution.py
+++ b/solution.py
@@ -72,34 +72,40 @@
     )(x, s_gate, s_up, s_down, *(() if init is None else (init,)))
 
 
-def dispatch_body(nblk_ref, pos_ref, x_ref, z_ref):
-    b = pl.program_id(0)
-
-    @pl.when(b < nblk_ref[0])
-    def _():
-        tokens = x_ref.shape[0]
-        row = b * BLK + lax.broadcasted_iota(jnp.int32, (BLK, tokens), 0)
-        hit = pos_ref[0:1, :] == row
-        for j in range(1, pos_ref.shape[0]):
-            hit = hit | (pos_ref[j : j + 1, :] == row)
-        p = jnp.where(hit, 1.0, 0.0).astype(BF16)
-        for c in range(0, x_ref.shape[1], 256):
-            z_ref[:, c : c + 256] = dot(p, x_ref[:, c : c + 256]).astype(BF16)
-
-
-def dispatch(nblk, pos, x, rows):
+def gather_block(pos_ref, x, z, b, out):
+    tokens = x.shape[0]
+    row = b * BLK + lax.broadcasted_iota(jnp.int32, (BLK, tokens), 0)
+    hit = pos_ref[0:1, :] == row
+    for j in range(1, pos_ref.shape[0]):
+        hit = hit | (pos_ref[j : j + 1, :] == row)
+    p = jnp.where(hit, 1.0, 0.0).astype(BF16)
+    for c in range(0, x.shape[1], 256):
+        z[out, c : c + 256] = dot(p, x[:, c : c + 256]).astype(BF16)
+
+
+def dispatch_body(nblk_ref, pos_ref, x_ref, z_ref, *, group):
+    step = pl.program_id(0)
+
+    def one(i, _):
+        gather_block(pos_ref, x_ref, z_ref, step * group + i, pl.ds(pl.multiple_of(i * BLK, BLK), BLK))
+        return _
+
+    lax.fori_loop(0, jnp.clip(nblk_ref[0] - step * group, 0, group), one, 0)
+
+
+def dispatch(nblk, pos, x, rows, group=4):
     tokens, d = x.shape
-    last = lambda b, n: jnp.minimum(b, jnp.maximum(n[0] - 1, 0))
+    last = lambda b, n: jnp.minimum(b, jnp.maximum(pl.cdiv(n[0], group) - 1, 0))
     return pl.pallas_call(
-        dispatch_body,
+        functools.partial(dispatch_body, group=group),
         grid_spec=pltpu.PrefetchScalarGridSpec(
             num_scalar_prefetch=1,
-            grid=(rows // BLK,),
+            grid=(rows // (BLK * group),),
             in_specs=[
                 pl.BlockSpec(pos.shape, lambda b, n: (0, 0)),
                 pl.BlockSpec((tokens, d), lambda b, n: (0, 0)),
             ],
-            out_specs=pl.BlockSpec((BLK, d), lambda b, n: (last(b, n), 0)),
+            out_specs=pl.BlockSpec((BLK * group, d), lambda b, n: (last(b, n), 0)),
         ),
         out_shape=jax.ShapeDtypeStruct((rows, d), BF16),
         compiler_params=pltpu.CompilerParams(vmem_limit_bytes=60 * MIB),
@@ -115,46 +121,67 @@
     return total
 
 
-def gate_up_body(n_ref, off_ref, wg_ref, wu_ref, *rest, experts, sources):
-    z_refs, h_ref, zs, sem = rest[:sources], rest[sources], rest[sources + 1], rest[sources + 2]
+def gate_up_body(n_ref, off_ref, nblk_ref, wg_ref, wu_ref, *rest, experts, ready, late, halves):
+    sources = ready + late
+    pos_refs, rest = rest[:late], rest[late:]
+    x_refs, rest = rest[: late * halves], rest[late * halves :]
+    z_refs, (h_ref, xv, zv, zs, xsem, zsem) = rest[:ready], rest[ready:]
     e = pl.program_id(0)
     width = wg_ref.shape[1]
 
-    def fetch(e, slot):
-        at = 0
-        for q in range(sources):
-            n = n_ref[q * experts + e]
-            off = off_ref[q * experts + e]
-
-            def one(i, _):
-                src = pl.ds(pl.multiple_of(off + i * ROW, ROW), ROW)
-                dst = pl.ds(pl.multiple_of(at + i * ROW, ROW), ROW)
-                pltpu.make_async_copy(z_refs[q].at[src, :], zs.at[slot, dst, :], sem.at[slot]).start()
-                return _
-
-            lax.fori_loop(0, n // ROW, one, 0)
-            at = at + n
+    def x_copy(i, j):
+        size = x_refs[0].shape[0]
+        return pltpu.make_async_copy(x_refs[i * halves + j], xv.at[i, pl.ds(j * size, size), :], xsem.at[i, j])
+
+    def z_copy(q, b):
+        r = pl.ds(pl.multiple_of(b * BLK, BLK), BLK)
+        return pltpu.make_async_copy(z_refs[q].at[r, :], zv.at[q, r, :], zsem.at[q])
 
     @pl.when(e == 0)
     def _():
-        fetch(0, 0)
-
-    @pl.when(e + 1 < experts)
-    def _():
-        fetch(e + 1, (e + 1) % 2)
-
-    slot = e % 2
-    total = rows_of(n_ref, e, sources, experts)
-
-    def wait(i, _):
-        r = pl.ds(0, ROW)
-        pltpu.make_async_copy(z_refs[0].at[r, :], zs.at[slot, r, :], sem.at[slot]).wait()
-        return _
-
-    lax.fori_loop(0, total // ROW, wait, 0)
+        for i in range(late):
+            for j in range(halves):
+                x_copy(i, j).start()
+
+        def each(q, act):
+            def one(b, _):
+                act(z_copy(q, b))
+                return _
+
+            lax.fori_loop(0, nblk_ref[q], one, 0)
+
+        for q in range(ready):
+            each(q, lambda c: c.start())
+        for i in range(late):
+            for j in range(halves):
+                x_copy(i, j).wait()
+            q = ready + i
+
+            def one(b, _):
+                gather_block(pos_refs[i], xv.at[i], zv.at[q], b, pl.ds(pl.multiple_of(b * BLK, BLK), BLK))
+                return _
+
+            lax.fori_loop(0, nblk_ref[q], one, 0)
+        for q in range(ready):
+            each(q, lambda c: c.wait())
+
+    at = 0
+    for q in range(sources):
+        n = n_ref[q * experts + e]
+        off = off_ref[q * experts + e]
+
+        def move(i, _):
+            src = pl.ds(pl.multiple_of(off + i * ROW, ROW), ROW)
+            dst = pl.ds(pl.multiple_of(at + i * ROW, ROW), ROW)
+            zs[dst, :] = zv[q, src, :]
+            return _
+
+        lax.fori_loop(0, n // ROW, move, 0)
+        at = at + n
+    total = at
 
     def block(rows):
-        z = zs[slot, :rows, :]
+        z = zs[:rows, :]
         whole = width // 256 * 256
         for c in range(0, whole, 256):
             g = dot(z, wg_ref[:, c : c + 256])
@@ -165,38 +192,43 @@
             gu = dot(z, jnp.concatenate([wg_ref[:, whole:], wu_ref[:, whole:]], axis=1))
             h_ref[:rows, whole:] = (jax.nn.silu(gu[:, :left]) * gu[:, left:]).astype(BF16)
 
-    for rows in range(BLK, zs.shape[1] + 1, BLK):
+    for rows in range(BLK, zs.shape[0] + 1, BLK):
         pl.when((total > rows - BLK) & (total <= rows))(functools.partial(block, rows))
 
 
-def gate_up(n, off, w_gate, w_up, zs, most):
+def gate_up(n, off, nblk, w_gate, w_up, pos, xs, zs, most):
     experts, d, f = w_gate.shape
-    sources = len(zs)
+    ready, late, halves = len(zs), len(xs), len(xs[0])
+    rows, tokens = zs[0].shape[0], sum(v.shape[0] for v in xs[0])
     return pl.pallas_call(
-        functools.partial(gate_up_body, experts=experts, sources=sources),
+        functools.partial(gate_up_body, experts=experts, ready=ready, late=late, halves=halves),
         grid_spec=pltpu.PrefetchScalarGridSpec(
-            num_scalar_prefetch=2,
+            num_scalar_prefetch=3,
             grid=(experts,),
             in_specs=[
                 pl.BlockSpec((None, d, f), lambda e, *_: (e, 0, 0)),
                 pl.BlockSpec((None, d, f), lambda e, *_: (e, 0, 0)),
             ]
-            + [pl.BlockSpec(memory_space=pl.ANY)] * sources,
+            + [pl.BlockSpec(p.shape, lambda e, *_: (0, 0)) for p in pos]
+            + [pl.BlockSpec(memory_space=pl.ANY)] * (late * halves + ready),
             out_specs=pl.BlockSpec((None, most, f), lambda e, *_: (e, 0, 0)),
             scratch_shapes=[
-                pltpu.VMEM((2, most, d), BF16),
-                pltpu.SemaphoreType.DMA((2,)),
+                pltpu.VMEM((late, tokens, d), BF16),
+                pltpu.VMEM((ready + late, rows, d), BF16),
+                pltpu.VMEM((most, d), BF16),
+                pltpu.SemaphoreType.DMA((late, halves)),
+                pltpu.SemaphoreType.DMA((ready,)),
             ],
         ),
         out_shape=jax.ShapeDtypeStruct((experts, most, f), BF16),
-        compiler_params=pltpu.CompilerParams(vmem_limit_bytes=60 * MIB),
+        compiler_params=pltpu.CompilerParams(vmem_limit_bytes=67_043_328),
         cost_estimate=cost(4 * experts * 256 * d * f, 2 * experts * d * f * 2),
         name="gate_up",
-    )(n, off, w_gate, w_up, *zs)
+    )(n, off, nblk, w_gate, w_up, *pos, *[v for x in xs for v in x], *zs)
 
 
 def down_body(n_ref, off_ref, k_ref, wd_ref, h_ref, c_ref, *rest, experts, sources, group):
-    y_refs, (hb, stage, outs, cb, acc, sem, csem) = rest[:sources], rest[sources:]
+    y_refs, (hb, stage, outs, cb, sem, csem) = rest[:sources], rest[sources:]
     step = pl.program_id(0)
 
     def c_copy(q):
@@ -232,14 +264,11 @@
 
         lax.fori_loop(0, blocks, arrive, 0)
 
-        def compute(b, _):
-            r = pl.ds(pl.multiple_of(b * BLK, BLK), BLK)
-            h = hb[e, r, :]
-            for c in range(0, wd_ref.shape[2], 256):
-                stage[r, c : c + 256] = dot(h, wd_ref[g, :, c : c + 256]).astype(BF16)
-            return _
-
-        lax.fori_loop(0, blocks, compute, 0)
+        def compute(rows):
+            stage[:rows, :] = dot(hb[e, :rows, :], wd_ref[g]).astype(BF16)
+
+        for rows in range(BLK, stage.shape[0] + 1, BLK):
+            pl.when(blocks == rows // BLK)(functools.partial(compute, rows))
 
         at = 0
         for q in range(sources):
@@ -260,21 +289,23 @@
 
     @pl.when(step == experts // group - 1)
     def _():
-        tokens, columns = acc.shape
+        tokens, columns = y_refs[0].shape
+        deepest = outs.shape[1] // 512
         for q in reversed(range(sources)):
             c_copy(q).wait()
-            acc[...] = jnp.zeros_like(acc)
-
-            def part(k, _):
-                r = pl.ds(pl.multiple_of(k * 256, 256), 256)
-                for t in range(0, tokens, 256):
-                    cm = cb[q % 2, t : t + 256, r]
-                    for c in range(0, columns, 256):
-                        acc[t : t + 256, c : c + 256] += dot(cm, outs[q, r, c : c + 256])
-                return _
-
-            lax.fori_loop(0, k_ref[q], part, 0)
-            y_refs[q][...] = acc[...].astype(y_refs[q].dtype)
+
+            def combine(depth):
+                def part(i, _):
+                    t = pl.ds(pl.multiple_of(i * 256, 256), 256)
+                    y_refs[q][t, :] = dot(cb[q % 2, t, :depth], outs[q, :depth, :]).astype(y_refs[q].dtype)
+                    return _
+
+                lax.fori_loop(0, tokens // 256, part, 0)
+
+            for i in range(2, deepest + 1):
+                upper = k_ref[q] <= i if i < deepest else True
+                lower = k_ref[q] > i - 1 if i > 2 else True
+                pl.when(jnp.logical_and(upper, lower))(functools.partial(combine, i * 512))
             if q >= 2:
                 c_copy(q - 2).start()
 
@@ -300,7 +331,6 @@
                 pltpu.VMEM((most, columns), BF16),
                 pltpu.VMEM((sources, rows, columns), BF16),
                 pltpu.VMEM((2, tokens, rows), BF16),
-                pltpu.VMEM((tokens, columns), F32),
                 pltpu.SemaphoreType.DMA((experts,)),
                 pltpu.SemaphoreType.DMA((2,)),
             ],
@@ -318,7 +348,7 @@
     local = w_gate.shape[0]
     slots = 5 * tokens * expert.shape[1] // (4 * experts)
     most_q = pl.cdiv(slots, ROW) * ROW
-    rows = pl.cdiv(local * most_q, 256) * 256
+    rows = pl.cdiv(local * most_q, 512) * 512
     most = pl.cdiv(members * most_q, BLK) * BLK
     me = lax.axis_index("ep")
 
@@ -331,7 +361,10 @@
     for q in range(1, members):
         metas.append(swap(meta, q))
     metas = jnp.stack(metas)
-    far = swap(x, 2)
+    half = tokens // 2
+    far = []
+    for i in range(2):
+        far.append(swap(x[i * half : (i + 1) * half], 2))
     near = swap(x, 1)
 
     mark = metas[:, 0].astype(jnp.int32)
@@ -352,7 +385,7 @@
 
     nf, of = n.reshape(-1), off.reshape(-1)
     nblk = (used + BLK - 1) // BLK
-    k = (used + 255) // 256
+    k = (used + 511) // 512
 
     def send(q, v):
         return dispatch(nblk[q : q + 1], pos[q], v, rows)
@@ -361,9 +394,10 @@
     cut = chunks * 2 // 3
     y_shared = shared_expert(x, s_gate, s_up, s_down, 0, cut)
     z = [send(0, x), send(1, near)]
-    far_near = swap(far, 1)
-    z += [send(2, far), send(3, far_near)]
-    h = gate_up(nf, of, w_gate, w_up, z, most)
+    far_near = []
+    for i in range(2):
+        far_near.append(swap(far[i], 1))
+    h = gate_up(nf, of, nblk, w_gate, w_up, [pos[2], pos[3]], [far, far_near], z, most)
 
     columns = 512
     own, side, back = [], [], []

time: 527 us -> 516 us (0.979)
  Pallas kernels: 315 us -> 306 us
  starting transfers between devices: 31.3 us -> 24 us
    ppermute x18 -> x20, starting transfers between devices: 31.3 us -> 24 us  [swap(): return lax.ppermute(v, 'ep', [(i, i ^ q) for i in range(members)])]
    pallas_call x5 -> x3, Pallas kernels: 107 us -> 101 us  [the longest x1 84 us: gate_up(): pl.pallas_call(functools.partial(gate_up_body, experts=experts, ready=rea...]
    ppermute x18 -> x20, waiting for transfers between devices: 135 us -> 135 us  [swap(): return lax.ppermute(v, 'ep', [(i, i ^ q) for i in range(members)])]
  transfers between devices with their start and end apart: 18 -> 20, of which waited for: 4 -> 5; matrix products, arithmetic and copies ran while one was open for 6% -> 7% of each run, Pallas kernels for 24% -> 23%
where the time goes in v1:
time: 516 us
  Pallas kernels  306 us (59%)
  waiting for transfers between devices  135 us (26%)
  other arithmetic  42.9 us (8%)
  starting transfers between devices  24 us (5%)
  local copies, waits for them, and re-layouts  7.06 us (1%)
    ppermute x20, waiting for transfers between devices, swap(): return lax.ppermute(v, 'ep', [(i, i ^ q) for i in range(members)])  135 us
    pallas_call x4, Pallas kernels, down(): pl.pallas_call(functools.partial(down_body, experts=experts, sources=sour...  106 us
    pallas_call x2, Pallas kernels, shared_expert(): pl.pallas_call(functools.partial(shared_body, rows=rows), grid=(last - fi...  98.9 us
    pallas_call x1, Pallas kernels, gate_up(): pl.pallas_call(functools.partial(gate_up_body, experts=experts, ready=rea...  84 us
    ppermute x20, starting transfers between devices, swap(): return lax.ppermute(v, 'ep', [(i, i ^ q) for i in range(members)])  24 us
    pallas_call x2, Pallas kernels, dispatch(): pl.pallas_call(functools.partial(dispatch_body, group=group), grid_spec=p...  17.4 us
    select_n x1, other arithmetic, layer(): comb = jnp.where(pos[:, j, :, None] == at, weight[:, j, :, None], comb)  16.2 us
    convert_element_type x4, other arithmetic, layer(): back.append(swap(mine.astype(BF16), 2))  10.8 us
  transfers between devices with their start and end apart: 20, of which 5 were waited for; matrix products, arithmetic and copies ran while one was open for 7% of the time, Pallas kernels for 23%

profile of v1, /device:TPU:0, one launch (start us, length us, event | category | flops | bytes accessed | tf_op | source)
XLA Modules:
  0.0 515.5 jit_solution(9822339380260821464)
XLA Ops:
  0.0 0.7 convert_bitcast_fusion
  0.7 0.7 fusion.26
  1.5 0.9 collective-permute-start
  2.3 2.5 collective-permute-start.1
  4.8 0.1 collective-permute-start.2
  4.9 0.1 collective-permute-start.7
  5.0 4.9 slice_bitcast_fusion
  9.9 1.9 collective-permute-start.3
  11.9 0.1 collective-permute-start.4
  12.1 0.1 and_bitcast_fusion
  12.2 1.2 select_reduce_fusion.1
  13.3 0.1 fusion.27
  13.5 0.4 select_reduce_fusion.2
  13.8 0.1 copy.20
  13.9 0.5 select_reduce_fusion
  14.7 43.9 %collective-permute-done.3.rest_2_ = bf16[512,2048]{1,0:T(8,128)(2,1)S(1)} collective-permute-done((bf16[512,2048]{1,0:T(8,128)(2,1)}, bf16[512,2048]{1,0:T(8,128)(2,1)S(1)}, u32[]{:S(2)}, u32[]{:S(2)}) %collective-permute-start.3) | collective-permute-done | bytes 2097184 | tf_op jit(solution)/shard_map/ppermute | solution.py:356
  58.6 44.5 %collective-permute-done.4.rest_3_ = bf16[512,2048]{1,0:T(8,128)(2,1)} collective-permute-done((bf16[512,2048]{1,0:T(8,128)(2,1)}, bf16[512,2048]{1,0:T(8,128)(2,1)}, u32[]{:S(2)}, u32[]{:S(2)}) %collective-permute-start.4) | collective-permute-done | bytes 2097184 | tf_op jit(solution)/shard_map/ppermute | solution.py:356
  103.1 16.2 %fusion.c_ref = bf16[4,1024,1536]{2,1,0:T(8,128)(2,1)} fusion(s32[4,1024]{1,0:T(4,128)S(1)} %get-tuple-element.68, s32[4,1024]{1,0:T(4,128)S(1)} %get-tuple-element.69, s32[4,1024]{1,0:T(4,128)S(1)} %get-tuple-element.70, s32[4,1024]{1,0:T(4,128)S(1)} %get-tuple-element.71, bf16[4,1024]{1,0:T(4,128)(2,1)S(1)} %get-tuple-element.72, ...), kind=kLoop, calls=%fused_computation.4 | loop fusion | flops 50331648 | bytes 12681216 | tf_op jit(solution)/shard_map/jit(_where)/select_n | solution.py:384
  119.3 0.6 reshape.56.off_ref
  119.9 0.1 sub.43
  120.0 0.6 and_select_fusion
  120.5 0.6 fusion.31
  121.1 0.6 slice_bitcast_fusion.2
  121.8 8.7 %dispatch.2.rest_6_ = bf16[1536,2048]{1,0:T(8,128)(2,1)} custom-call(s32[1]{0:T(128)} %get-tuple-element.65.nblk_ref, s32[4,1024]{1,0:T(4,128)} %get-tuple-element.54.pos_ref, bf16[1024,2048]{1,0:T(8,128)(2,1)} %bitcast.73), custom_call_target="tpu_custom_call" | custom-call | flops 2147483648 | bytes 8388608 | tf_op jit(solution)/shard_map/dispatch/pallas_call | solution.py:99
  130.4 0.5 fusion.25.n_ref
  131.0 8.7 %dispatch.3.rest_7_ = bf16[1536,2048]{1,0:T(8,128)(2,1)} custom-call(s32[1]{0:T(128)} %get-tuple-element.64.nblk_ref, s32[4,1024]{1,0:T(4,128)} %get-tuple-element.53.pos_ref, bf16[1024,2048]{1,0:T(8,128)(2,1)} %collective-permute-done.7.x_ref), custom_call_target="tpu_custom_call" | custom-call | flops 2147483648 | bytes 8388608 | tf_op jit(solution)/shard_map/dispatch/pallas_call | solution.py:99
  139.7 84.0 %gate_up.1.h_ref = bf16[15,384,1408]{2,1,0:T(8,128)(2,1)} custom-call(s32[60]{0:T(128)} %fusion.25.n_ref, s32[60]{0:T(128)} %reshape.56.off_ref, s32[4]{0:T(128)} %copy-done.6, bf16[15,2048,1408]{2,1,0:T(8,128)(2,1)} %wg_ref.1, bf16[15,2048,1408]{2,1,0:T(8,128)(2,1)} %wu_ref.1, s32[4,1024]{1,0:T(4,128)} %get-tuple-element.56.rest_0_, ...), custom_call_target="tpu_custom_call" | custom-call | flops 44291850240 | bytes 173015040 | tf_op jit(solution)/shard_map/gate_up/pallas_call | solution.py:203
  223.7 26.6 %down.5 = (f32[1024,512]{1,0:T(8,128)}, bf16[1024,512]{1,0:T(8,128)(2,1)}, f32[1024,512]{1,0:T(8,128)}, bf16[1024,512]{1,0:T(8,128)(2,1)}) custom-call(s32[60]{0:T(128)} %fusion.25.n_ref, s32[60]{0:T(128)} %reshape.56.off_ref, s32[4]{0:T(128)} %get-tuple-element.67.k_ref, bf16[15,1408,2048]{2,1,0:T(8,128)(2,1)} %wd_ref.7, ...), custom_call_target="tpu_custom_call" | custom-call | flops 5536481280 | bytes 21626880 | tf_op jit(solution)/shard_map/down/pallas_call | solution.py:318
  250.3 26.3 %down.6 = (f32[1024,512]{1,0:T(8,128)}, bf16[1024,512]{1,0:T(8,128)(2,1)}, f32[1024,512]{1,0:T(8,128)}, bf16[1024,512]{1,0:T(8,128)(2,1)}) custom-call(s32[60]{0:T(128)} %fusion.25.n_ref, s32[60]{0:T(128)} %reshape.56.off_ref, s32[4]{0:T(128)} %get-tuple-element.67.k_ref, bf16[15,1408,2048]{2,1,0:T(8,128)(2,1)} %wd_ref.7, ...), custom_call_target="tpu_custom_call" | custom-call | flops 5536481280 | bytes 21626880 | tf_op jit(solution)/shard_map/down/pallas_call | solution.py:318
  276.6 26.2 %down.7 = (f32[1024,512]{1,0:T(8,128)}, bf16[1024,512]{1,0:T(8,128)(2,1)}, f32[1024,512]{1,0:T(8,128)}, bf16[1024,512]{1,0:T(8,128)(2,1)}) custom-call(s32[60]{0:T(128)} %fusion.25.n_ref, s32[60]{0:T(128)} %reshape.56.off_ref, s32[4]{0:T(128)} %get-tuple-element.67.k_ref, bf16[15,1408,2048]{2,1,0:T(8,128)(2,1)} %wd_ref.7, ...), custom_call_target="tpu_custom_call" | custom-call | flops 5536481280 | bytes 21626880 | tf_op jit(solution)/shard_map/down/pallas_call | solution.py:318
  302.8 26.6 %down.4 = (f32[1024,512]{1,0:T(8,128)}, bf16[1024,512]{1,0:T(8,128)(2,1)}, f32[1024,512]{1,0:T(8,128)}, bf16[1024,512]{1,0:T(8,128)(2,1)}) custom-call(s32[60]{0:T(128)} %fusion.25.n_ref, s32[60]{0:T(128)} %reshape.56.off_ref, s32[4]{0:T(128)} %get-tuple-element.67.k_ref, bf16[15,1408,2048]{2,1,0:T(8,128)(2,1)} %wd_ref.7, ...), custom_call_target="tpu_custom_call" | custom-call | flops 5536481280 | bytes 21626880 | tf_op jit(solution)/shard_map/down/pallas_call | solution.py:318
  329.5 12.8 %collective-permute-start.12 = (bf16[1024,512]{1,0:T(8,128)(2,1)}, bf16[1024,512]{1,0:T(8,128)(2,1)}, u32[]{:S(2)}, u32[]{:S(2)}) collective-permute-start(bf16[1024,512]{1,0:T(8,128)(2,1)} %get-tuple-element.28), channel_id=1, source_target_pairs={{0,1},{1,0},{2,3},{3,2},{4,5},{5,4},{6,7},{7,6}} | collective-permute-start | bytes 3145736 | tf_op jit(solution)/shard_map/ppermute | solution.py:356
  342.3 0.5 collective-permute-start.18
  342.9 59.1 %shared.2.rest_0_ = f32[1024,2048]{1,0:T(8,128)} custom-call(bf16[1024,2048]{1,0:T(8,128)(2,1)} %bitcast.74, bf16[2048,5632]{1,0:T(8,128)(2,1)} %g_ref.3, bf16[2048,5632]{1,0:T(8,128)(2,1)} %u_ref.3, bf16[5632,2048]{1,0:T(8,128)(2,1)} %d_ref.3), custom_call_target="tpu_custom_call" | custom-call | flops 45097156608 | bytes 44040192 | tf_op jit(solution)/shard_map/shared/pallas_call | solution.py:57
  402.0 0.5 collective-permute-start.11
  402.5 0.5 collective-permute-start.17
  403.0 2.7 add_convert_fusion.2
  405.7 2.7 add_convert_fusion.1
  408.4 2.8 add_convert_fusion
  411.2 2.6 add_convert_fusion.3
  413.8 2.0 collective-permute-start.16
  415.8 2.0 collective-permute-start.10
  417.8 39.8 %shared.3 = f32[1024,2048]{1,0:T(8,128)} custom-call(bf16[1024,2048]{1,0:T(8,128)(2,1)} %bitcast.75, bf16[2048,5632]{1,0:T(8,128)(2,1)} %g_ref.3, bf16[2048,5632]{1,0:T(8,128)(2,1)} %u_ref.3, bf16[5632,2048]{1,0:T(8,128)(2,1)} %d_ref.3, f32[1024,2048]{1,0:T(8,128)} %shared.2.rest_0_), custom_call_target="tpu_custom_call" | custom-call | flops 25769803776 | bytes 25165824 | tf_op jit(solution)/shard_map/shared/pallas_call | solution.py:57
  457.6 2.4 collective-permute-done.16
  460.0 22.5 %collective-permute-done.19 = bf16[1024,512]{1,0:T(8,128)(2,1)} collective-permute-done((bf16[1024,512]{1,0:T(8,128)(2,1)}, bf16[1024,512]{1,0:T(8,128)(2,1)}, u32[]{:S(2)}, u32[]{:S(2)}) %collective-permute-start.19) | collective-permute-done | bytes 1048608 | tf_op jit(solution)/shard_map/ppermute | solution.py:356
  482.5 22.0 %collective-permute-done.10 = bf16[1024,512]{1,0:T(8,128)(2,1)} collective-permute-done((bf16[1024,512]{1,0:T(8,128)(2,1)}, bf16[1024,512]{1,0:T(8,128)(2,1)}, u32[]{:S(2)}, u32[]{:S(2)}) %collective-permute-start.10) | collective-permute-done | bytes 1048608 | tf_op jit(solution)/shard_map/ppermute | solution.py:356
  504.4 8.7 %fusion.15 = (bf16[1024,512]{1,0:T(8,128)(2,1)S(1)}, bf16[1024,512]{1,0:T(8,128)(2,1)S(1)}, bf16[1024,512]{1,0:T(8,128)(2,1)S(1)}, bf16[1024,512]{1,0:T(8,128)(2,1)S(1)}) fusion(f32[1024,512]{1,0:T(8,128)} %get-tuple-element.21, f32[1024,2048]{1,0:T(8,128)} %shared.3, bf16[1024,512]{1,0:T(8,128)(2,1)} %collective-permute-done.10, ...), kind=kLoop, calls=%fused_computation.24 | loop fusion | flops 12582912 | bytes 29360128 | tf_op jit(solution)/shard_map/convert_element_type | solution.py:412
  513.2 2.3 maximum_bitcast_fusion
  (48 shorter events, 0.5 us)
Async XLA Ops:
  1.5 10.4 %collective-permute-start = (f32[2,4,1024]{2,1,0:T(4,128)S(1)}, f32[2,4,1024]{2,1,0:T(4,128)S(1)}, u32[]{:S(2)}, u32[]{:S(2)}) collective-permute-start(f32[2,4,1024]{2,1,0:T(4,128)S(1)} %get-tuple-element.62), channel_id=1, source_target_pairs={{0,1},{1,0},{2,3},{3,2},{4,5},{5,4},{6,7},{7,6}} | collective-permute-start | bytes 98312 | tf_op jit(solution)/shard_map/ppermute | solution.py:356
  2.3 9.6 %collective-permute-start.1 = (f32[2,4,1024]{2,1,0:T(4,128)S(1)}, f32[2,4,1024]{2,1,0:T(4,128)S(1)}, u32[]{:S(2)}, u32[]{:S(2)}) collective-permute-start(f32[2,4,1024]{2,1,0:T(4,128)S(1)} %get-tuple-element.62), channel_id=1, source_target_pairs={{0,2},{1,3},{2,0},{3,1},{4,6},{5,7},{6,4},{7,5}} | collective-permute-start | bytes 98312 | tf_op jit(solution)/shard_map/ppermute | solution.py:356
  4.8 7.1 %collective-permute-start.2 = (f32[2,4,1024]{2,1,0:T(4,128)S(1)}, f32[2,4,1024]{2,1,0:T(4,128)S(1)}, u32[]{:S(2)}, u32[]{:S(2)}) collective-permute-start(f32[2,4,1024]{2,1,0:T(4,128)S(1)} %get-tuple-element.62), channel_id=1, source_target_pairs={{0,3},{1,2},{2,1},{3,0},{4,7},{5,6},{6,5},{7,4}} | collective-permute-start | bytes 98312 | tf_op jit(solution)/shard_map/ppermute | solution.py:356
  4.9 126.0 %collective-permute-start.7 = (bf16[1024,2048]{1,0:T(8,128)(2,1)}, bf16[1024,2048]{1,0:T(8,128)(2,1)}, u32[]{:S(2)}, u32[]{:S(2)}) collective-permute-start(bf16[1024,2048]{1,0:T(8,128)(2,1)} %bitcast.72), channel_id=1, source_target_pairs={{0,1},{1,0},{2,3},{3,2},{4,5},{5,4},{6,7},{7,6}} | collective-permute-start | bytes 12582920 | tf_op jit(solution)/shard_map/ppermute | solution.py:356
  9.9 48.7 %collective-permute-start.3 = (bf16[512,2048]{1,0:T(8,128)(2,1)}, bf16[512,2048]{1,0:T(8,128)(2,1)S(1)}, u32[]{:S(2)}, u32[]{:S(2)}) collective-permute-start(bf16[512,2048]{1,0:T(8,128)(2,1)} %get-tuple-element.46), channel_id=1, source_target_pairs={{0,2},{1,3},{2,0},{3,1},{4,6},{5,7},{6,4},{7,5}} | collective-permute-start | bytes 6291464 | tf_op jit(solution)/shard_map/ppermute | solution.py:356
  11.9 91.2 %collective-permute-start.4 = (bf16[512,2048]{1,0:T(8,128)(2,1)}, bf16[512,2048]{1,0:T(8,128)(2,1)}, u32[]{:S(2)}, u32[]{:S(2)}) collective-permute-start(bf16[512,2048]{1,0:T(8,128)(2,1)} %get-tuple-element.45), channel_id=1, source_target_pairs={{0,2},{1,3},{2,0},{3,1},{4,6},{5,7},{6,4},{7,5}} | collective-permute-start | bytes 6291464 | tf_op jit(solution)/shard_map/ppermute | solution.py:356
  58.6 60.7 %copy-start = (bf16[512,2048]{1,0:T(8,128)(2,1)}, bf16[512,2048]{1,0:T(8,128)(2,1)S(1)}, u32[]{:S(2)}) copy-start(bf16[512,2048]{1,0:T(8,128)(2,1)S(1)} %collective-permute-done.3.rest_2_) | copy-start | bytes 6291460
  58.6 81.0 %collective-permute-start.5 = (bf16[512,2048]{1,0:T(8,128)(2,1)S(1)}, bf16[512,2048]{1,0:T(8,128)(2,1)}, u32[]{:S(2)}, u32[]{:S(2)}) collective-permute-start(bf16[512,2048]{1,0:T(8,128)(2,1)S(1)} %collective-permute-done.3.rest_2_), channel_id=1, source_target_pairs={{0,1},{1,0},{2,3},{3,2},{4,5},{5,4},{6,7},{7,6}} | collective-permute-start | bytes 6291464 | tf_op jit(solution)/shard_map/ppermute | solution.py:356
  103.1 36.6 %collective-permute-start.6 = (bf16[512,2048]{1,0:T(8,128)(2,1)}, bf16[512,2048]{1,0:T(8,128)(2,1)}, u32[]{:S(2)}, u32[]{:S(2)}) collective-permute-start(bf16[512,2048]{1,0:T(8,128)(2,1)} %collective-permute-done.4.rest_3_), channel_id=1, source_target_pairs={{0,1},{1,0},{2,3},{3,2},{4,5},{5,4},{6,7},{7,6}} | collective-permute-start | bytes 6291464 | tf_op jit(solution)/shard_map/ppermute | solution.py:356
  120.5 9.9 %copy-start.6 = (s32[4]{0:T(128)}, s32[4]{0:T(128)S(1)}, u32[]{:S(2)}) copy-start(s32[4]{0:T(128)S(1)} %get-tuple-element.66.nblk_ref) | copy-start | bytes 52
  329.5 73.0 %collective-permute-start.12 = (bf16[1024,512]{1,0:T(8,128)(2,1)}, bf16[1024,512]{1,0:T(8,128)(2,1)}, u32[]{:S(2)}, u32[]{:S(2)}) collective-permute-start(bf16[1024,512]{1,0:T(8,128)(2,1)} %get-tuple-element.28), channel_id=1, source_target_pairs={{0,1},{1,0},{2,3},{3,2},{4,5},{5,4},{6,7},{7,6}} | collective-permute-start | bytes 3145736 | tf_op jit(solution)/shard_map/ppermute | solution.py:356
  342.3 60.2 %collective-permute-start.15 = (bf16[1024,512]{1,0:T(8,128)(2,1)}, bf16[1024,512]{1,0:T(8,128)(2,1)}, u32[]{:S(2)}, u32[]{:S(2)}) collective-permute-start(bf16[1024,512]{1,0:T(8,128)(2,1)} %get-tuple-element.32), channel_id=1, source_target_pairs={{0,1},{1,0},{2,3},{3,2},{4,5},{5,4},{6,7},{7,6}} | collective-permute-start | bytes 3145736 | tf_op jit(solution)/shard_map/ppermute | solution.py:356
  342.3 66.0 %collective-permute-start.18 = (bf16[1024,512]{1,0:T(8,128)(2,1)}, bf16[1024,512]{1,0:T(8,128)(2,1)}, u32[]{:S(2)}, u32[]{:S(2)}) collective-permute-start(bf16[1024,512]{1,0:T(8,128)(2,1)} %get-tuple-element.36), channel_id=1, source_target_pairs={{0,1},{1,0},{2,3},{3,2},{4,5},{5,4},{6,7},{7,6}} | collective-permute-start | bytes 3145736 | tf_op jit(solution)/shard_map/ppermute | solution.py:356
  342.8 60.1 %copy-start.4 = (f32[1024,512]{1,0:T(8,128)S(1)}, f32[1024,512]{1,0:T(8,128)}, u32[]{:S(2)}) copy-start(f32[1024,512]{1,0:T(8,128)} %get-tuple-element.27) | copy-start | bytes 6291460
  342.8 68.4 %collective-permute-start.9 = (bf16[1024,512]{1,0:T(8,128)(2,1)}, bf16[1024,512]{1,0:T(8,128)(2,1)}, u32[]{:S(2)}, u32[]{:S(2)}) collective-permute-start(bf16[1024,512]{1,0:T(8,128)(2,1)} %get-tuple-element.24), channel_id=1, source_target_pairs={{0,1},{1,0},{2,3},{3,2},{4,5},{5,4},{6,7},{7,6}} | collective-permute-start | bytes 3145736 | tf_op jit(solution)/shard_map/ppermute | solution.py:356
  402.0 11.8 %collective-permute-start.11 = (bf16[1024,512]{1,0:T(8,128)(2,1)}, bf16[1024,512]{1,0:T(8,128)(2,1)S(1)}, u32[]{:S(2)}, u32[]{:S(2)}) collective-permute-start(bf16[1024,512]{1,0:T(8,128)(2,1)} %get-tuple-element.26), channel_id=1, source_target_pairs={{0,1},{1,0},{2,3},{3,2},{4,5},{5,4},{6,7},{7,6}} | collective-permute-start | bytes 3145736 | tf_op jit(solution)/shard_map/ppermute | solution.py:356
  402.4 13.4 %collective-permute-start.14 = (bf16[1024,512]{1,0:T(8,128)(2,1)}, bf16[1024,512]{1,0:T(8,128)(2,1)}, u32[]{:S(2)}, u32[]{:S(2)}) collective-permute-start(bf16[1024,512]{1,0:T(8,128)(2,1)} %get-tuple-element.30), channel_id=1, source_target_pairs={{0,1},{1,0},{2,3},{3,2},{4,5},{5,4},{6,7},{7,6}} | collective-permute-start | bytes 3145736 | tf_op jit(solution)/shard_map/ppermute | solution.py:356
  402.5 13.4 %collective-permute-start.17 = (bf16[1024,512]{1,0:T(8,128)(2,1)}, bf16[1024,512]{1,0:T(8,128)(2,1)}, u32[]{:S(2)}, u32[]{:S(2)}) collective-permute-start(bf16[1024,512]{1,0:T(8,128)(2,1)} %get-tuple-element.34), channel_id=1, source_target_pairs={{0,1},{1,0},{2,3},{3,2},{4,5},{5,4},{6,7},{7,6}} | collective-permute-start | bytes 3145736 | tf_op jit(solution)/shard_map/ppermute | solution.py:356
  403.0 2.7 copy-start.5
  405.7 2.8 copy-start.3
  408.4 49.2 %collective-permute-start.8 = (bf16[1024,512]{1,0:T(8,128)(2,1)}, bf16[1024,512]{1,0:T(8,128)(2,1)}, u32[]{:S(2)}, u32[]{:S(2)}) collective-permute-start(bf16[1024,512]{1,0:T(8,128)(2,1)} %get-tuple-element.22), channel_id=1, source_target_pairs={{0,1},{1,0},{2,3},{3,2},{4,5},{5,4},{6,7},{7,6}} | collective-permute-start | bytes 3145736 | tf_op jit(solution)/shard_map/ppermute | solution.py:356
  408.4 2.8 copy-start.2
  411.2 46.4 %collective-permute-start.13 = (bf16[1024,512]{1,0:T(8,128)(2,1)}, bf16[1024,512]{1,0:T(8,128)(2,1)}, u32[]{:S(2)}, u32[]{:S(2)}) collective-permute-start(bf16[1024,512]{1,0:T(8,128)(2,1)} %add_convert_fusion.2), channel_id=1, source_target_pairs={{0,2},{1,3},{2,0},{3,1},{4,6},{5,7},{6,4},{7,5}} | collective-permute-start | bytes 3145736 | tf_op jit(solution)/shard_map/ppermute | solution.py:356
  413.8 90.7 %copy-start.1 = (f32[1024,512]{1,0:T(8,128)S(1)}, f32[1024,512]{1,0:T(8,128)}, u32[]{:S(2)}) copy-start(f32[1024,512]{1,0:T(8,128)} %get-tuple-element.25) | copy-start | bytes 6291460
  413.8 46.2 %collective-permute-start.16 = (bf16[1024,512]{1,0:T(8,128)(2,1)}, bf16[1024,512]{1,0:T(8,128)(2,1)}, u32[]{:S(2)}, u32[]{:S(2)}) collective-permute-start(bf16[1024,512]{1,0:T(8,128)(2,1)} %add_convert_fusion.1), channel_id=1, source_target_pairs={{0,2},{1,3},{2,0},{3,1},{4,6},{5,7},{6,4},{7,5}} | collective-permute-start | bytes 3145736 | tf_op jit(solution)/shard_map/ppermute | solution.py:356
  415.8 66.7 %collective-permute-start.19 = (bf16[1024,512]{1,0:T(8,128)(2,1)}, bf16[1024,512]{1,0:T(8,128)(2,1)}, u32[]{:S(2)}, u32[]{:S(2)}) collective-permute-start(bf16[1024,512]{1,0:T(8,128)(2,1)} %add_convert_fusion), channel_id=1, source_target_pairs={{0,2},{1,3},{2,0},{3,1},{4,6},{5,7},{6,4},{7,5}} | collective-permute-start | bytes 3145736 | tf_op jit(solution)/shard_map/ppermute | solution.py:356
  415.8 88.6 %collective-permute-start.10 = (bf16[1024,512]{1,0:T(8,128)(2,1)}, bf16[1024,512]{1,0:T(8,128)(2,1)}, u32[]{:S(2)}, u32[]{:S(2)}) collective-permute-start(bf16[1024,512]{1,0:T(8,128)(2,1)} %add_convert_fusion.3), channel_id=1, source_target_pairs={{0,2},{1,3},{2,0},{3,1},{4,6},{5,7},{6,4},{7,5}} | collective-permute-start | bytes 3145736 | tf_op jit(solution)/shard_map/ppermute | solution.py:356

commit v2 on v1

--- a/solution.py
+++ b/solution.py
@@ -11,6 +11,7 @@
 MIB = 1 << 20
 ROW = 16
 BLK = 128
+DEPTH = 512
 F32, BF16 = jnp.float32, jnp.bfloat16
 
 
@@ -51,7 +52,7 @@
     lax.fori_loop(0, tokens // rows, one, 0)
 
 
-def shared_expert(x, s_gate, s_up, s_down, first, last, init=None, chunk=512, rows=256):
+def shared_expert(x, s_gate, s_up, s_down, first, last, init=None, chunk=512, rows=512):
     tokens, d = x.shape
     once = dict(pipeline_mode=pl.Buffered(1))
     return pl.pallas_call(
@@ -227,12 +228,65 @@
     )(n, off, nblk, w_gate, w_up, *pos, *[v for x in xs for v in x], *zs)
 
 
-def down_body(n_ref, off_ref, k_ref, wd_ref, h_ref, c_ref, *rest, experts, sources, group):
-    y_refs, (hb, stage, outs, cb, sem, csem) = rest[:sources], rest[sources:]
+def comb_body(k_ref, pos_ref, gate_ref, c_ref):
+    q, b = pl.program_id(0), pl.program_id(1)
+    tokens, width = c_ref.shape
+
+    @pl.when(b < k_ref[q])
+    def _():
+        column = b * width + lax.broadcasted_iota(jnp.int32, (BLK, width), 1)
+
+        def one(i, _):
+            t = pl.ds(pl.multiple_of(i * BLK, BLK), BLK)
+            pos, gate = pos_ref[t, :], gate_ref[t, :]
+            value = jnp.zeros((BLK, width), F32)
+            for j in range(pos.shape[1]):
+                value = jnp.where(pos[:, j : j + 1] == column, gate[:, j : j + 1], value)
+            c_ref[t, :] = value.astype(BF16)
+            return _
+
+        lax.fori_loop(0, tokens // BLK, one, 0)
+
+
+def combine_matrices(k, pos, gate, rows):
+    sources, tokens, top = pos.shape
+    return pl.pallas_call(
+        comb_body,
+        grid_spec=pltpu.PrefetchScalarGridSpec(
+            num_scalar_prefetch=1,
+            grid=(sources, rows // DEPTH),
+            in_specs=[pl.BlockSpec((None, tokens, top), lambda q, b, k: (q, 0, 0))] * 2,
+            out_specs=pl.BlockSpec((None, tokens, DEPTH), lambda q, b, k: (q, 0, jnp.minimum(b, k[q] - 1))),
+        ),
+        out_shape=jax.ShapeDtypeStruct((sources, tokens, rows), BF16),
+        compiler_params=pltpu.CompilerParams(vmem_limit_bytes=60 * MIB),
+        cost_estimate=cost(4 * MIB, 8 * MIB),
+        name="comb",
+    )(k, pos, gate)
+
+
+def combine(k, c, rows, out):
+    deepest = rows.shape[0] // DEPTH
+
+    def whole(depth):
+        def part(i, _):
+            t = pl.ds(pl.multiple_of(i * 256, 256), 256)
+            out(t, dot(c[t, :depth], rows[:depth, :]))
+            return _
+
+        lax.fori_loop(0, c.shape[0] // 256, part, 0)
+
+    pl.when(k < deepest)(functools.partial(whole, (deepest - 1) * DEPTH))
+    pl.when(k >= deepest)(functools.partial(whole, deepest * DEPTH))
+
+
+def down_body(n_ref, off_ref, k_ref, wd_ref, h_ref, c_ref, *rest, experts, own, far, group):
+    y_refs, own_ref, (hb, stage, outs, cb, sem, csem) = rest[-far - 7 : -7], rest[-7], rest[-6:]
     step = pl.program_id(0)
-
-    def c_copy(q):
-        return pltpu.make_async_copy(c_ref.at[q], cb.at[q % 2], csem.at[q % 2])
+    sources = own + far
+
+    def c_copy(i):
+        return pltpu.make_async_copy(c_ref.at[own + i], cb.at[i], csem.at[i])
 
     def h_copy(e, b):
         r = pl.ds(pl.multiple_of(b * BLK, BLK), BLK)
@@ -249,9 +303,10 @@
             return _
 
         lax.fori_loop(0, experts, fetch, 0)
-        for q in range(2):
-            c_copy(sources - 1 - q).start()
+        for i in range(far):
+            c_copy(i).start()
         outs[...] = jnp.zeros_like(outs)
+        own_ref[...] = jnp.zeros_like(own_ref)
 
     def expert(g, _):
         e = step * group + g
@@ -274,11 +329,12 @@
         for q in range(sources):
             n = n_ref[q * experts + e]
             off = off_ref[q * experts + e]
+            to = own_ref.at[q] if q < own else outs.at[q - own]
 
             def move(i, _):
                 src = pl.ds(pl.multiple_of(at + i * ROW, ROW), ROW)
                 dst = pl.ds(pl.multiple_of(off + i * ROW, ROW), ROW)
-                outs[q, dst, :] = stage[src, :]
+                to[dst, :] = stage[src, :]
                 return _
 
             lax.fori_loop(0, n // ROW, move, 0)
@@ -289,57 +345,79 @@
 
     @pl.when(step == experts // group - 1)
     def _():
-        tokens, columns = y_refs[0].shape
-        deepest = outs.shape[1] // 512
-        for q in reversed(range(sources)):
-            c_copy(q).wait()
-
-            def combine(depth):
-                def part(i, _):
-                    t = pl.ds(pl.multiple_of(i * 256, 256), 256)
-                    y_refs[q][t, :] = dot(cb[q % 2, t, :depth], outs[q, :depth, :]).astype(y_refs[q].dtype)
-                    return _
-
-                lax.fori_loop(0, tokens // 256, part, 0)
-
-            for i in range(2, deepest + 1):
-                upper = k_ref[q] <= i if i < deepest else True
-                lower = k_ref[q] > i - 1 if i > 2 else True
-                pl.when(jnp.logical_and(upper, lower))(functools.partial(combine, i * 512))
-            if q >= 2:
-                c_copy(q - 2).start()
-
-
-def down(n, off, k, w_down, h, comb, column, columns, group=3):
+        for i in reversed(range(far)):
+            c_copy(i).wait()
+
+            def out(t, v):
+                y_refs[i][t, :] = v.astype(y_refs[i].dtype)
+
+            combine(k_ref[own + i], cb.at[i], outs.at[i], out)
+
+
+def down(n, off, k, w_down, h, comb, kept, column, columns, own, group=3):
     experts, f, d = w_down.shape
     sources, tokens, rows = comb.shape
+    far = sources - own
     most = h.shape[1]
     once = dict(pipeline_mode=pl.Buffered(1))
-    return pl.pallas_call(
-        functools.partial(down_body, experts=experts, sources=sources, group=group),
+    at = column // columns
+    aliased = [] if kept is None else [kept]
+    return pl.pallas_call(
+        functools.partial(down_body, experts=experts, own=own, far=far, group=group),
         grid_spec=pltpu.PrefetchScalarGridSpec(
             num_scalar_prefetch=3,
             grid=(experts // group,),
-            in_specs=[
-                pl.BlockSpec((group, f, columns), lambda e, *_: (e, 0, column // columns)),
-                pl.BlockSpec(memory_space=pl.ANY),
-                pl.BlockSpec(memory_space=pl.ANY),
-            ],
-            out_specs=[pl.BlockSpec((tokens, columns), lambda e, *_: (0, 0), **once)] * sources,
+            in_specs=[pl.BlockSpec((group, f, columns), lambda e, *_: (e, 0, at))]
+            + [pl.BlockSpec(memory_space=pl.ANY)] * (2 + len(aliased)),
+            out_specs=[pl.BlockSpec((tokens, columns), lambda e, *_: (0, 0), **once)] * far
+            + [pl.BlockSpec((own, rows, columns), lambda e, *_: (0, 0, at), **once)],
             scratch_shapes=[
                 pltpu.VMEM((experts, most, f), BF16),
                 pltpu.VMEM((most, columns), BF16),
-                pltpu.VMEM((sources, rows, columns), BF16),
-                pltpu.VMEM((2, tokens, rows), BF16),
+                pltpu.VMEM((far, rows, columns), BF16),
+                pltpu.VMEM((far, tokens, rows), BF16),
                 pltpu.SemaphoreType.DMA((experts,)),
-                pltpu.SemaphoreType.DMA((2,)),
+                pltpu.SemaphoreType.DMA((far,)),
             ],
         ),
-        out_shape=[jax.ShapeDtypeStruct((tokens, columns), F32 if q % 2 == 0 else BF16) for q in range(sources)],
-        compiler_params=pltpu.CompilerParams(vmem_limit_bytes=60 * MIB),
+        out_shape=[jax.ShapeDtypeStruct((tokens, columns), F32 if i == 0 else BF16) for i in range(far)]
+        + [jax.ShapeDtypeStruct((own, rows, d), BF16)],
+        input_output_aliases={6: far} if aliased else {},
+        compiler_params=pltpu.CompilerParams(vmem_limit_bytes=67_043_328),
         cost_estimate=cost(2 * experts * 256 * f * columns, experts * f * columns * 2),
         name="down",
-    )(n, off, k, w_down, h, comb)
+    )(n, off, k, w_down, h, comb, *aliased)
+
+
+def own_body(k_ref, c_ref, r_ref, s_ref, *y_refs):
+    for i in reversed(range(len(y_refs))):
+
+        def out(t, v):
+            y_refs[i][t, :] = v + s_ref[t, :] if i == 0 else v.astype(BF16)
+
+        combine(k_ref[i], c_ref.at[i], r_ref.at[i], out)
+
+
+def own_sums(k, comb, kept, shared, columns=512):
+    own, rows, d = kept.shape
+    tokens = comb.shape[1]
+    return pl.pallas_call(
+        own_body,
+        grid_spec=pltpu.PrefetchScalarGridSpec(
+            num_scalar_prefetch=1,
+            grid=(d // columns,),
+            in_specs=[
+                pl.BlockSpec((own, tokens, rows), lambda c, *_: (0, 0, 0), pipeline_mode=pl.Buffered(1)),
+                pl.BlockSpec((own, rows, columns), lambda c, *_: (0, 0, c)),
+                pl.BlockSpec((tokens, columns), lambda c, *_: (0, c)),
+            ],
+            out_specs=[pl.BlockSpec((tokens, columns), lambda c, *_: (0, c))] * own,
+        ),
+        out_shape=[jax.ShapeDtypeStruct((tokens, d), F32 if i == 0 else BF16) for i in range(own)],
+        compiler_params=pltpu.CompilerParams(vmem_limit_bytes=60 * MIB),
+        cost_estimate=cost(4 * tokens * rows * d, 20 * MIB),
+        name="own",
+    )(k, comb, kept, shared)
 
 
 def layer(x, expert, slot, gate, w_gate, w_up, w_down, s_gate, s_up, s_down, *, members, experts):
@@ -348,7 +426,7 @@
     local = w_gate.shape[0]
     slots = 5 * tokens * expert.shape[1] // (4 * experts)
     most_q = pl.cdiv(slots, ROW) * ROW
-    rows = pl.cdiv(local * most_q, 512) * 512
+    rows = pl.cdiv(local * most_q, DEPTH) * DEPTH
     most = pl.cdiv(members * most_q, BLK) * BLK
     me = lax.axis_index("ep")
 
@@ -361,10 +439,7 @@
     for q in range(1, members):
         metas.append(swap(meta, q))
     metas = jnp.stack(metas)
-    half = tokens // 2
-    far = []
-    for i in range(2):
-        far.append(swap(x[i * half : (i + 1) * half], 2))
+    far = swap(x, 2)
     near = swap(x, 1)
 
     mark = metas[:, 0].astype(jnp.int32)
@@ -377,42 +452,32 @@
     off = jnp.sum(jnp.where(ids[None, :] < ids[:, None], n[:, None, :], 0), axis=2)
     used = jnp.sum(n, axis=1)
     pos = jnp.where(ok, jnp.sum(jnp.where(is_it, off[:, :, None, None], 0), axis=1) + s, -1)
-    weight = metas[:, 1].astype(BF16)
-    at = jnp.arange(rows, dtype=jnp.int32)
-    comb = jnp.zeros((members, tokens, rows), BF16)
-    for j in range(pos.shape[1]):
-        comb = jnp.where(pos[:, j, :, None] == at, weight[:, j, :, None], comb)
-
     nf, of = n.reshape(-1), off.reshape(-1)
     nblk = (used + BLK - 1) // BLK
-    k = (used + 511) // 512
+    k = jnp.maximum((used + DEPTH - 1) // DEPTH, rows // DEPTH - 1)
 
     def send(q, v):
         return dispatch(nblk[q : q + 1], pos[q], v, rows)
 
     chunks = s_gate.shape[1] // 512
-    cut = chunks * 2 // 3
+    cut = chunks * 8 // 11
     y_shared = shared_expert(x, s_gate, s_up, s_down, 0, cut)
     z = [send(0, x), send(1, near)]
-    far_near = []
-    for i in range(2):
-        far_near.append(swap(far[i], 1))
-    h = gate_up(nf, of, nblk, w_gate, w_up, [pos[2], pos[3]], [far, far_near], z, most)
-
-    columns = 512
-    own, side, back = [], [], []
-    for c in range(0, d, columns):
-        y0, y1, y2, y3 = down(nf, of, k, w_down, h, comb, c, columns)
+    far_near = swap(far, 1)
+    gates = metas[:, 1].astype(BF16).astype(F32)
+    comb = combine_matrices(k, pos.transpose(0, 2, 1), gates.transpose(0, 2, 1), rows)
+    h = gate_up(nf, of, nblk, w_gate, w_up, [pos[2], pos[3]], [[far], [far_near]], z, most)
+
+    back, kept, at = [], None, 0
+    for columns in (d // 4, d // 4, d // 2):
+        y2, y3, kept = down(nf, of, k, w_down, h, comb, kept, at, columns, 2)
         mine = y2 + swap(y3, 1).astype(F32)
         back.append(swap(mine.astype(BF16), 2))
-        side.append(swap(y1, 1))
-        own.append(y0)
-    y_shared = shared_expert(x, s_gate, s_up, s_down, cut, chunks, y_shared)
-    out = [
-        (y_shared[:, i * columns : (i + 1) * columns] + own[i] + side[i].astype(F32) + back[i].astype(F32)).astype(BF16)
-        for i in range(len(own))
-    ]
-    return jnp.concatenate(out, axis=1)[None, None]
+        at += columns
+    y0, y1 = own_sums(k, comb, kept, y_shared)
+    side = swap(y1, 1)
+    y_shared = shared_expert(x, s_gate, s_up, s_down, cut, chunks, y0)
+    return (y_shared + side.astype(F32) + jnp.concatenate(back, axis=1).astype(F32)).astype(BF16)[None, None]
 
 
 def solution(mesh):

time: 516 us -> 514 us (level)
  other arithmetic: 42.9 us -> 18.7 us
  waiting for transfers between devices: 135 us -> 150 us
  Pallas kernels: 306 us -> 319 us
    pallas_call x4 -> x5, Pallas kernels: 106 us -> 122 us  [the longest x3 80.4 us: down(): pl.pallas_call(functools.partial(down_body, experts=experts, own=own, far...]
    select_n x1 -> x0, other arithmetic: 16.2 us -> none  [layer(): comb = jnp.where(pos[:, j, :, None] == at, weight[:, j, :, None], comb)]
    ppermute x20 -> x13, waiting for transfers between devices: 135 us -> 150 us  [swap(): return lax.ppermute(v, 'ep', [(i, i ^ q) for i in range(members)])]
    convert_element_type x1 -> x0, other arithmetic: 8.73 us -> none  [layer(): (y_shared[:, i * columns:(i + 1) * columns] + own[i] + side[i].astype(F32...]
    ppermute x20 -> x13, starting transfers between devices: 24 us -> 19.6 us  [swap(): return lax.ppermute(v, 'ep', [(i, i ^ q) for i in range(members)])]
    convert_element_type x4 -> x3, other arithmetic: 10.8 us -> 6.64 us  [layer(): back.append(swap(mine.astype(BF16), 2))]
  transfers between devices with their start and end apart: 20 -> 13, of which waited for: 5 -> 3; matrix products, arithmetic and copies ran while one was open for 7% -> 3% of each run, Pallas kernels for 23% -> 30%
where the time goes in v2:
time: 514 us
  Pallas kernels  319 us (62%)
  waiting for transfers between devices  150 us (29%)
  starting transfers between devices  19.6 us (4%)
  other arithmetic  18.7 us (4%)
  local copies, waits for them, and re-layouts  6.03 us (1%)
    ppermute x13, waiting for transfers between devices, swap(): return lax.ppermute(v, 'ep', [(i, i ^ q) for i in range(members)])  150 us
    pallas_call x2, Pallas kernels, shared_expert(): pl.pallas_call(functools.partial(shared_body, rows=rows), grid=(last - fi...  95 us
    pallas_call x1, Pallas kernels, gate_up(): pl.pallas_call(functools.partial(gate_up_body, experts=experts, ready=rea...  84.2 us
    pallas_call x3, Pallas kernels, down(): pl.pallas_call(functools.partial(down_body, experts=experts, own=own, far...  80.4 us
    pallas_call x1, Pallas kernels, own_sums(): pl.pallas_call(own_body, grid_spec=pltpu.PrefetchScalarGridSpec(num_scala...  21.3 us
    pallas_call x1, Pallas kernels, combine_matrices(): pl.pallas_call(comb_body, grid_spec=pltpu.PrefetchScalarGridSpec(num_scal...  20.7 us
    ppermute x13, starting transfers between devices, swap(): return lax.ppermute(v, 'ep', [(i, i ^ q) for i in range(members)])  19.6 us
    pallas_call x2, Pallas kernels, dispatch(): pl.pallas_call(functools.partial(dispatch_body, group=group), grid_spec=p...  17.4 us
  transfers between devices with their start and end apart: 13, of which 3 were waited for; matrix products, arithmetic and copies ran while one was open for 3% of the time, Pallas kernels for 30%

profile of v2, /device:TPU:0, one launch (start us, length us, event | category | flops | bytes accessed | tf_op | source)
XLA Modules:
  0.0 513.8 jit_solution(10610991857255863666)
XLA Ops:
  0.0 3.3 collective-permute-start.3
  3.3 0.7 convert_bitcast_fusion.1
  4.1 0.7 fusion.12
  4.8 0.0 collective-permute-start
  4.8 0.0 collective-permute-start.1
  4.9 1.8 collective-permute-start.2
  6.7 0.3 collective-permute-start.5
  7.0 87.9 %collective-permute-done.3.rest_2_ = bf16[1024,2048]{1,0:T(8,128)(2,1)} collective-permute-done((bf16[1024,2048]{1,0:T(8,128)(2,1)}, bf16[1024,2048]{1,0:T(8,128)(2,1)}, u32[]{:S(2)}, u32[]{:S(2)}) %collective-permute-start.3) | collective-permute-done | bytes 4194336 | tf_op jit(solution)/shard_map/ppermute | solution.py:434
  94.9 63.4 %shared.2.s_ref = f32[1024,2048]{1,0:T(8,128)} custom-call(bf16[1024,2048]{1,0:T(8,128)(2,1)} %bitcast.60, bf16[2048,5632]{1,0:T(8,128)(2,1)} %g_ref.3, bf16[2048,5632]{1,0:T(8,128)(2,1)} %u_ref.3, bf16[5632,2048]{1,0:T(8,128)(2,1)} %d_ref.3), custom_call_target="tpu_custom_call" | custom-call | flops 51539607552 | bytes 50331648 | tf_op jit(solution)/shard_map/shared/pallas_call | solution.py:58
  158.4 0.0 collective-permute-done.2
  158.4 0.1 and_bitcast_fusion
  158.5 1.2 select_reduce_fusion.1
  159.7 0.1 fusion.13
  159.8 0.4 select_reduce_fusion.2
  160.2 0.1 copy.21
  160.3 0.7 reshape.48.off_ref
  160.9 0.1 sub.52
  161.0 0.5 select_reduce_fusion
  161.6 2.0 copy.22.pos_ref
  163.6 2.0 copy.23.gate_ref
  165.6 0.5 and_select_fusion
  166.1 20.7 %comb.1.c_ref = bf16[4,1024,1536]{2,1,0:T(8,128)(2,1)} custom-call(s32[4]{0:T(128)} %get-tuple-element.43.k_ref, s32[4,1024,4]{2,1,0:T(8,128)} %copy.22.pos_ref, f32[4,1024,4]{2,1,0:T(8,128)} %copy.23.gate_ref), custom_call_target="tpu_custom_call" | custom-call | flops 4194304 | bytes 8388608 | tf_op jit(solution)/shard_map/comb/pallas_call | solution.py:253
  186.8 0.6 fusion.15
  187.4 0.6 slice_bitcast_fusion
  188.0 8.7 %dispatch.2.rest_4_ = bf16[1536,2048]{1,0:T(8,128)(2,1)} custom-call(s32[1]{0:T(128)} %get-tuple-element.41.nblk_ref, s32[4,1024]{1,0:T(4,128)} %get-tuple-element.34.pos_ref, bf16[1024,2048]{1,0:T(8,128)(2,1)} %bitcast.61), custom_call_target="tpu_custom_call" | custom-call | flops 2147483648 | bytes 8388608 | tf_op jit(solution)/shard_map/dispatch/pallas_call | solution.py:100
  196.7 0.5 fusion.10.n_ref
  197.3 0.0 collective-permute-done.5.x_ref
  197.3 8.7 %dispatch.3.rest_5_ = bf16[1536,2048]{1,0:T(8,128)(2,1)} custom-call(s32[1]{0:T(128)} %get-tuple-element.40.nblk_ref, s32[4,1024]{1,0:T(4,128)} %get-tuple-element.33.pos_ref, bf16[1024,2048]{1,0:T(8,128)(2,1)} %collective-permute-done.5.x_ref), custom_call_target="tpu_custom_call" | custom-call | flops 2147483648 | bytes 8388608 | tf_op jit(solution)/shard_map/dispatch/pallas_call | solution.py:100
  206.0 0.0 collective-permute-done.4.rest_3_
  206.0 84.2 %gate_up.1.h_ref = bf16[15,384,1408]{2,1,0:T(8,128)(2,1)} custom-call(s32[60]{0:T(128)} %fusion.10.n_ref, s32[60]{0:T(128)} %reshape.48.off_ref, s32[4]{0:T(128)} %copy-done.3, bf16[15,2048,1408]{2,1,0:T(8,128)(2,1)} %wg_ref.1, bf16[15,2048,1408]{2,1,0:T(8,128)(2,1)} %wu_ref.1, s32[4,1024]{1,0:T(4,128)} %get-tuple-element.36.rest_0_, ...), custom_call_target="tpu_custom_call" | custom-call | flops 44291850240 | bytes 173015040 | tf_op jit(solution)/shard_map/gate_up/pallas_call | solution.py:204
  290.1 22.7 %down.3 = (f32[1024,512]{1,0:T(8,128)}, bf16[1024,512]{1,0:T(8,128)(2,1)}, bf16[2,1536,2048]{2,1,0:T(8,128)(2,1)}) custom-call(s32[60]{0:T(128)} %fusion.10.n_ref, s32[60]{0:T(128)} %reshape.48.off_ref, s32[4]{0:T(128)} %get-tuple-element.43.k_ref, bf16[15,1408,2048]{2,1,0:T(8,128)(2,1)} %wd_ref.5, bf16[15,384,1408]{2,1,0:T(8,128)(2,1)} %gate_up.1.h_ref, ...), custom_call_target="tpu_custom_call" | custom-call | flops 5536481280 | bytes 21626880 | tf_op jit(solution)/shard_map/down/pallas_call | solution.py:365
  312.8 23.0 %down.4 = (f32[1024,512]{1,0:T(8,128)}, bf16[1024,512]{1,0:T(8,128)(2,1)}, bf16[2,1536,2048]{2,1,0:T(8,128)(2,1)}) custom-call(s32[60]{0:T(128)} %fusion.10.n_ref, s32[60]{0:T(128)} %reshape.48.off_ref, s32[4]{0:T(128)} %get-tuple-element.43.k_ref, bf16[15,1408,2048]{2,1,0:T(8,128)(2,1)} %wd_ref.5, ...), custom_call_target="tpu_custom_call", output_to_operand_aliasing={{2}: (6, {})} | custom-call | flops 5536481280 | bytes 21626880 | tf_op jit(solution)/shard_map/down/pallas_call | solution.py:365
  335.8 34.7 %down.5 = (f32[1024,1024]{1,0:T(8,128)}, bf16[1024,1024]{1,0:T(8,128)(2,1)}, bf16[2,1536,2048]{2,1,0:T(8,128)(2,1)}) custom-call(s32[60]{0:T(128)} %fusion.10.n_ref, s32[60]{0:T(128)} %reshape.48.off_ref, s32[4]{0:T(128)} %get-tuple-element.43.k_ref, bf16[15,1408,2048]{2,1,0:T(8,128)(2,1)} %wd_ref.5, ...), custom_call_target="tpu_custom_call", output_to_operand_aliasing={{2}: (6, {})} | custom-call | flops 11072962560 | bytes 43253760 | tf_op jit(solution)/shard_map/down/pallas_call | solution.py:365
  370.5 11.5 %collective-permute-start.11 = (bf16[1024,1024]{1,0:T(8,128)(2,1)}, bf16[1024,1024]{1,0:T(8,128)(2,1)}, u32[]{:S(2)}, u32[]{:S(2)}) collective-permute-start(bf16[1024,1024]{1,0:T(8,128)(2,1)} %get-tuple-element.26), channel_id=1, source_target_pairs={{0,1},{1,0},{2,3},{3,2},{4,5},{5,4},{6,7},{7,6}} | collective-permute-start | bytes 6291464 | tf_op jit(solution)/shard_map/ppermute | solution.py:434
  382.1 21.3 %own.1 = (f32[1024,2048]{1,0:T(8,128)}, bf16[1024,2048]{1,0:T(8,128)(2,1)}) custom-call(s32[4]{0:T(128)} %get-tuple-element.43.k_ref, bf16[4,1024,1536]{2,1,0:T(8,128)(2,1)} %comb.1.c_ref, bf16[2,1536,2048]{2,1,0:T(8,128)(2,1)} %get-tuple-element.18.r_ref, f32[1024,2048]{1,0:T(8,128)} %shared.2.s_ref), custom_call_target="tpu_custom_call" | custom-call | flops 12884901888 | bytes 20971520 | tf_op jit(solution)/shard_map/own/pallas_call | solution.py:404
  403.4 0.0 collective-permute-start.6
  403.4 0.5 collective-permute-start.7
  403.9 0.0 collective-permute-start.9
  404.0 8.3 %collective-permute-done.7 = bf16[1024,512]{1,0:T(8,128)(2,1)S(1)} collective-permute-done((bf16[1024,512]{1,0:T(8,128)(2,1)S(1)}, bf16[1024,512]{1,0:T(8,128)(2,1)S(1)}, u32[]{:S(2)}, u32[]{:S(2)}) %collective-permute-start.7) | collective-permute-done | bytes 1048608 | tf_op jit(solution)/shard_map/ppermute | solution.py:434
  412.3 1.4 add_convert_fusion.3
  413.7 3.9 add_convert_fusion.1
  417.6 2.0 collective-permute-start.12
  419.6 1.4 add_convert_fusion.2
  421.0 0.0 collective-permute-start.10
  421.0 31.6 %shared.3 = f32[1024,2048]{1,0:T(8,128)} custom-call(bf16[1024,2048]{1,0:T(8,128)(2,1)} %bitcast.62, bf16[2048,5632]{1,0:T(8,128)(2,1)} %g_ref.3, bf16[2048,5632]{1,0:T(8,128)(2,1)} %u_ref.3, bf16[5632,2048]{1,0:T(8,128)(2,1)} %d_ref.3, f32[1024,2048]{1,0:T(8,128)} %get-tuple-element.19.rest_0_), custom_call_target="tpu_custom_call" | custom-call | flops 19327352832 | bytes 18874368 | tf_op jit(solution)/shard_map/shared/pallas_call | solution.py:58
  452.6 0.0 collective-permute-done.8
  452.6 54.0 %collective-permute-done.10 = bf16[1024,512]{1,0:T(8,128)(2,1)} collective-permute-done((bf16[1024,512]{1,0:T(8,128)(2,1)}, bf16[1024,512]{1,0:T(8,128)(2,1)}, u32[]{:S(2)}, u32[]{:S(2)}) %collective-permute-start.10) | collective-permute-done | bytes 1048608 | tf_op jit(solution)/shard_map/ppermute | solution.py:434
  506.6 7.2 %fusion = bf16[1,1,1024,2048]{3,2,1,0:T(8,128)(2,1)} fusion(f32[1024,2048]{1,0:T(8,128)} %shared.3, bf16[1024,2048]{1,0:T(8,128)(2,1)} %collective-permute-done.6, bf16[1024,1024]{1,0:T(8,128)(2,1)S(1)} %collective-permute-done.12, bf16[1024,512]{1,0:T(8,128)(2,1)} %collective-permute-done.10, bf16[1024,512]{1,0:T(8,128)(2,1)S(1)} %collective-permute-done.8), kind=kLoop, calls=%fused_computation.1 | loop fusion | flops 20971520 | bytes 20971520 | tf_op jit(solution)/shard_map/broadcast_in_dim | solution.py:480
  (23 shorter events, 0.2 us)
Async XLA Ops:
  0.0 94.9 %collective-permute-start.3 = (bf16[1024,2048]{1,0:T(8,128)(2,1)}, bf16[1024,2048]{1,0:T(8,128)(2,1)}, u32[]{:S(2)}, u32[]{:S(2)}) collective-permute-start(bf16[1024,2048]{1,0:T(8,128)(2,1)} %bitcast.58), channel_id=1, source_target_pairs={{0,2},{1,3},{2,0},{3,1},{4,6},{5,7},{6,4},{7,5}} | collective-permute-start | bytes 12582920 | tf_op jit(solution)/shard_map/ppermute | solution.py:434
  4.8 153.6 %collective-permute-start = (f32[2,4,1024]{2,1,0:T(4,128)S(1)}, f32[2,4,1024]{2,1,0:T(4,128)S(1)}, u32[]{:S(2)}, u32[]{:S(2)}) collective-permute-start(f32[2,4,1024]{2,1,0:T(4,128)S(1)} %get-tuple-element.38), channel_id=1, source_target_pairs={{0,1},{1,0},{2,3},{3,2},{4,5},{5,4},{6,7},{7,6}} | collective-permute-start | bytes 98312 | tf_op jit(solution)/shard_map/ppermute | solution.py:434
  4.8 153.5 %collective-permute-start.1 = (f32[2,4,1024]{2,1,0:T(4,128)S(1)}, f32[2,4,1024]{2,1,0:T(4,128)S(1)}, u32[]{:S(2)}, u32[]{:S(2)}) collective-permute-start(f32[2,4,1024]{2,1,0:T(4,128)S(1)} %get-tuple-element.38), channel_id=1, source_target_pairs={{0,2},{1,3},{2,0},{3,1},{4,6},{5,7},{6,4},{7,5}} | collective-permute-start | bytes 98312 | tf_op jit(solution)/shard_map/ppermute | solution.py:434
  4.9 153.5 %collective-permute-start.2 = (f32[2,4,1024]{2,1,0:T(4,128)S(1)}, f32[2,4,1024]{2,1,0:T(4,128)S(1)}, u32[]{:S(2)}, u32[]{:S(2)}) collective-permute-start(f32[2,4,1024]{2,1,0:T(4,128)S(1)} %get-tuple-element.38), channel_id=1, source_target_pairs={{0,3},{1,2},{2,1},{3,0},{4,7},{5,6},{6,5},{7,4}} | collective-permute-start | bytes 98312 | tf_op jit(solution)/shard_map/ppermute | solution.py:434
  6.7 190.6 %collective-permute-start.5 = (bf16[1024,2048]{1,0:T(8,128)(2,1)}, bf16[1024,2048]{1,0:T(8,128)(2,1)}, u32[]{:S(2)}, u32[]{:S(2)}) collective-permute-start(bf16[1024,2048]{1,0:T(8,128)(2,1)} %bitcast.59), channel_id=1, source_target_pairs={{0,1},{1,0},{2,3},{3,2},{4,5},{5,4},{6,7},{7,6}} | collective-permute-start | bytes 12582920 | tf_op jit(solution)/shard_map/ppermute | solution.py:434
  94.9 111.1 %collective-permute-start.4 = (bf16[1024,2048]{1,0:T(8,128)(2,1)}, bf16[1024,2048]{1,0:T(8,128)(2,1)}, u32[]{:S(2)}, u32[]{:S(2)}) collective-permute-start(bf16[1024,2048]{1,0:T(8,128)(2,1)} %collective-permute-done.3.rest_2_), channel_id=1, source_target_pairs={{0,1},{1,0},{2,3},{3,2},{4,5},{5,4},{6,7},{7,6}} | collective-permute-start | bytes 12582920 | tf_op jit(solution)/shard_map/ppermute | solution.py:434
  166.1 20.7 %copy-start.3 = (s32[4]{0:T(128)}, s32[4]{0:T(128)S(1)}, u32[]{:S(2)}) copy-start(s32[4]{0:T(128)S(1)} %get-tuple-element.42.nblk_ref) | copy-start | bytes 52
  370.5 43.1 %collective-permute-start.11 = (bf16[1024,1024]{1,0:T(8,128)(2,1)}, bf16[1024,1024]{1,0:T(8,128)(2,1)}, u32[]{:S(2)}, u32[]{:S(2)}) collective-permute-start(bf16[1024,1024]{1,0:T(8,128)(2,1)} %get-tuple-element.26), channel_id=1, source_target_pairs={{0,1},{1,0},{2,3},{3,2},{4,5},{5,4},{6,7},{7,6}} | collective-permute-start | bytes 6291464 | tf_op jit(solution)/shard_map/ppermute | solution.py:434
  382.1 21.4 %copy-start.4 = (bf16[1024,512]{1,0:T(8,128)(2,1)S(1)}, bf16[1024,512]{1,0:T(8,128)(2,1)}, u32[]{:S(2)}) copy-start(bf16[1024,512]{1,0:T(8,128)(2,1)} %get-tuple-element.22) | copy-start | bytes 3145732
  382.1 30.2 %copy-start.2 = (f32[1024,512]{1,0:T(8,128)S(1)}, f32[1024,512]{1,0:T(8,128)}, u32[]{:S(2)}) copy-start(f32[1024,512]{1,0:T(8,128)} %get-tuple-element.21) | copy-start | bytes 6291460
  403.4 10.2 %copy-start = (f32[1024,1024]{1,0:T(8,128)S(1)}, f32[1024,1024]{1,0:T(8,128)}, u32[]{:S(2)}) copy-start(f32[1024,1024]{1,0:T(8,128)} %get-tuple-element.25) | copy-start | bytes 12582916
  403.4 103.2 %collective-permute-start.6 = (bf16[1024,2048]{1,0:T(8,128)(2,1)}, bf16[1024,2048]{1,0:T(8,128)(2,1)}, u32[]{:S(2)}, u32[]{:S(2)}) collective-permute-start(bf16[1024,2048]{1,0:T(8,128)(2,1)} %get-tuple-element.20), channel_id=1, source_target_pairs={{0,1},{1,0},{2,3},{3,2},{4,5},{5,4},{6,7},{7,6}} | collective-permute-start | bytes 12582920 | tf_op jit(solution)/shard_map/ppermute | solution.py:434
  403.4 8.8 %collective-permute-start.7 = (bf16[1024,512]{1,0:T(8,128)(2,1)S(1)}, bf16[1024,512]{1,0:T(8,128)(2,1)S(1)}, u32[]{:S(2)}, u32[]{:S(2)}) collective-permute-start(bf16[1024,512]{1,0:T(8,128)(2,1)S(1)} %copy-done.4), channel_id=1, source_target_pairs={{0,1},{1,0},{2,3},{3,2},{4,5},{5,4},{6,7},{7,6}} | collective-permute-start | bytes 3145736 | tf_op jit(solution)/shard_map/ppermute | solution.py:434
  403.9 15.7 %collective-permute-start.9 = (bf16[1024,512]{1,0:T(8,128)(2,1)}, bf16[1024,512]{1,0:T(8,128)(2,1)S(1)}, u32[]{:S(2)}, u32[]{:S(2)}) collective-permute-start(bf16[1024,512]{1,0:T(8,128)(2,1)} %get-tuple-element.24), channel_id=1, source_target_pairs={{0,1},{1,0},{2,3},{3,2},{4,5},{5,4},{6,7},{7,6}} | collective-permute-start | bytes 3145736 | tf_op jit(solution)/shard_map/ppermute | solution.py:434
  413.6 38.9 %collective-permute-start.8 = (bf16[1024,512]{1,0:T(8,128)(2,1)}, bf16[1024,512]{1,0:T(8,128)(2,1)S(1)}, u32[]{:S(2)}, u32[]{:S(2)}) collective-permute-start(bf16[1024,512]{1,0:T(8,128)(2,1)} %add_convert_fusion.3), channel_id=1, source_target_pairs={{0,2},{1,3},{2,0},{3,1},{4,6},{5,7},{6,4},{7,5}} | collective-permute-start | bytes 3145736 | tf_op jit(solution)/shard_map/ppermute | solution.py:434
  413.6 6.0 %copy-start.1 = (f32[1024,512]{1,0:T(8,128)S(1)}, f32[1024,512]{1,0:T(8,128)}, u32[]{:S(2)}) copy-start(f32[1024,512]{1,0:T(8,128)} %get-tuple-element.23) | copy-start | bytes 6291460
  417.6 89.0 %collective-permute-start.12 = (bf16[1024,1024]{1,0:T(8,128)(2,1)}, bf16[1024,1024]{1,0:T(8,128)(2,1)S(1)}, u32[]{:S(2)}, u32[]{:S(2)}) collective-permute-start(bf16[1024,1024]{1,0:T(8,128)(2,1)} %add_convert_fusion.1), channel_id=1, source_target_pairs={{0,2},{1,3},{2,0},{3,1},{4,6},{5,7},{6,4},{7,5}} | collective-permute-start | bytes 6291464 | tf_op jit(solution)/shard_map/ppermute | solution.py:434
  421.0 85.6 %collective-permute-start.10 = (bf16[1024,512]{1,0:T(8,128)(2,1)}, bf16[1024,512]{1,0:T(8,128)(2,1)}, u32[]{:S(2)}, u32[]{:S(2)}) collective-permute-start(bf16[1024,512]{1,0:T(8,128)(2,1)} %add_convert_fusion.2), channel_id=1, source_target_pairs={{0,2},{1,3},{2,0},{3,1},{4,6},{5,7},{6,4},{7,5}} | collective-permute-start | bytes 3145736 | tf_op jit(solution)/shard_map/ppermute | solution.py:434

commit v3 on v2

--- a/solution.py
+++ b/solution.py
@@ -73,25 +73,37 @@
     )(x, s_gate, s_up, s_down, *(() if init is None else (init,)))
 
 
-def gather_block(pos_ref, x, z, b, out):
-    tokens = x.shape[0]
-    row = b * BLK + lax.broadcasted_iota(jnp.int32, (BLK, tokens), 0)
-    hit = pos_ref[0:1, :] == row
-    for j in range(1, pos_ref.shape[0]):
-        hit = hit | (pos_ref[j : j + 1, :] == row)
-    p = jnp.where(hit, 1.0, 0.0).astype(BF16)
-    for c in range(0, x.shape[1], 256):
-        z[out, c : c + 256] = dot(p, x[:, c : c + 256]).astype(BF16)
-
-
-def dispatch_body(nblk_ref, pos_ref, x_ref, z_ref, *, group):
+def picked(values, tokens, first, pos, other=None):
+    row = (first + lax.broadcasted_iota(jnp.int32, (values.shape[0], 1), 0)).astype(F32)
+    tile = jnp.zeros(values.shape, F32)
+    for j in range(pos.shape[0]):
+        hit = jnp.broadcast_to(pos[j : j + 1, tokens], values.shape) == row
+        tile = jnp.where(hit, 1.0 if other is None else other[j : j + 1, tokens], tile)
+    return tile.astype(BF16)
+
+
+def select_rows(pos, first, out):
+    for r in range(0, out.shape[0], 32):
+        for t in range(0, out.shape[1], 256):
+            tile = out.at[r : r + 32, t : t + 256]
+            tile[...] = picked(tile, slice(t, t + 256), first + r, pos)
+
+
+def gather(count, pos, x, z, p, first=0):
+    def one(i, _):
+        select_rows(pos, (first + i + 1) * BLK, p.at[(i + 1) % 2])
+        r = pl.ds(pl.multiple_of(i * BLK, BLK), BLK)
+        for c in range(0, x.shape[1], 256):
+            z[r, c : c + 256] = dot(p[i % 2], x[:, c : c + 256]).astype(BF16)
+        return _
+
+    pl.when(count > 0)(lambda: select_rows(pos, first * BLK, p.at[0]))
+    lax.fori_loop(0, count, one, 0)
+
+
+def dispatch_body(nblk_ref, pos_ref, x_ref, z_ref, p, *, group):
     step = pl.program_id(0)
-
-    def one(i, _):
-        gather_block(pos_ref, x_ref, z_ref, step * group + i, pl.ds(pl.multiple_of(i * BLK, BLK), BLK))
-        return _
-
-    lax.fori_loop(0, jnp.clip(nblk_ref[0] - step * group, 0, group), one, 0)
+    gather(jnp.clip(nblk_ref[0] - step * group, 0, group), pos_ref, x_ref, z_ref, p, step * group)
 
 
 def dispatch(nblk, pos, x, rows, group=4):
@@ -107,6 +119,7 @@
                 pl.BlockSpec((tokens, d), lambda b, n: (0, 0)),
             ],
             out_specs=pl.BlockSpec((BLK * group, d), lambda b, n: (last(b, n), 0)),
+            scratch_shapes=[pltpu.VMEM((2, BLK, tokens), BF16)],
         ),
         out_shape=jax.ShapeDtypeStruct((rows, d), BF16),
         compiler_params=pltpu.CompilerParams(vmem_limit_bytes=60 * MIB),
@@ -126,7 +139,7 @@
     sources = ready + late
     pos_refs, rest = rest[:late], rest[late:]
     x_refs, rest = rest[: late * halves], rest[late * halves :]
-    z_refs, (h_ref, xv, zv, zs, xsem, zsem) = rest[:ready], rest[ready:]
+    z_refs, (h_ref, xv, zv, zs, p, xsem, zsem) = rest[:ready], rest[ready:]
     e = pl.program_id(0)
     width = wg_ref.shape[1]
 
@@ -158,11 +171,7 @@
                 x_copy(i, j).wait()
             q = ready + i
 
-            def one(b, _):
-                gather_block(pos_refs[i], xv.at[i], zv.at[q], b, pl.ds(pl.multiple_of(b * BLK, BLK), BLK))
-                return _
-
-            lax.fori_loop(0, nblk_ref[q], one, 0)
+            gather(nblk_ref[q], pos_refs[i], xv.at[i], zv.at[q], p)
         for q in range(ready):
             each(q, lambda c: c.wait())
 
@@ -217,6 +226,7 @@
                 pltpu.VMEM((late, tokens, d), BF16),
                 pltpu.VMEM((ready + late, rows, d), BF16),
                 pltpu.VMEM((most, d), BF16),
+                pltpu.VMEM((2, BLK, tokens), BF16),
                 pltpu.SemaphoreType.DMA((late, halves)),
                 pltpu.SemaphoreType.DMA((ready,)),
             ],
@@ -229,36 +239,30 @@
 
 
 def comb_body(k_ref, pos_ref, gate_ref, c_ref):
-    q, b = pl.program_id(0), pl.program_id(1)
-    tokens, width = c_ref.shape
-
-    @pl.when(b < k_ref[q])
-    def _():
-        column = b * width + lax.broadcasted_iota(jnp.int32, (BLK, width), 1)
-
-        def one(i, _):
-            t = pl.ds(pl.multiple_of(i * BLK, BLK), BLK)
-            pos, gate = pos_ref[t, :], gate_ref[t, :]
-            value = jnp.zeros((BLK, width), F32)
-            for j in range(pos.shape[1]):
-                value = jnp.where(pos[:, j : j + 1] == column, gate[:, j : j + 1], value)
-            c_ref[t, :] = value.astype(BF16)
-            return _
-
-        lax.fori_loop(0, tokens // BLK, one, 0)
+    q = pl.program_id(0)
+    tokens = c_ref.shape[1]
+
+    def one(i, _):
+        r = pl.ds(pl.multiple_of(i * 32, 32), 32)
+        for t in range(0, tokens, 256):
+            tile = c_ref.at[r, t : t + 256]
+            tile[...] = picked(tile, slice(t, t + 256), i * 32, pos_ref, gate_ref)
+        return _
+
+    lax.fori_loop(0, k_ref[q] * (DEPTH // 32), one, 0)
 
 
 def combine_matrices(k, pos, gate, rows):
-    sources, tokens, top = pos.shape
+    sources, top, tokens = pos.shape
     return pl.pallas_call(
         comb_body,
         grid_spec=pltpu.PrefetchScalarGridSpec(
             num_scalar_prefetch=1,
-            grid=(sources, rows // DEPTH),
-            in_specs=[pl.BlockSpec((None, tokens, top), lambda q, b, k: (q, 0, 0))] * 2,
-            out_specs=pl.BlockSpec((None, tokens, DEPTH), lambda q, b, k: (q, 0, jnp.minimum(b, k[q] - 1))),
+            grid=(sources,),
+            in_specs=[pl.BlockSpec((None, top, tokens), lambda q, k: (q, 0, 0))] * 2,
+            out_specs=pl.BlockSpec((None, rows, tokens), lambda q, k: (q, 0, 0)),
         ),
-        out_shape=jax.ShapeDtypeStruct((sources, tokens, rows), BF16),
+        out_shape=jax.ShapeDtypeStruct((sources, rows, tokens), BF16),
         compiler_params=pltpu.CompilerParams(vmem_limit_bytes=60 * MIB),
         cost_estimate=cost(4 * MIB, 8 * MIB),
         name="comb",
@@ -270,11 +274,12 @@
 
     def whole(depth):
         def part(i, _):
-            t = pl.ds(pl.multiple_of(i * 256, 256), 256)
-            out(t, dot(c[t, :depth], rows[:depth, :]))
+            t = pl.ds(pl.multiple_of(i * 512, 512), 512)
+            both = (((0,), (0,)), ((), ()))
+            out(t, lax.dot_general(c[:depth, t], rows[:depth, :], both, preferred_element_type=F32))
             return _
 
-        lax.fori_loop(0, c.shape[0] // 256, part, 0)
+        lax.fori_loop(0, c.shape[1] // 512, part, 0)
 
     pl.when(k < deepest)(functools.partial(whole, (deepest - 1) * DEPTH))
     pl.when(k >= deepest)(functools.partial(whole, deepest * DEPTH))
@@ -354,9 +359,9 @@
             combine(k_ref[own + i], cb.at[i], outs.at[i], out)
 
 
-def down(n, off, k, w_down, h, comb, kept, column, columns, own, group=3):
+def down(n, off, k, w_down, h, comb, kept, column, columns, own, group=1):
     experts, f, d = w_down.shape
-    sources, tokens, rows = comb.shape
+    sources, rows, tokens = comb.shape
     far = sources - own
     most = h.shape[1]
     once = dict(pipeline_mode=pl.Buffered(1))
@@ -375,7 +380,7 @@
                 pltpu.VMEM((experts, most, f), BF16),
                 pltpu.VMEM((most, columns), BF16),
                 pltpu.VMEM((far, rows, columns), BF16),
-                pltpu.VMEM((far, tokens, rows), BF16),
+                pltpu.VMEM((far, rows, tokens), BF16),
                 pltpu.SemaphoreType.DMA((experts,)),
                 pltpu.SemaphoreType.DMA((far,)),
             ],
@@ -400,14 +405,14 @@
 
 def own_sums(k, comb, kept, shared, columns=512):
     own, rows, d = kept.shape
-    tokens = comb.shape[1]
+    tokens = comb.shape[2]
     return pl.pallas_call(
         own_body,
         grid_spec=pltpu.PrefetchScalarGridSpec(
             num_scalar_prefetch=1,
             grid=(d // columns,),
             in_specs=[
-                pl.BlockSpec((own, tokens, rows), lambda c, *_: (0, 0, 0), pipeline_mode=pl.Buffered(1)),
+                pl.BlockSpec((own, rows, tokens), lambda c, *_: (0, 0, 0), pipeline_mode=pl.Buffered(1)),
                 pl.BlockSpec((own, rows, columns), lambda c, *_: (0, 0, c)),
                 pl.BlockSpec((tokens, columns), lambda c, *_: (0, c)),
             ],
@@ -451,7 +456,7 @@
     n = (n + ROW - 1) // ROW * ROW
     off = jnp.sum(jnp.where(ids[None, :] < ids[:, None], n[:, None, :], 0), axis=2)
     used = jnp.sum(n, axis=1)
-    pos = jnp.where(ok, jnp.sum(jnp.where(is_it, off[:, :, None, None], 0), axis=1) + s, -1)
+    pos = jnp.where(ok, jnp.sum(jnp.where(is_it, off[:, :, None, None], 0), axis=1) + s, -1).astype(F32)
     nf, of = n.reshape(-1), off.reshape(-1)
     nblk = (used + BLK - 1) // BLK
     k = jnp.maximum((used + DEPTH - 1) // DEPTH, rows // DEPTH - 1)
@@ -460,16 +465,15 @@
         return dispatch(nblk[q : q + 1], pos[q], v, rows)
 
     chunks = s_gate.shape[1] // 512
-    cut = chunks * 8 // 11
+    cut = chunks * 7 // 11
     y_shared = shared_expert(x, s_gate, s_up, s_down, 0, cut)
     z = [send(0, x), send(1, near)]
     far_near = swap(far, 1)
-    gates = metas[:, 1].astype(BF16).astype(F32)
-    comb = combine_matrices(k, pos.transpose(0, 2, 1), gates.transpose(0, 2, 1), rows)
+    comb = combine_matrices(k, pos, metas[:, 1].astype(BF16).astype(F32), rows)
     h = gate_up(nf, of, nblk, w_gate, w_up, [pos[2], pos[3]], [[far], [far_near]], z, most)
 
     back, kept, at = [], None, 0
-    for columns in (d // 4, d // 4, d // 2):
+    for columns in (d // 2, d // 2):
         y2, y3, kept = down(nf, of, k, w_down, h, comb, kept, at, columns, 2)
         mine = y2 + swap(y3, 1).astype(F32)
         back.append(swap(mine.astype(BF16), 2))

time: 514 us -> 493 us (0.959); the launches traced: 514 us -> 486 us
  Pallas kernels: 319 us -> 302 us
  waiting for transfers between devices: 150 us -> 137 us
    ppermute x13 -> x11, waiting for transfers between devices: 150 us -> 137 us  [swap(): return lax.ppermute(v, 'ep', [(i, i ^ q) for i in range(members)])]
    pallas_call x1, Pallas kernels: 20.7 us -> 8.95 us  [combine_matrices(): pl.pallas_call(comb_body, grid_spec=pltpu.PrefetchScalarGridSpec(num_scal...]
    pallas_call x3 -> x2, Pallas kernels: 80.4 us -> 74.7 us  [down(): pl.pallas_call(functools.partial(down_body, experts=experts, own=own, far...]
    ppermute x13 -> x11, starting transfers between devices: 19.6 us -> 22.7 us  [swap(): return lax.ppermute(v, 'ep', [(i, i ^ q) for i in range(members)])]
  transfers between devices with their start and end apart: 13 -> 11, of which waited for: 3 -> 3; matrix products, arithmetic and copies ran while one was open for 3% -> 4% of each run, Pallas kernels for 30% -> 37%
where the time goes in v3:
time: 493 us; the launch traced here: 486 us
  Pallas kernels  302 us (61%)
  waiting for transfers between devices  137 us (28%)
  other arithmetic  22.8 us (5%)
  starting transfers between devices  22.7 us (5%)
    ppermute x11, waiting for transfers between devices, swap(): return lax.ppermute(v, 'ep', [(i, i ^ q) for i in range(members)])  137 us
    pallas_call x2, Pallas kernels, shared_expert(): pl.pallas_call(functools.partial(shared_body, rows=rows), grid=(last - fi...  95.3 us
    pallas_call x1, Pallas kernels, gate_up(): pl.pallas_call(functools.partial(gate_up_body, experts=experts, ready=rea...  84.4 us
    pallas_call x2, Pallas kernels, down(): pl.pallas_call(functools.partial(down_body, experts=experts, own=own, far...  74.7 us
    ppermute x11, starting transfers between devices, swap(): return lax.ppermute(v, 'ep', [(i, i ^ q) for i in range(members)])  22.7 us
    pallas_call x1, Pallas kernels, own_sums(): pl.pallas_call(own_body, grid_spec=pltpu.PrefetchScalarGridSpec(num_scala...  20.6 us
    pallas_call x2, Pallas kernels, dispatch(): pl.pallas_call(functools.partial(dispatch_body, group=group), grid_spec=p...  17.8 us
  transfers between devices with their start and end apart: 11, of which 3 were waited for; matrix products, arithmetic and copies ran while one was open for 4% of the time, Pallas kernels for 37%

profile of v3, /device:TPU:0, one launch (start us, length us, event | category | flops | bytes accessed | tf_op | source)
XLA Modules:
  0.0 486.3 jit_solution(3326977722092060257)
XLA Ops:
  0.0 3.3 collective-permute-start.3
  3.3 0.7 convert_bitcast_fusion
  4.1 0.7 fusion.14
  4.8 0.0 collective-permute-start
  4.8 0.0 collective-permute-start.1
  4.9 1.8 collective-permute-start.2
  6.7 0.3 collective-permute-start.5
  7.0 87.9 %collective-permute-done.3.rest_2_ = bf16[1024,2048]{1,0:T(8,128)(2,1)} collective-permute-done((bf16[1024,2048]{1,0:T(8,128)(2,1)}, bf16[1024,2048]{1,0:T(8,128)(2,1)}, u32[]{:S(2)}, u32[]{:S(2)}) %collective-permute-start.3) | collective-permute-done | bytes 4194336 | tf_op jit(solution)/shard_map/ppermute | solution.py:439
  94.9 0.0 collective-permute-start.4
  94.9 56.5 %shared.2.s_ref = f32[1024,2048]{1,0:T(8,128)} custom-call(bf16[1024,2048]{1,0:T(8,128)(2,1)} %bitcast.59, bf16[2048,5632]{1,0:T(8,128)(2,1)} %g_ref.3, bf16[2048,5632]{1,0:T(8,128)(2,1)} %u_ref.3, bf16[5632,2048]{1,0:T(8,128)(2,1)} %d_ref.3), custom_call_target="tpu_custom_call" | custom-call | flops 45097156608 | bytes 44040192 | tf_op jit(solution)/shard_map/shared/pallas_call | solution.py:58
  151.5 0.0 collective-permute-done
  151.5 0.0 collective-permute-done.1
  151.5 0.0 collective-permute-done.2
  151.5 0.1 and_bitcast_fusion
  151.7 1.2 select_reduce_fusion.1
  152.8 0.1 fusion.15
  153.0 0.4 select_reduce_fusion.2
  153.3 0.1 copy.18
  153.4 0.6 reshape.48.off_ref
  154.0 0.1 sub.52
  154.1 0.5 select_reduce_fusion
  154.6 0.6 and_select_fusion
  155.2 0.6 fusion.8.gate_ref
  155.8 0.7 fusion.3.pos_ref
  156.5 9.0 %comb.1.c_ref = bf16[4,1536,1024]{2,1,0:T(8,128)(2,1)} custom-call(s32[4]{0:T(128)} %get-tuple-element.37.k_ref, f32[4,4,1024]{2,1,0:T(4,128)} %fusion.3.pos_ref, f32[4,4,1024]{2,1,0:T(4,128)} %fusion.8.gate_ref), custom_call_target="tpu_custom_call" | custom-call | flops 4194304 | bytes 8388608 | tf_op jit(solution)/shard_map/comb/pallas_call | solution.py:257
  165.5 0.7 fusion.17
  166.1 0.6 slice_bitcast_fusion
  166.7 8.8 %dispatch.2.rest_4_ = bf16[1536,2048]{1,0:T(8,128)(2,1)} custom-call(s32[1]{0:T(128)} %get-tuple-element.35.nblk_ref, f32[4,1024]{1,0:T(4,128)} %get-tuple-element.28.pos_ref, bf16[1024,2048]{1,0:T(8,128)(2,1)} %bitcast.60), custom_call_target="tpu_custom_call" | custom-call | flops 2147483648 | bytes 8388608 | tf_op jit(solution)/shard_map/dispatch/pallas_call | solution.py:112
  175.5 0.5 fusion.12.n_ref
  176.0 0.0 collective-permute-done.5.x_ref
  176.0 9.1 %dispatch.3.rest_5_ = bf16[1536,2048]{1,0:T(8,128)(2,1)} custom-call(s32[1]{0:T(128)} %get-tuple-element.34.nblk_ref, f32[4,1024]{1,0:T(4,128)} %get-tuple-element.27.pos_ref, bf16[1024,2048]{1,0:T(8,128)(2,1)} %collective-permute-done.5.x_ref), custom_call_target="tpu_custom_call" | custom-call | flops 2147483648 | bytes 8388608 | tf_op jit(solution)/shard_map/dispatch/pallas_call | solution.py:112
  185.1 0.0 collective-permute-done.4.rest_3_
  185.1 84.4 %gate_up.1.h_ref = bf16[15,384,1408]{2,1,0:T(8,128)(2,1)} custom-call(s32[60]{0:T(128)} %fusion.12.n_ref, s32[60]{0:T(128)} %reshape.48.off_ref, s32[4]{0:T(128)} %copy-done.2, bf16[15,2048,1408]{2,1,0:T(8,128)(2,1)} %wg_ref.1, bf16[15,2048,1408]{2,1,0:T(8,128)(2,1)} %wu_ref.1, f32[4,1024]{1,0:T(4,128)} %get-tuple-element.30.rest_0_, ...), custom_call_target="tpu_custom_call" | custom-call | flops 44291850240 | bytes 173015040 | tf_op jit(solution)/shard_map/gate_up/pallas_call | solution.py:213
  269.5 37.6 %down.2 = (f32[1024,1024]{1,0:T(8,128)}, bf16[1024,1024]{1,0:T(8,128)(2,1)}, bf16[2,1536,2048]{2,1,0:T(8,128)(2,1)}) custom-call(s32[60]{0:T(128)} %fusion.12.n_ref, s32[60]{0:T(128)} %reshape.48.off_ref, s32[4]{0:T(128)} %get-tuple-element.37.k_ref, bf16[15,1408,2048]{2,1,0:T(8,128)(2,1)} %wd_ref.3, bf16[15,384,1408]{2,1,0:T(8,128)(2,1)} %gate_up.1.h_ref, ...), custom_call_target="tpu_custom_call" | custom-call | flops 11072962560 | bytes 43253760 | tf_op jit(solution)/shard_map/down/pallas_call | solution.py:370
  307.2 12.2 %collective-permute-start.7 = (bf16[1024,1024]{1,0:T(8,128)(2,1)}, bf16[1024,1024]{1,0:T(8,128)(2,1)}, u32[]{:S(2)}, u32[]{:S(2)}) collective-permute-start(bf16[1024,1024]{1,0:T(8,128)(2,1)} %get-tuple-element.18), channel_id=1, source_target_pairs={{0,1},{1,0},{2,3},{3,2},{4,5},{5,4},{6,7},{7,6}} | collective-permute-start | bytes 6291464 | tf_op jit(solution)/shard_map/ppermute | solution.py:439
  319.3 37.1 %down.3 = (f32[1024,1024]{1,0:T(8,128)}, bf16[1024,1024]{1,0:T(8,128)(2,1)}, bf16[2,1536,2048]{2,1,0:T(8,128)(2,1)}) custom-call(s32[60]{0:T(128)} %fusion.12.n_ref, s32[60]{0:T(128)} %reshape.48.off_ref, s32[4]{0:T(128)} %get-tuple-element.37.k_ref, bf16[15,1408,2048]{2,1,0:T(8,128)(2,1)} %wd_ref.3, ...), custom_call_target="tpu_custom_call", output_to_operand_aliasing={{2}: (6, {})} | custom-call | flops 11072962560 | bytes 43253760 | tf_op jit(solution)/shard_map/down/pallas_call | solution.py:370
  356.4 3.0 collective-permute-start.9
  359.4 20.6 %own.1 = (f32[1024,2048]{1,0:T(8,128)}, bf16[1024,2048]{1,0:T(8,128)(2,1)}) custom-call(s32[4]{0:T(128)} %get-tuple-element.37.k_ref, bf16[4,1536,1024]{2,1,0:T(8,128)(2,1)} %comb.1.c_ref, bf16[2,1536,2048]{2,1,0:T(8,128)(2,1)} %get-tuple-element.14.r_ref, f32[1024,2048]{1,0:T(8,128)} %shared.2.s_ref), custom_call_target="tpu_custom_call" | custom-call | flops 12884901888 | bytes 20971520 | tf_op jit(solution)/shard_map/own/pallas_call | solution.py:409
  380.0 0.0 collective-permute-start.6
  380.0 0.0 collective-permute-done.7
  380.0 5.1 %add_convert_fusion.2 = bf16[1024,1024]{1,0:T(8,128)(2,1)} fusion(f32[1024,1024]{1,0:T(8,128)} %get-tuple-element.17, bf16[1024,1024]{1,0:T(8,128)(2,1)} %collective-permute-done.7), kind=kLoop, calls=%fused_computation.3 | loop fusion | flops 3145728 | bytes 8388608 | tf_op jit(solution)/shard_map/convert_element_type | solution.py:479
  385.2 3.8 add_convert_fusion.1
  389.0 2.0 collective-permute-start.10
  391.0 38.7 %shared.3 = f32[1024,2048]{1,0:T(8,128)} custom-call(bf16[1024,2048]{1,0:T(8,128)(2,1)} %bitcast.61, bf16[2048,5632]{1,0:T(8,128)(2,1)} %g_ref.3, bf16[2048,5632]{1,0:T(8,128)(2,1)} %u_ref.3, bf16[5632,2048]{1,0:T(8,128)(2,1)} %d_ref.3, f32[1024,2048]{1,0:T(8,128)} %get-tuple-element.15.rest_0_), custom_call_target="tpu_custom_call" | custom-call | flops 25769803776 | bytes 25165824 | tf_op jit(solution)/shard_map/shared/pallas_call | solution.py:58
  429.7 0.0 collective-permute-done.6
  429.7 4.2 collective-permute-done.8
  433.9 44.6 %collective-permute-done.10 = bf16[1024,1024]{1,0:T(8,128)(2,1)} collective-permute-done((bf16[1024,1024]{1,0:T(8,128)(2,1)}, bf16[1024,1024]{1,0:T(8,128)(2,1)}, u32[]{:S(2)}, u32[]{:S(2)}) %collective-permute-start.10) | collective-permute-done | bytes 2097184 | tf_op jit(solution)/shard_map/ppermute | solution.py:439
  478.5 7.7 %fusion = bf16[1,1,1024,2048]{3,2,1,0:T(8,128)(2,1)} fusion(f32[1024,2048]{1,0:T(8,128)} %shared.3, bf16[1024,2048]{1,0:T(8,128)(2,1)} %collective-permute-done.6, bf16[1024,1024]{1,0:T(8,128)(2,1)} %collective-permute-done.10, bf16[1024,1024]{1,0:T(8,128)(2,1)S(1)} %collective-permute-done.8), kind=kLoop, calls=%fused_computation.1 | loop fusion | flops 16777216 | bytes 20971520 | tf_op jit(solution)/shard_map/broadcast_in_dim | solution.py:484
  (11 shorter events, 0.1 us)
Async XLA Ops:
  0.0 94.9 %collective-permute-start.3 = (bf16[1024,2048]{1,0:T(8,128)(2,1)}, bf16[1024,2048]{1,0:T(8,128)(2,1)}, u32[]{:S(2)}, u32[]{:S(2)}) collective-permute-start(bf16[1024,2048]{1,0:T(8,128)(2,1)} %bitcast.57), channel_id=1, source_target_pairs={{0,2},{1,3},{2,0},{3,1},{4,6},{5,7},{6,4},{7,5}} | collective-permute-start | bytes 12582920 | tf_op jit(solution)/shard_map/ppermute | solution.py:439
  4.8 146.7 %collective-permute-start = (f32[2,4,1024]{2,1,0:T(4,128)S(1)}, f32[2,4,1024]{2,1,0:T(4,128)S(1)}, u32[]{:S(2)}, u32[]{:S(2)}) collective-permute-start(f32[2,4,1024]{2,1,0:T(4,128)S(1)} %get-tuple-element.32), channel_id=1, source_target_pairs={{0,1},{1,0},{2,3},{3,2},{4,5},{5,4},{6,7},{7,6}} | collective-permute-start | bytes 98312 | tf_op jit(solution)/shard_map/ppermute | solution.py:439
  4.8 146.6 %collective-permute-start.1 = (f32[2,4,1024]{2,1,0:T(4,128)S(1)}, f32[2,4,1024]{2,1,0:T(4,128)S(1)}, u32[]{:S(2)}, u32[]{:S(2)}) collective-permute-start(f32[2,4,1024]{2,1,0:T(4,128)S(1)} %get-tuple-element.32), channel_id=1, source_target_pairs={{0,2},{1,3},{2,0},{3,1},{4,6},{5,7},{6,4},{7,5}} | collective-permute-start | bytes 98312 | tf_op jit(solution)/shard_map/ppermute | solution.py:439
  4.9 146.6 %collective-permute-start.2 = (f32[2,4,1024]{2,1,0:T(4,128)S(1)}, f32[2,4,1024]{2,1,0:T(4,128)S(1)}, u32[]{:S(2)}, u32[]{:S(2)}) collective-permute-start(f32[2,4,1024]{2,1,0:T(4,128)S(1)} %get-tuple-element.32), channel_id=1, source_target_pairs={{0,3},{1,2},{2,1},{3,0},{4,7},{5,6},{6,5},{7,4}} | collective-permute-start | bytes 98312 | tf_op jit(solution)/shard_map/ppermute | solution.py:439
  6.7 169.4 %collective-permute-start.5 = (bf16[1024,2048]{1,0:T(8,128)(2,1)}, bf16[1024,2048]{1,0:T(8,128)(2,1)}, u32[]{:S(2)}, u32[]{:S(2)}) collective-permute-start(bf16[1024,2048]{1,0:T(8,128)(2,1)} %bitcast.58), channel_id=1, source_target_pairs={{0,1},{1,0},{2,3},{3,2},{4,5},{5,4},{6,7},{7,6}} | collective-permute-start | bytes 12582920 | tf_op jit(solution)/shard_map/ppermute | solution.py:439
  94.9 90.2 %collective-permute-start.4 = (bf16[1024,2048]{1,0:T(8,128)(2,1)}, bf16[1024,2048]{1,0:T(8,128)(2,1)}, u32[]{:S(2)}, u32[]{:S(2)}) collective-permute-start(bf16[1024,2048]{1,0:T(8,128)(2,1)} %collective-permute-done.3.rest_2_), channel_id=1, source_target_pairs={{0,1},{1,0},{2,3},{3,2},{4,5},{5,4},{6,7},{7,6}} | collective-permute-start | bytes 12582920 | tf_op jit(solution)/shard_map/ppermute | solution.py:439
  155.2 10.3 %copy-start.2 = (s32[4]{0:T(128)}, s32[4]{0:T(128)S(1)}, u32[]{:S(2)}) copy-start(s32[4]{0:T(128)S(1)} %get-tuple-element.36.nblk_ref) | copy-start | bytes 52
  156.5 9.6 %copy-start.1 = (f32[4,4,1024]{2,1,0:T(4,128)S(1)}, f32[4,4,1024]{2,1,0:T(4,128)}, u32[]{:S(2)}) copy-start(f32[4,4,1024]{2,1,0:T(4,128)} %fusion.3.pos_ref) | copy-start | bytes 196612
  307.2 72.9 %collective-permute-start.7 = (bf16[1024,1024]{1,0:T(8,128)(2,1)}, bf16[1024,1024]{1,0:T(8,128)(2,1)}, u32[]{:S(2)}, u32[]{:S(2)}) collective-permute-start(bf16[1024,1024]{1,0:T(8,128)(2,1)} %get-tuple-element.18), channel_id=1, source_target_pairs={{0,1},{1,0},{2,3},{3,2},{4,5},{5,4},{6,7},{7,6}} | collective-permute-start | bytes 6291464 | tf_op jit(solution)/shard_map/ppermute | solution.py:439
  356.4 28.8 %collective-permute-start.9 = (bf16[1024,1024]{1,0:T(8,128)(2,1)}, bf16[1024,1024]{1,0:T(8,128)(2,1)}, u32[]{:S(2)}, u32[]{:S(2)}) collective-permute-start(bf16[1024,1024]{1,0:T(8,128)(2,1)} %get-tuple-element.20), channel_id=1, source_target_pairs={{0,1},{1,0},{2,3},{3,2},{4,5},{5,4},{6,7},{7,6}} | collective-permute-start | bytes 6291464 | tf_op jit(solution)/shard_map/ppermute | solution.py:439
  380.0 49.7 %collective-permute-start.6 = (bf16[1024,2048]{1,0:T(8,128)(2,1)}, bf16[1024,2048]{1,0:T(8,128)(2,1)}, u32[]{:S(2)}, u32[]{:S(2)}) collective-permute-start(bf16[1024,2048]{1,0:T(8,128)(2,1)} %get-tuple-element.16), channel_id=1, source_target_pairs={{0,1},{1,0},{2,3},{3,2},{4,5},{5,4},{6,7},{7,6}} | collective-permute-start | bytes 12582920 | tf_op jit(solution)/shard_map/ppermute | solution.py:439
  380.0 5.1 %copy-start = (f32[1024,1024]{1,0:T(8,128)S(1)}, f32[1024,1024]{1,0:T(8,128)}, u32[]{:S(2)}) copy-start(f32[1024,1024]{1,0:T(8,128)} %get-tuple-element.19) | copy-start | bytes 12582916
  385.2 48.7 %collective-permute-start.8 = (bf16[1024,1024]{1,0:T(8,128)(2,1)}, bf16[1024,1024]{1,0:T(8,128)(2,1)S(1)}, u32[]{:S(2)}, u32[]{:S(2)}) collective-permute-start(bf16[1024,1024]{1,0:T(8,128)(2,1)} %add_convert_fusion.2), channel_id=1, source_target_pairs={{0,2},{1,3},{2,0},{3,1},{4,6},{5,7},{6,4},{7,5}} | collective-permute-start | bytes 6291464 | tf_op jit(solution)/shard_map/ppermute | solution.py:439
  389.0 89.5 %collective-permute-start.10 = (bf16[1024,1024]{1,0:T(8,128)(2,1)}, bf16[1024,1024]{1,0:T(8,128)(2,1)}, u32[]{:S(2)}, u32[]{:S(2)}) collective-permute-start(bf16[1024,1024]{1,0:T(8,128)(2,1)} %add_convert_fusion.1), channel_id=1, source_target_pairs={{0,2},{1,3},{2,0},{3,1},{4,6},{5,7},{6,4},{7,5}} | collective-permute-start | bytes 6291464 | tf_op jit(solution)/shard_map/ppermute | solution.py:439

commit v4 on v3

--- a/solution.py
+++ b/solution.py
@@ -23,18 +23,26 @@
     return pl.CostEstimate(flops=int(flops), bytes_accessed=int(nbytes), transcendentals=0)
 
 
-def shared_body(x_ref, g_ref, u_ref, d_ref, *rest, rows):
-    init_ref, y_ref = rest if len(rest) == 2 else (None, rest[0])
+def shared_body(*refs, rows, steps, more):
+    if more:
+        k_ref, x_ref, g_ref, u_ref, d_ref, init_ref, c_ref, r_ref, y_ref, ib, cb, rb, sem = refs
+        copies = [
+            pltpu.make_async_copy(init_ref, ib, sem.at[0]),
+            pltpu.make_async_copy(c_ref.at[0], cb, sem.at[1]),
+            pltpu.make_async_copy(r_ref.at[0], rb, sem.at[2]),
+        ]
+    else:
+        x_ref, g_ref, u_ref, d_ref, y_ref = refs
     step = pl.program_id(0)
     tokens, width = x_ref.shape[0], g_ref.shape[1]
     depth = d_ref.shape[1]
 
     @pl.when(step == 0)
     def _():
-        if init_ref is None:
-            y_ref[...] = jnp.zeros_like(y_ref)
-        else:
-            y_ref[...] = init_ref[...]
+        if more:
+            for copy in copies:
+                copy.start()
+        y_ref[...] = jnp.zeros_like(y_ref)
 
     def one(i, _):
         r = pl.ds(pl.multiple_of(i * rows, rows), rows)
@@ -51,26 +59,52 @@
 
     lax.fori_loop(0, tokens // rows, one, 0)
 
-
-def shared_expert(x, s_gate, s_up, s_down, first, last, init=None, chunk=512, rows=512):
+    if more:
+
+        @pl.when(step == steps - 1)
+        def _():
+            for copy in copies:
+                copy.wait()
+
+            def out(t, c, v):
+                y_ref[t, c] += v + ib[t, c]
+
+            combine(k_ref[0], cb, rb, out)
+
+
+def shared_expert(x, s_gate, s_up, s_down, first, last, more=None, chunk=512, rows=512):
     tokens, d = x.shape
     once = dict(pipeline_mode=pl.Buffered(1))
+    scratch, rest = [], ()
+    if more is not None:
+        k, *rest = more
+        _, comb, kept = rest
+        scratch = [
+            pltpu.VMEM((tokens, d), F32),
+            pltpu.VMEM(comb.shape[1:], BF16),
+            pltpu.VMEM(kept.shape[1:], BF16),
+            pltpu.SemaphoreType.DMA((3,)),
+        ]
     return pl.pallas_call(
-        functools.partial(shared_body, rows=rows),
-        grid=(last - first,),
-        in_specs=[
-            pl.BlockSpec((tokens, d), lambda i: (0, 0), **once),
-            pl.BlockSpec((d, chunk), lambda i: (0, i + first)),
-            pl.BlockSpec((d, chunk), lambda i: (0, i + first)),
-            pl.BlockSpec((chunk, d), lambda i: (i + first, 0)),
-        ]
-        + ([] if init is None else [pl.BlockSpec((tokens, d), lambda i: (0, 0), **once)]),
-        out_specs=pl.BlockSpec((tokens, d), lambda i: (0, 0), **once),
+        functools.partial(shared_body, rows=rows, steps=last - first, more=more is not None),
+        grid_spec=pltpu.PrefetchScalarGridSpec(
+            num_scalar_prefetch=0 if more is None else 1,
+            grid=(last - first,),
+            in_specs=[
+                pl.BlockSpec((tokens, d), lambda i, *_: (0, 0), **once),
+                pl.BlockSpec((d, chunk), lambda i, *_: (0, i + first)),
+                pl.BlockSpec((d, chunk), lambda i, *_: (0, i + first)),
+                pl.BlockSpec((chunk, d), lambda i, *_: (i + first, 0)),
+            ]
+            + [pl.BlockSpec(memory_space=pl.ANY)] * len(rest),
+            out_specs=pl.BlockSpec((tokens, d), lambda i, *_: (0, 0), **once),
+            scratch_shapes=scratch,
+        ),
         out_shape=jax.ShapeDtypeStruct((tokens, d), F32),
         compiler_params=pltpu.CompilerParams(vmem_limit_bytes=60 * MIB),
         cost_estimate=cost(6 * tokens * d * chunk * (last - first), 6 * d * chunk * (last - first)),
         name="shared",
-    )(x, s_gate, s_up, s_down, *(() if init is None else (init,)))
+    )(*([] if more is None else [k]), x, s_gate, s_up, s_down, *rest)
 
 
 def picked(values, tokens, first, pos, other=None):
@@ -274,19 +308,21 @@
 
     def whole(depth):
         def part(i, _):
-            t = pl.ds(pl.multiple_of(i * 512, 512), 512)
+            t = pl.ds(pl.multiple_of(i * 256, 256), 256)
             both = (((0,), (0,)), ((), ()))
-            out(t, lax.dot_general(c[:depth, t], rows[:depth, :], both, preferred_element_type=F32))
+            for n in range(0, rows.shape[1], 256):
+                n = slice(n, n + 256)
+                out(t, n, lax.dot_general(c[:depth, t], rows[:depth, n], both, preferred_element_type=F32))
             return _
 
-        lax.fori_loop(0, c.shape[1] // 512, part, 0)
+        lax.fori_loop(0, c.shape[1] // 256, part, 0)
 
     pl.when(k < deepest)(functools.partial(whole, (deepest - 1) * DEPTH))
     pl.when(k >= deepest)(functools.partial(whole, deepest * DEPTH))
 
 
-def down_body(n_ref, off_ref, k_ref, wd_ref, h_ref, c_ref, *rest, experts, own, far, group):
-    y_refs, own_ref, (hb, stage, outs, cb, sem, csem) = rest[-far - 7 : -7], rest[-7], rest[-6:]
+def down_body(n_ref, off_ref, k_ref, wd_ref, h_ref, c_ref, *rest, experts, own, far, group, column):
+    y_refs, kept_ref, (hb, stage, outs, cb, sem, csem, osem) = rest[-far - 8 : -8], rest[-8], rest[-7:]
     step = pl.program_id(0)
     sources = own + far
 
@@ -310,8 +346,15 @@
         lax.fori_loop(0, experts, fetch, 0)
         for i in range(far):
             c_copy(i).start()
-        outs[...] = jnp.zeros_like(outs)
-        own_ref[...] = jnp.zeros_like(own_ref)
+        zeros = jnp.zeros((ROW, outs.shape[2]), BF16)
+        for q in range(sources):
+            used = off_ref[(q + 1) * experts - 1] + n_ref[(q + 1) * experts - 1]
+
+            def clear(i, _):
+                outs[q, pl.ds(pl.multiple_of(i * ROW, ROW), ROW), :] = zeros
+                return _
+
+            lax.fori_loop(used // ROW, outs.shape[1] // ROW, clear, 0)
 
     def expert(g, _):
         e = step * group + g
@@ -334,12 +377,11 @@
         for q in range(sources):
             n = n_ref[q * experts + e]
             off = off_ref[q * experts + e]
-            to = own_ref.at[q] if q < own else outs.at[q - own]
 
             def move(i, _):
                 src = pl.ds(pl.multiple_of(at + i * ROW, ROW), ROW)
                 dst = pl.ds(pl.multiple_of(off + i * ROW, ROW), ROW)
-                to[dst, :] = stage[src, :]
+                outs[q, dst, :] = stage[src, :]
                 return _
 
             lax.fori_loop(0, n // ROW, move, 0)
@@ -350,16 +392,20 @@
 
     @pl.when(step == experts // group - 1)
     def _():
+        columns = pl.ds(column, outs.shape[2])
+        leave = pltpu.make_async_copy(outs.at[:own], kept_ref.at[:, :, columns], osem)
+        leave.start()
         for i in reversed(range(far)):
             c_copy(i).wait()
 
-            def out(t, v):
-                y_refs[i][t, :] = v.astype(y_refs[i].dtype)
-
-            combine(k_ref[own + i], cb.at[i], outs.at[i], out)
-
-
-def down(n, off, k, w_down, h, comb, kept, column, columns, own, group=1):
+            def out(t, c, v):
+                y_refs[i][t, c] = v.astype(y_refs[i].dtype)
+
+            combine(k_ref[own + i], cb.at[i], outs.at[own + i], out)
+        leave.wait()
+
+
+def down(n, off, k, w_down, h, comb, kept, column, columns, own, group=3):
     experts, f, d = w_down.shape
     sources, rows, tokens = comb.shape
     far = sources - own
@@ -368,21 +414,22 @@
     at = column // columns
     aliased = [] if kept is None else [kept]
     return pl.pallas_call(
-        functools.partial(down_body, experts=experts, own=own, far=far, group=group),
+        functools.partial(down_body, experts=experts, own=own, far=far, group=group, column=column),
         grid_spec=pltpu.PrefetchScalarGridSpec(
             num_scalar_prefetch=3,
             grid=(experts // group,),
             in_specs=[pl.BlockSpec((group, f, columns), lambda e, *_: (e, 0, at))]
             + [pl.BlockSpec(memory_space=pl.ANY)] * (2 + len(aliased)),
             out_specs=[pl.BlockSpec((tokens, columns), lambda e, *_: (0, 0), **once)] * far
-            + [pl.BlockSpec((own, rows, columns), lambda e, *_: (0, 0, at), **once)],
+            + [pl.BlockSpec(memory_space=pl.ANY)],
             scratch_shapes=[
                 pltpu.VMEM((experts, most, f), BF16),
                 pltpu.VMEM((most, columns), BF16),
-                pltpu.VMEM((far, rows, columns), BF16),
+                pltpu.VMEM((sources, rows, columns), BF16),
                 pltpu.VMEM((far, rows, tokens), BF16),
                 pltpu.SemaphoreType.DMA((experts,)),
                 pltpu.SemaphoreType.DMA((far,)),
+                pltpu.SemaphoreType.DMA,
             ],
         ),
         out_shape=[jax.ShapeDtypeStruct((tokens, columns), F32 if i == 0 else BF16) for i in range(far)]
@@ -394,35 +441,32 @@
     )(n, off, k, w_down, h, comb, *aliased)
 
 
-def own_body(k_ref, c_ref, r_ref, s_ref, *y_refs):
-    for i in reversed(range(len(y_refs))):
-
-        def out(t, v):
-            y_refs[i][t, :] = v + s_ref[t, :] if i == 0 else v.astype(BF16)
-
-        combine(k_ref[i], c_ref.at[i], r_ref.at[i], out)
-
-
-def own_sums(k, comb, kept, shared, columns=512):
+def side_body(k_ref, c_ref, r_ref, y_ref, *, member):
+    def out(t, c, v):
+        y_ref[t, c] = v.astype(BF16)
+
+    combine(k_ref[member], c_ref, r_ref, out)
+
+
+def side_sums(k, comb, kept, member, columns=1024):
     own, rows, d = kept.shape
     tokens = comb.shape[2]
     return pl.pallas_call(
-        own_body,
+        functools.partial(side_body, member=member),
         grid_spec=pltpu.PrefetchScalarGridSpec(
             num_scalar_prefetch=1,
             grid=(d // columns,),
             in_specs=[
-                pl.BlockSpec((own, rows, tokens), lambda c, *_: (0, 0, 0), pipeline_mode=pl.Buffered(1)),
-                pl.BlockSpec((own, rows, columns), lambda c, *_: (0, 0, c)),
-                pl.BlockSpec((tokens, columns), lambda c, *_: (0, c)),
+                pl.BlockSpec((None, rows, tokens), lambda c, *_: (member, 0, 0), pipeline_mode=pl.Buffered(1)),
+                pl.BlockSpec((None, rows, columns), lambda c, *_: (member, 0, c)),
             ],
-            out_specs=[pl.BlockSpec((tokens, columns), lambda c, *_: (0, c))] * own,
+            out_specs=pl.BlockSpec((tokens, columns), lambda c, *_: (0, c)),
         ),
-        out_shape=[jax.ShapeDtypeStruct((tokens, d), F32 if i == 0 else BF16) for i in range(own)],
+        out_shape=jax.ShapeDtypeStruct((tokens, d), BF16),
         compiler_params=pltpu.CompilerParams(vmem_limit_bytes=60 * MIB),
-        cost_estimate=cost(4 * tokens * rows * d, 20 * MIB),
-        name="own",
-    )(k, comb, kept, shared)
+        cost_estimate=cost(2 * tokens * rows * d, 14 * MIB),
+        name="side",
+    )(k, comb, kept)
 
 
 def layer(x, expert, slot, gate, w_gate, w_up, w_down, s_gate, s_up, s_down, *, members, experts):
@@ -465,7 +509,7 @@
         return dispatch(nblk[q : q + 1], pos[q], v, rows)
 
     chunks = s_gate.shape[1] // 512
-    cut = chunks * 7 // 11
+    cut = chunks * 8 // 11
     y_shared = shared_expert(x, s_gate, s_up, s_down, 0, cut)
     z = [send(0, x), send(1, near)]
     far_near = swap(far, 1)
@@ -478,9 +522,9 @@
         mine = y2 + swap(y3, 1).astype(F32)
         back.append(swap(mine.astype(BF16), 2))
         at += columns
-    y0, y1 = own_sums(k, comb, kept, y_shared)
+    y1 = side_sums(k, comb, kept, 1)
     side = swap(y1, 1)
-    y_shared = shared_expert(x, s_gate, s_up, s_down, cut, chunks, y0)
+    y_shared = shared_expert(x, s_gate, s_up, s_down, cut, chunks, (k, y_shared, comb, kept))
     return (y_shared + side.astype(F32) + jnp.concatenate(back, axis=1).astype(F32)).astype(BF16)[None, None]
 
 

time: 493 us -> 429 us (0.87)
  waiting for transfers between devices: 137 us -> 94.7 us
  Pallas kernels: 302 us -> 289 us
  starting transfers between devices: 22.7 us -> 17.7 us
    ppermute x11, waiting for transfers between devices: 137 us -> 94.7 us  [swap(): return lax.ppermute(v, 'ep', [(i, i ^ q) for i in range(members)])]
    pallas_call x2, Pallas kernels: 74.7 us -> 66.9 us  [down(): pl.pallas_call(functools.partial(down_body, experts=experts, own=own, far...]
    pallas_call x3, Pallas kernels: 116 us -> 111 us  [the longest x2 99.2 us: shared_expert(): pl.pallas_call(functools.partial(shared_body, rows=rows, steps=last - fir...]
    ppermute x11, starting transfers between devices: 22.7 us -> 17.7 us  [swap(): return lax.ppermute(v, 'ep', [(i, i ^ q) for i in range(members)])]
  transfers between devices with their start and end apart: 11 -> 11, of which waited for: 3 -> 4; matrix products, arithmetic and copies ran while one was open for 4% -> 4% of each run, Pallas kernels for 37% -> 40%
where the time goes in v4:
time: 429 us; the launch traced here: 426 us
  Pallas kernels  289 us (67%)
  waiting for transfers between devices  94.7 us (22%)
  other arithmetic  22.8 us (5%)
  starting transfers between devices  17.7 us (4%)
    pallas_call x2, Pallas kernels, shared_expert(): pl.pallas_call(functools.partial(shared_body, rows=rows, steps=last - fir...  99.2 us
    ppermute x11, waiting for transfers between devices, swap(): return lax.ppermute(v, 'ep', [(i, i ^ q) for i in range(members)])  94.7 us
    pallas_call x1, Pallas kernels, gate_up(): pl.pallas_call(functools.partial(gate_up_body, experts=experts, ready=rea...  84.1 us
    pallas_call x2, Pallas kernels, down(): pl.pallas_call(functools.partial(down_body, experts=experts, own=own, far...  66.9 us
    pallas_call x2, Pallas kernels, dispatch(): pl.pallas_call(functools.partial(dispatch_body, group=group), grid_spec=p...  17.8 us
    ppermute x11, starting transfers between devices, swap(): return lax.ppermute(v, 'ep', [(i, i ^ q) for i in range(members)])  17.7 us
    pallas_call x1, Pallas kernels, side_sums(): pl.pallas_call(functools.partial(side_body, member=member), grid_spec=plt...  11.4 us
    pallas_call x1, Pallas kernels, combine_matrices(): pl.pallas_call(comb_body, grid_spec=pltpu.PrefetchScalarGridSpec(num_scal...  9.22 us
  transfers between devices with their start and end apart: 11, of which 4 were waited for; matrix products, arithmetic and copies ran while one was open for 4% of the time, Pallas kernels for 40%

profile of v4, /device:TPU:0, one launch (start us, length us, event | category | flops | bytes accessed | tf_op | source)
XLA Modules:
  0.0 426.1 jit_solution(2290504606462903203)
XLA Ops:
  0.0 3.3 collective-permute-start.3
  3.3 0.0 collective-permute-start.5
  3.3 90.9 %collective-permute-done.3.rest_2_ = bf16[1024,2048]{1,0:T(8,128)(2,1)} collective-permute-done((bf16[1024,2048]{1,0:T(8,128)(2,1)}, bf16[1024,2048]{1,0:T(8,128)(2,1)}, u32[]{:S(2)}, u32[]{:S(2)}) %collective-permute-start.3) | collective-permute-done | bytes 4194336 | tf_op jit(solution)/shard_map/ppermute | solution.py:483
  94.2 0.0 collective-permute-start.4
  94.2 0.7 convert_bitcast_fusion
  94.9 0.7 fusion.14
  95.7 1.8 collective-permute-start.1
  97.4 0.1 collective-permute-start.2
  97.6 0.3 collective-permute-start
  97.9 1.8 collective-permute-done.1
  99.6 1.2 collective-permute-done.2
  100.8 0.9 collective-permute-done
  101.7 0.1 and_bitcast_fusion
  101.9 1.2 select_reduce_fusion.1
  103.0 0.1 fusion.15
  103.2 0.4 select_reduce_fusion.2
  103.5 0.1 copy.18
  103.6 0.6 reshape.48.off_ref
  104.2 0.1 sub.52
  104.3 0.5 select_reduce_fusion
  104.9 0.6 and_select_fusion
  105.4 0.6 fusion.8.gate_ref
  106.1 0.7 fusion.3.pos_ref
  106.7 9.2 %comb.1.c_ref.refs_6_ = bf16[4,1536,1024]{2,1,0:T(8,128)(2,1)} custom-call(s32[4]{0:T(128)} %get-tuple-element.33.k_ref.refs_0_, f32[4,4,1024]{2,1,0:T(4,128)} %fusion.3.pos_ref, f32[4,4,1024]{2,1,0:T(4,128)} %fusion.8.gate_ref), custom_call_target="tpu_custom_call" | custom-call | flops 4194304 | bytes 8388608 | tf_op jit(solution)/shard_map/comb/pallas_call | solution.py:291
  116.0 0.6 fusion.17
  116.6 0.6 slice_bitcast_fusion
  117.2 8.8 %dispatch.2.rest_4_ = bf16[1536,2048]{1,0:T(8,128)(2,1)} custom-call(s32[1]{0:T(128)} %get-tuple-element.31.nblk_ref, f32[4,1024]{1,0:T(4,128)} %get-tuple-element.24.pos_ref, bf16[1024,2048]{1,0:T(8,128)(2,1)} %bitcast.59), custom_call_target="tpu_custom_call" | custom-call | flops 2147483648 | bytes 8388608 | tf_op jit(solution)/shard_map/dispatch/pallas_call | solution.py:146
  126.0 0.5 fusion.12.n_ref
  126.5 9.0 %dispatch.3.rest_5_ = bf16[1536,2048]{1,0:T(8,128)(2,1)} custom-call(s32[1]{0:T(128)} %get-tuple-element.30.nblk_ref, f32[4,1024]{1,0:T(4,128)} %get-tuple-element.23.pos_ref, bf16[1024,2048]{1,0:T(8,128)(2,1)} %collective-permute-done.5.x_ref), custom_call_target="tpu_custom_call" | custom-call | flops 2147483648 | bytes 8388608 | tf_op jit(solution)/shard_map/dispatch/pallas_call | solution.py:146
  135.5 0.0 collective-permute-done.4.rest_3_
  135.5 84.1 %gate_up.1.h_ref = bf16[15,384,1408]{2,1,0:T(8,128)(2,1)} custom-call(s32[60]{0:T(128)} %fusion.12.n_ref, s32[60]{0:T(128)} %reshape.48.off_ref, s32[4]{0:T(128)} %copy-done.2, bf16[15,2048,1408]{2,1,0:T(8,128)(2,1)} %wg_ref.1, bf16[15,2048,1408]{2,1,0:T(8,128)(2,1)} %wu_ref.1, f32[4,1024]{1,0:T(4,128)} %get-tuple-element.26.rest_0_, ...), custom_call_target="tpu_custom_call" | custom-call | flops 44291850240 | bytes 173015040 | tf_op jit(solution)/shard_map/gate_up/pallas_call | solution.py:247
  219.5 33.7 %down.2 = (f32[1024,1024]{1,0:T(8,128)}, bf16[1024,1024]{1,0:T(8,128)(2,1)}, bf16[2,1536,2048]{2,1,0:T(8,128)(2,1)}) custom-call(s32[60]{0:T(128)} %fusion.12.n_ref, s32[60]{0:T(128)} %reshape.48.off_ref, s32[4]{0:T(128)} %get-tuple-element.33.k_ref.refs_0_, bf16[15,1408,2048]{2,1,0:T(8,128)(2,1)} %wd_ref.3, bf16[15,384,1408]{2,1,0:T(8,128)(2,1)} %gate_up.1.h_ref, ...), custom_call_target="tpu_custom_call" | custom-call | flops 11072962560 | bytes 43253760 | tf_op jit(solution)/shard_map/down/pallas_call | solution.py:416
  253.2 9.4 %collective-permute-start.7 = (bf16[1024,1024]{1,0:T(8,128)(2,1)}, bf16[1024,1024]{1,0:T(8,128)(2,1)}, u32[]{:S(2)}, u32[]{:S(2)}) collective-permute-start(bf16[1024,1024]{1,0:T(8,128)(2,1)} %get-tuple-element.14), channel_id=1, source_target_pairs={{0,1},{1,0},{2,3},{3,2},{4,5},{5,4},{6,7},{7,6}} | collective-permute-start | bytes 6291464 | tf_op jit(solution)/shard_map/ppermute | solution.py:483
  262.7 33.2 %down.3 = (f32[1024,1024]{1,0:T(8,128)}, bf16[1024,1024]{1,0:T(8,128)(2,1)}, bf16[2,1536,2048]{2,1,0:T(8,128)(2,1)}) custom-call(s32[60]{0:T(128)} %fusion.12.n_ref, s32[60]{0:T(128)} %reshape.48.off_ref, s32[4]{0:T(128)} %get-tuple-element.33.k_ref.refs_0_, bf16[15,1408,2048]{2,1,0:T(8,128)(2,1)} %wd_ref.3, ...), custom_call_target="tpu_custom_call", output_to_operand_aliasing={{2}: (6, {})} | custom-call | flops 11072962560 | bytes 43253760 | tf_op jit(solution)/shard_map/down/pallas_call | solution.py:416
  295.9 0.8 collective-permute-start.9
  296.7 11.4 %side.1 = bf16[1024,2048]{1,0:T(8,128)(2,1)} custom-call(s32[4]{0:T(128)} %get-tuple-element.33.k_ref.refs_0_, bf16[4,1536,1024]{2,1,0:T(8,128)(2,1)} %comb.1.c_ref.refs_6_, bf16[2,1536,2048]{2,1,0:T(8,128)(2,1)} %get-tuple-element.12.refs_7_.r_ref), custom_call_target="tpu_custom_call" | custom-call | flops 6442450944 | bytes 14680064 | tf_op jit(solution)/shard_map/side/pallas_call | solution.py:454
  308.0 0.0 collective-permute-start.6
  308.1 0.0 collective-permute-done.7
  308.1 5.1 %add_convert_fusion.2 = bf16[1024,1024]{1,0:T(8,128)(2,1)} fusion(f32[1024,1024]{1,0:T(8,128)} %get-tuple-element.13, bf16[1024,1024]{1,0:T(8,128)(2,1)} %collective-permute-done.7), kind=kLoop, calls=%fused_computation.3 | loop fusion | flops 3145728 | bytes 8388608 | tf_op jit(solution)/shard_map/convert_element_type | solution.py:523
  313.2 0.0 collective-permute-start.8
  313.2 0.0 collective-permute-done.9
  313.2 3.8 add_convert_fusion.1
  317.0 2.0 collective-permute-start.10
  319.0 63.5 %shared.2.refs_5_ = f32[1024,2048]{1,0:T(8,128)} custom-call(bf16[1024,2048]{1,0:T(8,128)(2,1)} %bitcast.60, bf16[2048,5632]{1,0:T(8,128)(2,1)} %refs_2_.3, bf16[2048,5632]{1,0:T(8,128)(2,1)} %refs_3_.3, bf16[5632,2048]{1,0:T(8,128)(2,1)} %refs_4_.1), custom_call_target="tpu_custom_call" | custom-call | flops 51539607552 | bytes 50331648 | tf_op jit(solution)/shard_map/shared/pallas_call | solution.py:88
  382.5 35.7 %shared.3 = f32[1024,2048]{1,0:T(8,128)} custom-call(s32[4]{0:T(128)} %get-tuple-element.33.k_ref.refs_0_, bf16[1024,2048]{1,0:T(8,128)(2,1)} %bitcast.61, bf16[2048,5632]{1,0:T(8,128)(2,1)} %refs_2_.3, bf16[2048,5632]{1,0:T(8,128)(2,1)} %refs_3_.3, bf16[5632,2048]{1,0:T(8,128)(2,1)} %refs_4_.1, f32[1024,2048]{1,0:T(8,128)} %shared.2.refs_5_, ...), custom_call_target="tpu_custom_call" | custom-call | flops 19327352832 | bytes 18874368 | tf_op jit(solution)/shard_map/shared/pallas_call | solution.py:88
  418.2 0.0 collective-permute-done.8
  418.2 0.0 collective-permute-done.10
  418.2 7.7 %fusion = bf16[1,1,1024,2048]{3,2,1,0:T(8,128)(2,1)} fusion(f32[1024,2048]{1,0:T(8,128)} %shared.3, bf16[1024,2048]{1,0:T(8,128)(2,1)} %collective-permute-done.6, bf16[1024,1024]{1,0:T(8,128)(2,1)} %collective-permute-done.10, bf16[1024,1024]{1,0:T(8,128)(2,1)S(1)} %collective-permute-done.8), kind=kLoop, calls=%fused_computation.1 | loop fusion | flops 16777216 | bytes 20971520 | tf_op jit(solution)/shard_map/broadcast_in_dim | solution.py:528
  (11 shorter events, 0.1 us)
Async XLA Ops:
  0.0 94.2 %collective-permute-start.3 = (bf16[1024,2048]{1,0:T(8,128)(2,1)}, bf16[1024,2048]{1,0:T(8,128)(2,1)}, u32[]{:S(2)}, u32[]{:S(2)}) collective-permute-start(bf16[1024,2048]{1,0:T(8,128)(2,1)} %bitcast.57), channel_id=1, source_target_pairs={{0,2},{1,3},{2,0},{3,1},{4,6},{5,7},{6,4},{7,5}} | collective-permute-start | bytes 12582920 | tf_op jit(solution)/shard_map/ppermute | solution.py:483
  3.3 123.2 %collective-permute-start.5 = (bf16[1024,2048]{1,0:T(8,128)(2,1)}, bf16[1024,2048]{1,0:T(8,128)(2,1)}, u32[]{:S(2)}, u32[]{:S(2)}) collective-permute-start(bf16[1024,2048]{1,0:T(8,128)(2,1)} %bitcast.58), channel_id=1, source_target_pairs={{0,1},{1,0},{2,3},{3,2},{4,5},{5,4},{6,7},{7,6}} | collective-permute-start | bytes 12582920 | tf_op jit(solution)/shard_map/ppermute | solution.py:483
  94.2 41.3 %collective-permute-start.4 = (bf16[1024,2048]{1,0:T(8,128)(2,1)}, bf16[1024,2048]{1,0:T(8,128)(2,1)}, u32[]{:S(2)}, u32[]{:S(2)}) collective-permute-start(bf16[1024,2048]{1,0:T(8,128)(2,1)} %collective-permute-done.3.rest_2_), channel_id=1, source_target_pairs={{0,1},{1,0},{2,3},{3,2},{4,5},{5,4},{6,7},{7,6}} | collective-permute-start | bytes 12582920 | tf_op jit(solution)/shard_map/ppermute | solution.py:483
  95.7 3.9 collective-permute-start.1
  97.4 3.3 collective-permute-start.2
  97.6 4.1 collective-permute-start
  105.4 10.5 %copy-start.2 = (s32[4]{0:T(128)}, s32[4]{0:T(128)S(1)}, u32[]{:S(2)}) copy-start(s32[4]{0:T(128)S(1)} %get-tuple-element.32.nblk_ref) | copy-start | bytes 52
  106.7 9.8 %copy-start.1 = (f32[4,4,1024]{2,1,0:T(4,128)S(1)}, f32[4,4,1024]{2,1,0:T(4,128)}, u32[]{:S(2)}) copy-start(f32[4,4,1024]{2,1,0:T(4,128)} %fusion.3.pos_ref) | copy-start | bytes 196612
  253.2 54.8 %collective-permute-start.7 = (bf16[1024,1024]{1,0:T(8,128)(2,1)}, bf16[1024,1024]{1,0:T(8,128)(2,1)}, u32[]{:S(2)}, u32[]{:S(2)}) collective-permute-start(bf16[1024,1024]{1,0:T(8,128)(2,1)} %get-tuple-element.14), channel_id=1, source_target_pairs={{0,1},{1,0},{2,3},{3,2},{4,5},{5,4},{6,7},{7,6}} | collective-permute-start | bytes 6291464 | tf_op jit(solution)/shard_map/ppermute | solution.py:483
  295.9 17.3 %collective-permute-start.9 = (bf16[1024,1024]{1,0:T(8,128)(2,1)}, bf16[1024,1024]{1,0:T(8,128)(2,1)}, u32[]{:S(2)}, u32[]{:S(2)}) collective-permute-start(bf16[1024,1024]{1,0:T(8,128)(2,1)} %get-tuple-element.16), channel_id=1, source_target_pairs={{0,1},{1,0},{2,3},{3,2},{4,5},{5,4},{6,7},{7,6}} | collective-permute-start | bytes 6291464 | tf_op jit(solution)/shard_map/ppermute | solution.py:483
  308.0 110.1 %collective-permute-start.6 = (bf16[1024,2048]{1,0:T(8,128)(2,1)}, bf16[1024,2048]{1,0:T(8,128)(2,1)}, u32[]{:S(2)}, u32[]{:S(2)}) collective-permute-start(bf16[1024,2048]{1,0:T(8,128)(2,1)} %side.1), channel_id=1, source_target_pairs={{0,1},{1,0},{2,3},{3,2},{4,5},{5,4},{6,7},{7,6}} | collective-permute-start | bytes 12582920 | tf_op jit(solution)/shard_map/ppermute | solution.py:483
  308.1 5.1 %copy-start = (f32[1024,1024]{1,0:T(8,128)S(1)}, f32[1024,1024]{1,0:T(8,128)}, u32[]{:S(2)}) copy-start(f32[1024,1024]{1,0:T(8,128)} %get-tuple-element.15) | copy-start | bytes 12582916
  313.2 105.0 %collective-permute-start.8 = (bf16[1024,1024]{1,0:T(8,128)(2,1)}, bf16[1024,1024]{1,0:T(8,128)(2,1)S(1)}, u32[]{:S(2)}, u32[]{:S(2)}) collective-permute-start(bf16[1024,1024]{1,0:T(8,128)(2,1)} %add_convert_fusion.2), channel_id=1, source_target_pairs={{0,2},{1,3},{2,0},{3,1},{4,6},{5,7},{6,4},{7,5}} | collective-permute-start | bytes 6291464 | tf_op jit(solution)/shard_map/ppermute | solution.py:483
  317.0 101.2 %collective-permute-start.10 = (bf16[1024,1024]{1,0:T(8,128)(2,1)}, bf16[1024,1024]{1,0:T(8,128)(2,1)}, u32[]{:S(2)}, u32[]{:S(2)}) collective-permute-start(bf16[1024,1024]{1,0:T(8,128)(2,1)} %add_convert_fusion.1), channel_id=1, source_target_pairs={{0,2},{1,3},{2,0},{3,1},{4,6},{5,7},{6,4},{7,5}} | collective-permute-start | bytes 6291464 | tf_op jit(solution)/shard_map/ppermute | solution.py:483

commit v5 on v4

--- a/solution.py
+++ b/solution.py
@@ -169,13 +169,26 @@
     return total
 
 
-def gate_up_body(n_ref, off_ref, nblk_ref, wg_ref, wu_ref, *rest, experts, ready, late, halves):
+def gate_up_body(n_ref, off_ref, nblk_ref, wg_ref, wu_ref, *rest, experts, ready, late, halves, parts):
     sources = ready + late
     pos_refs, rest = rest[:late], rest[late:]
     x_refs, rest = rest[: late * halves], rest[late * halves :]
-    z_refs, (h_ref, xv, zv, zs, p, xsem, zsem) = rest[:ready], rest[ready:]
+    z_refs, (h_ref, xv, zv, zs, p, wb, xsem, zsem, wsem) = rest[:ready], rest[ready:]
     e = pl.program_id(0)
-    width = wg_ref.shape[1]
+    slot = e % 2
+
+    def w_copies(e, part):
+        columns = slice(*parts[part])
+        for i, w_ref in enumerate((wg_ref, wu_ref)):
+            to = wb.at[e % 2, i, :, columns]
+            yield pltpu.make_async_copy(w_ref.at[e, :, columns], to, wsem.at[e % 2, part, i])
+
+    @pl.when(e == 0)
+    def _():
+        for first in range(2):
+            for part in range(len(parts)):
+                for copy in w_copies(first, part):
+                    copy.start()
 
     def x_copy(i, j):
         size = x_refs[0].shape[0]
@@ -224,35 +237,43 @@
         at = at + n
     total = at
 
-    def block(rows):
+    def block(first, last, rows):
         z = zs[:rows, :]
-        whole = width // 256 * 256
-        for c in range(0, whole, 256):
-            g = dot(z, wg_ref[:, c : c + 256])
-            u = dot(z, wu_ref[:, c : c + 256])
-            h_ref[:rows, c : c + 256] = (jax.nn.silu(g) * u).astype(BF16)
-        if whole < width:
-            left = width - whole
-            gu = dot(z, jnp.concatenate([wg_ref[:, whole:], wu_ref[:, whole:]], axis=1))
-            h_ref[:rows, whole:] = (jax.nn.silu(gu[:, :left]) * gu[:, left:]).astype(BF16)
-
-    for rows in range(BLK, zs.shape[0] + 1, BLK):
-        pl.when((total > rows - BLK) & (total <= rows))(functools.partial(block, rows))
+        whole = first + (last - first) // 256 * 256
+        for c in range(first, whole, 256):
+            c = slice(c, c + 256)
+            g = dot(z, wb[slot, 0, :, c])
+            u = dot(z, wb[slot, 1, :, c])
+            h_ref[:rows, c] = (jax.nn.silu(g) * u).astype(BF16)
+        if whole < last:
+            left, c = last - whole, slice(whole, last)
+            gu = dot(z, jnp.concatenate([wb[slot, 0, :, c], wb[slot, 1, :, c]], axis=1))
+            h_ref[:rows, c] = (jax.nn.silu(gu[:, :left]) * gu[:, left:]).astype(BF16)
+
+    for part, (first, last) in enumerate(parts):
+        for copy in w_copies(e, part):
+            copy.wait()
+        for rows in range(BLK, zs.shape[0] + 1, BLK):
+            pl.when((total > rows - BLK) & (total <= rows))(functools.partial(block, first, last, rows))
+
+        @pl.when(e + 2 < experts)
+        def _():
+            for copy in w_copies(e + 2, part):
+                copy.start()
 
 
 def gate_up(n, off, nblk, w_gate, w_up, pos, xs, zs, most):
     experts, d, f = w_gate.shape
     ready, late, halves = len(zs), len(xs), len(xs[0])
     rows, tokens = zs[0].shape[0], sum(v.shape[0] for v in xs[0])
+    half = pl.cdiv(f, 512) * 256
+    parts = ((0, half), (half, f))
     return pl.pallas_call(
-        functools.partial(gate_up_body, experts=experts, ready=ready, late=late, halves=halves),
+        functools.partial(gate_up_body, experts=experts, ready=ready, late=late, halves=halves, parts=parts),
         grid_spec=pltpu.PrefetchScalarGridSpec(
             num_scalar_prefetch=3,
             grid=(experts,),
-            in_specs=[
-                pl.BlockSpec((None, d, f), lambda e, *_: (e, 0, 0)),
-                pl.BlockSpec((None, d, f), lambda e, *_: (e, 0, 0)),
-            ]
+            in_specs=[pl.BlockSpec(memory_space=pl.ANY)] * 2
             + [pl.BlockSpec(p.shape, lambda e, *_: (0, 0)) for p in pos]
             + [pl.BlockSpec(memory_space=pl.ANY)] * (late * halves + ready),
             out_specs=pl.BlockSpec((None, most, f), lambda e, *_: (e, 0, 0)),
@@ -261,8 +282,10 @@
                 pltpu.VMEM((ready + late, rows, d), BF16),
                 pltpu.VMEM((most, d), BF16),
                 pltpu.VMEM((2, BLK, tokens), BF16),
+                pltpu.VMEM((2, 2, d, f), BF16),
                 pltpu.SemaphoreType.DMA((late, halves)),
                 pltpu.SemaphoreType.DMA((ready,)),
+                pltpu.SemaphoreType.DMA((2, len(parts), 2)),
             ],
         ),
         out_shape=jax.ShapeDtypeStruct((experts, most, f), BF16),
@@ -303,28 +326,30 @@
     )(k, pos, gate)
 
 
-def combine(k, c, rows, out):
+def combine(k, mat, rows, out):
     deepest = rows.shape[0] // DEPTH
 
     def whole(depth):
+        groups = rows.shape[1] // 1024
+        both = (((0,), (0,)), ((), ()))
+
         def part(i, _):
-            t = pl.ds(pl.multiple_of(i * 256, 256), 256)
-            both = (((0,), (0,)), ((), ()))
-            for n in range(0, rows.shape[1], 256):
-                n = slice(n, n + 256)
-                out(t, n, lax.dot_general(c[:depth, t], rows[:depth, n], both, preferred_element_type=F32))
+            t = pl.ds(pl.multiple_of(i // groups * 256, 256), 256)
+            for c in range(4):
+                n = pl.ds(pl.multiple_of(i % groups * 1024 + c * 256, 256), 256)
+                out(t, n, lax.dot_general(mat[:depth, t], rows[:depth, n], both, preferred_element_type=F32))
             return _
 
-        lax.fori_loop(0, c.shape[1] // 256, part, 0)
+        lax.fori_loop(0, mat.shape[1] // 256 * groups, part, 0)
 
     pl.when(k < deepest)(functools.partial(whole, (deepest - 1) * DEPTH))
     pl.when(k >= deepest)(functools.partial(whole, deepest * DEPTH))
 
 
-def down_body(n_ref, off_ref, k_ref, wd_ref, h_ref, c_ref, *rest, experts, own, far, group, column):
-    y_refs, kept_ref, (hb, stage, outs, cb, sem, csem, osem) = rest[-far - 8 : -8], rest[-8], rest[-7:]
-    step = pl.program_id(0)
-    sources = own + far
+def down_body(n_ref, off_ref, k_ref, wd_ref, h_ref, c_ref, *rest, experts, own, far, column):
+    y_refs, kept_ref, (hb, stage, outs, cb, wb, sem, csem, osem, wsem) = rest[-far - 10 : -10], rest[-10], rest[-9:]
+    sources, slots = own + far, wb.shape[0]
+    columns = pl.ds(column, outs.shape[2])
 
     def c_copy(i):
         return pltpu.make_async_copy(c_ref.at[own + i], cb.at[i], csem.at[i])
@@ -333,31 +358,34 @@
         r = pl.ds(pl.multiple_of(b * BLK, BLK), BLK)
         return pltpu.make_async_copy(h_ref.at[e, r, :], hb.at[e, r, :], sem.at[e])
 
-    @pl.when(step == 0)
-    def _():
-        def fetch(e, _):
-            def one(b, _):
-                h_copy(e, b).start()
-                return _
-
-            lax.fori_loop(0, pl.cdiv(rows_of(n_ref, e, sources, experts), BLK), one, 0)
+    def w_copy(e):
+        return pltpu.make_async_copy(wd_ref.at[e, :, columns], wb.at[e % slots], wsem.at[e % slots])
+
+    for e in range(slots):
+        w_copy(e).start()
+
+    def fetch(e, _):
+        def one(b, _):
+            h_copy(e, b).start()
             return _
 
-        lax.fori_loop(0, experts, fetch, 0)
-        for i in range(far):
-            c_copy(i).start()
-        zeros = jnp.zeros((ROW, outs.shape[2]), BF16)
-        for q in range(sources):
-            used = off_ref[(q + 1) * experts - 1] + n_ref[(q + 1) * experts - 1]
-
-            def clear(i, _):
-                outs[q, pl.ds(pl.multiple_of(i * ROW, ROW), ROW), :] = zeros
-                return _
-
-            lax.fori_loop(used // ROW, outs.shape[1] // ROW, clear, 0)
-
-    def expert(g, _):
-        e = step * group + g
+        lax.fori_loop(0, pl.cdiv(rows_of(n_ref, e, sources, experts), BLK), one, 0)
+        return _
+
+    lax.fori_loop(0, experts, fetch, 0)
+    for i in range(far):
+        c_copy(i).start()
+    zeros = jnp.zeros((ROW, outs.shape[2]), BF16)
+    for q in range(sources):
+        used = off_ref[(q + 1) * experts - 1] + n_ref[(q + 1) * experts - 1]
+
+        def clear(i, _):
+            outs[q, pl.ds(pl.multiple_of(i * ROW, ROW), ROW), :] = zeros
+            return _
+
+        lax.fori_loop(used // ROW, outs.shape[1] // ROW, clear, 0)
+
+    def expert(e, _):
         total = rows_of(n_ref, e, sources, experts)
         blocks = pl.cdiv(total, BLK)
 
@@ -366,12 +394,17 @@
             return _
 
         lax.fori_loop(0, blocks, arrive, 0)
+        w_copy(e).wait()
 
         def compute(rows):
-            stage[:rows, :] = dot(hb[e, :rows, :], wd_ref[g]).astype(BF16)
+            stage[:rows, :] = dot(hb[e, :rows, :], wb[e % slots]).astype(BF16)
 
         for rows in range(BLK, stage.shape[0] + 1, BLK):
             pl.when(blocks == rows // BLK)(functools.partial(compute, rows))
+
+        @pl.when(e + slots < experts)
+        def more():
+            w_copy(e + slots).start()
 
         at = 0
         for q in range(sources):
@@ -388,38 +421,33 @@
             at = at + n
         return _
 
-    lax.fori_loop(0, group, expert, 0)
-
-    @pl.when(step == experts // group - 1)
-    def _():
-        columns = pl.ds(column, outs.shape[2])
-        leave = pltpu.make_async_copy(outs.at[:own], kept_ref.at[:, :, columns], osem)
-        leave.start()
-        for i in reversed(range(far)):
-            c_copy(i).wait()
-
-            def out(t, c, v):
-                y_refs[i][t, c] = v.astype(y_refs[i].dtype)
-
-            combine(k_ref[own + i], cb.at[i], outs.at[own + i], out)
-        leave.wait()
-
-
-def down(n, off, k, w_down, h, comb, kept, column, columns, own, group=3):
+    lax.fori_loop(0, experts, expert, 0)
+
+    leave = pltpu.make_async_copy(outs.at[:own], kept_ref.at[:, :, columns], osem)
+    leave.start()
+    for i in reversed(range(far)):
+        c_copy(i).wait()
+
+        def out(t, c, v):
+            y_refs[i][t, c] = v.astype(y_refs[i].dtype)
+
+        combine(k_ref[own + i], cb.at[i], outs.at[own + i], out)
+    leave.wait()
+
+
+def down(n, off, k, w_down, h, comb, kept, column, columns, own, slots=6):
     experts, f, d = w_down.shape
     sources, rows, tokens = comb.shape
     far = sources - own
     most = h.shape[1]
     once = dict(pipeline_mode=pl.Buffered(1))
-    at = column // columns
     aliased = [] if kept is None else [kept]
     return pl.pallas_call(
-        functools.partial(down_body, experts=experts, own=own, far=far, group=group, column=column),
+        functools.partial(down_body, experts=experts, own=own, far=far, column=column),
         grid_spec=pltpu.PrefetchScalarGridSpec(
             num_scalar_prefetch=3,
-            grid=(experts // group,),
-            in_specs=[pl.BlockSpec((group, f, columns), lambda e, *_: (e, 0, at))]
-            + [pl.BlockSpec(memory_space=pl.ANY)] * (2 + len(aliased)),
+            grid=(1,),
+            in_specs=[pl.BlockSpec(memory_space=pl.ANY)] * (3 + len(aliased)),
             out_specs=[pl.BlockSpec((tokens, columns), lambda e, *_: (0, 0), **once)] * far
             + [pl.BlockSpec(memory_space=pl.ANY)],
             scratch_shapes=[
@@ -427,9 +455,11 @@
                 pltpu.VMEM((most, columns), BF16),
                 pltpu.VMEM((sources, rows, columns), BF16),
                 pltpu.VMEM((far, rows, tokens), BF16),
+                pltpu.VMEM((slots, f, columns), BF16),
                 pltpu.SemaphoreType.DMA((experts,)),
                 pltpu.SemaphoreType.DMA((far,)),
                 pltpu.SemaphoreType.DMA,
+                pltpu.SemaphoreType.DMA((slots,)),
             ],
         ),
         out_shape=[jax.ShapeDtypeStruct((tokens, columns), F32 if i == 0 else BF16) for i in range(far)]
@@ -524,7 +554,7 @@
         at += columns
     y1 = side_sums(k, comb, kept, 1)
     side = swap(y1, 1)
-    y_shared = shared_expert(x, s_gate, s_up, s_down, cut, chunks, (k, y_shared, comb, kept))
+    y_shared = shared_expert(x, s_gate, s_up, s_down, cut, chunks, (k, y_shared, comb, kept), rows=256)
     return (y_shared + side.astype(F32) + jnp.concatenate(back, axis=1).astype(F32)).astype(BF16)[None, None]
 
 

time: 429 us -> 418 us (0.974)
  Pallas kernels: 289 us -> 281 us
    pallas_call x1, Pallas kernels: 84.1 us -> 77.9 us  [gate_up(): pl.pallas_call(functools.partial(gate_up_body, experts=experts, ready=rea...]
  transfers between devices with their start and end apart: 11 -> 11, of which waited for: 4 -> 4; matrix products, arithmetic and copies ran while one was open for 4% -> 4% of each run, Pallas kernels for 40% -> 41%
where the time goes in v5:
time: 418 us; the launch traced here: 417 us
  Pallas kernels  281 us (67%)
  waiting for transfers between devices  94.7 us (23%)
  other arithmetic  22.8 us (5%)
  starting transfers between devices  16 us (4%)
    pallas_call x2, Pallas kernels, shared_expert(): pl.pallas_call(functools.partial(shared_body, rows=rows, steps=last - fir...  102 us
    ppermute x11, waiting for transfers between devices, swap(): return lax.ppermute(v, 'ep', [(i, i ^ q) for i in range(members)])  94.7 us
    pallas_call x1, Pallas kernels, gate_up(): pl.pallas_call(functools.partial(gate_up_body, experts=experts, ready=rea...  77.9 us
    pallas_call x2, Pallas kernels, down(): pl.pallas_call(functools.partial(down_body, experts=experts, own=own, far...  63.7 us
    pallas_call x2, Pallas kernels, dispatch(): pl.pallas_call(functools.partial(dispatch_body, group=group), grid_spec=p...  17.7 us
    ppermute x11, starting transfers between devices, swap(): return lax.ppermute(v, 'ep', [(i, i ^ q) for i in range(members)])  16 us
    pallas_call x1, Pallas kernels, side_sums(): pl.pallas_call(functools.partial(side_body, member=member), grid_spec=plt...  11.4 us
    pallas_call x1, Pallas kernels, combine_matrices(): pl.pallas_call(comb_body, grid_spec=pltpu.PrefetchScalarGridSpec(num_scal...  9.11 us
  transfers between devices with their start and end apart: 11, of which 4 were waited for; matrix products, arithmetic and copies ran while one was open for 4% of the time, Pallas kernels for 41%

profile of v5, /device:TPU:0, one launch (start us, length us, event | category | flops | bytes accessed | tf_op | source)
XLA Modules:
  0.0 417.1 jit_solution(14257566793147243124)
XLA Ops:
  0.0 3.3 collective-permute-start.3
  3.3 0.0 collective-permute-start.5
  3.3 90.9 %collective-permute-done.3.rest_2_ = bf16[1024,2048]{1,0:T(8,128)(2,1)} collective-permute-done((bf16[1024,2048]{1,0:T(8,128)(2,1)}, bf16[1024,2048]{1,0:T(8,128)(2,1)}, u32[]{:S(2)}, u32[]{:S(2)}) %collective-permute-start.3) | collective-permute-done | bytes 4194336 | tf_op jit(solution)/shard_map/ppermute | solution.py:513
  94.2 0.0 collective-permute-start.4
  94.2 0.7 convert_bitcast_fusion
  94.9 0.7 fusion.14
  95.7 1.8 collective-permute-start.1
  97.4 0.1 collective-permute-start.2
  97.6 0.3 collective-permute-start
  97.9 1.8 collective-permute-done.1
  99.6 1.2 collective-permute-done.2
  100.8 0.9 collective-permute-done
  101.7 0.1 and_bitcast_fusion
  101.9 1.2 select_reduce_fusion.1
  103.0 0.1 fusion.15
  103.2 0.4 select_reduce_fusion.2
  103.5 0.1 copy.18
  103.6 0.6 reshape.48.off_ref
  104.2 0.1 sub.52
  104.3 0.5 select_reduce_fusion
  104.9 0.6 and_select_fusion
  105.4 0.6 fusion.8.gate_ref
  106.1 0.7 fusion.3.pos_ref
  106.7 9.1 %comb.1.c_ref.refs_6_ = bf16[4,1536,1024]{2,1,0:T(8,128)(2,1)} custom-call(s32[4]{0:T(128)} %get-tuple-element.33.k_ref.refs_0_, f32[4,4,1024]{2,1,0:T(4,128)} %fusion.3.pos_ref, f32[4,4,1024]{2,1,0:T(4,128)} %fusion.8.gate_ref), custom_call_target="tpu_custom_call" | custom-call | flops 4194304 | bytes 8388608 | tf_op jit(solution)/shard_map/comb/pallas_call | solution.py:314
  115.9 0.6 fusion.17
  116.4 0.6 slice_bitcast_fusion
  117.1 8.8 %dispatch.2.rest_4_ = bf16[1536,2048]{1,0:T(8,128)(2,1)} custom-call(s32[1]{0:T(128)} %get-tuple-element.31.nblk_ref, f32[4,1024]{1,0:T(4,128)} %get-tuple-element.24.pos_ref, bf16[1024,2048]{1,0:T(8,128)(2,1)} %bitcast.59), custom_call_target="tpu_custom_call" | custom-call | flops 2147483648 | bytes 8388608 | tf_op jit(solution)/shard_map/dispatch/pallas_call | solution.py:146
  125.9 0.5 fusion.12.n_ref
  126.4 0.0 collective-permute-done.5.x_ref
  126.4 8.9 %dispatch.3.rest_5_ = bf16[1536,2048]{1,0:T(8,128)(2,1)} custom-call(s32[1]{0:T(128)} %get-tuple-element.30.nblk_ref, f32[4,1024]{1,0:T(4,128)} %get-tuple-element.23.pos_ref, bf16[1024,2048]{1,0:T(8,128)(2,1)} %collective-permute-done.5.x_ref), custom_call_target="tpu_custom_call" | custom-call | flops 2147483648 | bytes 8388608 | tf_op jit(solution)/shard_map/dispatch/pallas_call | solution.py:146
  135.3 0.0 collective-permute-done.4.rest_3_
  135.3 77.9 %gate_up.1.h_ref = bf16[15,384,1408]{2,1,0:T(8,128)(2,1)} custom-call(s32[60]{0:T(128)} %fusion.12.n_ref, s32[60]{0:T(128)} %reshape.48.off_ref, s32[4]{0:T(128)} %copy-done.2, bf16[15,2048,1408]{2,1,0:T(8,128)(2,1)} %wg_ref.1, bf16[15,2048,1408]{2,1,0:T(8,128)(2,1)} %wu_ref.1, f32[4,1024]{1,0:T(4,128)} %get-tuple-element.26.rest_0_, ...), custom_call_target="tpu_custom_call" | custom-call | flops 44291850240 | bytes 173015040 | tf_op jit(solution)/shard_map/gate_up/pallas_call | solution.py:271
  213.2 31.8 %down.2 = (f32[1024,1024]{1,0:T(8,128)}, bf16[1024,1024]{1,0:T(8,128)(2,1)}, bf16[2,1536,2048]{2,1,0:T(8,128)(2,1)}) custom-call(s32[60]{0:T(128)} %fusion.12.n_ref, s32[60]{0:T(128)} %reshape.48.off_ref, s32[4]{0:T(128)} %get-tuple-element.33.k_ref.refs_0_, bf16[15,1408,2048]{2,1,0:T(8,128)(2,1)} %wd_ref.3, bf16[15,384,1408]{2,1,0:T(8,128)(2,1)} %gate_up.1.h_ref, ...), custom_call_target="tpu_custom_call" | custom-call | flops 11072962560 | bytes 43253760 | tf_op jit(solution)/shard_map/down/pallas_call | solution.py:445
  245.0 6.8 %collective-permute-start.7 = (bf16[1024,1024]{1,0:T(8,128)(2,1)}, bf16[1024,1024]{1,0:T(8,128)(2,1)}, u32[]{:S(2)}, u32[]{:S(2)}) collective-permute-start(bf16[1024,1024]{1,0:T(8,128)(2,1)} %get-tuple-element.14), channel_id=1, source_target_pairs={{0,1},{1,0},{2,3},{3,2},{4,5},{5,4},{6,7},{7,6}} | collective-permute-start | bytes 6291464 | tf_op jit(solution)/shard_map/ppermute | solution.py:513
  251.8 31.9 %down.3 = (f32[1024,1024]{1,0:T(8,128)}, bf16[1024,1024]{1,0:T(8,128)(2,1)}, bf16[2,1536,2048]{2,1,0:T(8,128)(2,1)}) custom-call(s32[60]{0:T(128)} %fusion.12.n_ref, s32[60]{0:T(128)} %reshape.48.off_ref, s32[4]{0:T(128)} %get-tuple-element.33.k_ref.refs_0_, bf16[15,1408,2048]{2,1,0:T(8,128)(2,1)} %wd_ref.3, ...), custom_call_target="tpu_custom_call", output_to_operand_aliasing={{2}: (6, {})} | custom-call | flops 11072962560 | bytes 43253760 | tf_op jit(solution)/shard_map/down/pallas_call | solution.py:445
  283.7 1.7 collective-permute-start.9
  285.4 11.4 %side.1 = bf16[1024,2048]{1,0:T(8,128)(2,1)} custom-call(s32[4]{0:T(128)} %get-tuple-element.33.k_ref.refs_0_, bf16[4,1536,1024]{2,1,0:T(8,128)(2,1)} %comb.1.c_ref.refs_6_, bf16[2,1536,2048]{2,1,0:T(8,128)(2,1)} %get-tuple-element.12.refs_7_.r_ref), custom_call_target="tpu_custom_call" | custom-call | flops 6442450944 | bytes 14680064 | tf_op jit(solution)/shard_map/side/pallas_call | solution.py:484
  296.8 0.0 collective-permute-start.6
  296.8 0.0 collective-permute-done.7
  296.9 5.1 %add_convert_fusion.2 = bf16[1024,1024]{1,0:T(8,128)(2,1)} fusion(f32[1024,1024]{1,0:T(8,128)} %get-tuple-element.13, bf16[1024,1024]{1,0:T(8,128)(2,1)} %collective-permute-done.7), kind=kLoop, calls=%fused_computation.3 | loop fusion | flops 3145728 | bytes 8388608 | tf_op jit(solution)/shard_map/convert_element_type | solution.py:553
  302.0 0.0 collective-permute-start.8
  302.0 0.0 collective-permute-done.9
  302.0 3.8 add_convert_fusion.1
  305.8 2.0 collective-permute-start.10
  307.8 63.5 %shared.2.refs_5_ = f32[1024,2048]{1,0:T(8,128)} custom-call(bf16[1024,2048]{1,0:T(8,128)(2,1)} %bitcast.60, bf16[2048,5632]{1,0:T(8,128)(2,1)} %refs_2_.3, bf16[2048,5632]{1,0:T(8,128)(2,1)} %refs_3_.3, bf16[5632,2048]{1,0:T(8,128)(2,1)} %refs_4_.1), custom_call_target="tpu_custom_call" | custom-call | flops 51539607552 | bytes 50331648 | tf_op jit(solution)/shard_map/shared/pallas_call | solution.py:88
  371.3 38.1 %shared.3 = f32[1024,2048]{1,0:T(8,128)} custom-call(s32[4]{0:T(128)} %get-tuple-element.33.k_ref.refs_0_, bf16[1024,2048]{1,0:T(8,128)(2,1)} %bitcast.61, bf16[2048,5632]{1,0:T(8,128)(2,1)} %refs_2_.3, bf16[2048,5632]{1,0:T(8,128)(2,1)} %refs_3_.3, bf16[5632,2048]{1,0:T(8,128)(2,1)} %refs_4_.1, f32[1024,2048]{1,0:T(8,128)} %shared.2.refs_5_, ...), custom_call_target="tpu_custom_call" | custom-call | flops 19327352832 | bytes 18874368 | tf_op jit(solution)/shard_map/shared/pallas_call | solution.py:88
  409.4 0.0 collective-permute-done.10
  409.4 7.7 %fusion = bf16[1,1,1024,2048]{3,2,1,0:T(8,128)(2,1)} fusion(f32[1024,2048]{1,0:T(8,128)} %shared.3, bf16[1024,2048]{1,0:T(8,128)(2,1)} %collective-permute-done.6, bf16[1024,1024]{1,0:T(8,128)(2,1)} %collective-permute-done.10, bf16[1024,1024]{1,0:T(8,128)(2,1)S(1)} %collective-permute-done.8), kind=kLoop, calls=%fused_computation.1 | loop fusion | flops 16777216 | bytes 20971520 | tf_op jit(solution)/shard_map/broadcast_in_dim | solution.py:558
  (11 shorter events, 0.1 us)
Async XLA Ops:
  0.0 94.2 %collective-permute-start.3 = (bf16[1024,2048]{1,0:T(8,128)(2,1)}, bf16[1024,2048]{1,0:T(8,128)(2,1)}, u32[]{:S(2)}, u32[]{:S(2)}) collective-permute-start(bf16[1024,2048]{1,0:T(8,128)(2,1)} %bitcast.57), channel_id=1, source_target_pairs={{0,2},{1,3},{2,0},{3,1},{4,6},{5,7},{6,4},{7,5}} | collective-permute-start | bytes 12582920 | tf_op jit(solution)/shard_map/ppermute | solution.py:513
  3.3 123.1 %collective-permute-start.5 = (bf16[1024,2048]{1,0:T(8,128)(2,1)}, bf16[1024,2048]{1,0:T(8,128)(2,1)}, u32[]{:S(2)}, u32[]{:S(2)}) collective-permute-start(bf16[1024,2048]{1,0:T(8,128)(2,1)} %bitcast.58), channel_id=1, source_target_pairs={{0,1},{1,0},{2,3},{3,2},{4,5},{5,4},{6,7},{7,6}} | collective-permute-start | bytes 12582920 | tf_op jit(solution)/shard_map/ppermute | solution.py:513
  94.2 41.1 %collective-permute-start.4 = (bf16[1024,2048]{1,0:T(8,128)(2,1)}, bf16[1024,2048]{1,0:T(8,128)(2,1)}, u32[]{:S(2)}, u32[]{:S(2)}) collective-permute-start(bf16[1024,2048]{1,0:T(8,128)(2,1)} %collective-permute-done.3.rest_2_), channel_id=1, source_target_pairs={{0,1},{1,0},{2,3},{3,2},{4,5},{5,4},{6,7},{7,6}} | collective-permute-start | bytes 12582920 | tf_op jit(solution)/shard_map/ppermute | solution.py:513
  95.7 3.9 collective-permute-start.1
  97.4 3.3 collective-permute-start.2
  97.6 4.1 collective-permute-start
  105.4 10.4 %copy-start.2 = (s32[4]{0:T(128)}, s32[4]{0:T(128)S(1)}, u32[]{:S(2)}) copy-start(s32[4]{0:T(128)S(1)} %get-tuple-element.32.nblk_ref) | copy-start | bytes 52
  106.7 9.7 %copy-start.1 = (f32[4,4,1024]{2,1,0:T(4,128)S(1)}, f32[4,4,1024]{2,1,0:T(4,128)}, u32[]{:S(2)}) copy-start(f32[4,4,1024]{2,1,0:T(4,128)} %fusion.3.pos_ref) | copy-start | bytes 196612
  245.0 51.8 %collective-permute-start.7 = (bf16[1024,1024]{1,0:T(8,128)(2,1)}, bf16[1024,1024]{1,0:T(8,128)(2,1)}, u32[]{:S(2)}, u32[]{:S(2)}) collective-permute-start(bf16[1024,1024]{1,0:T(8,128)(2,1)} %get-tuple-element.14), channel_id=1, source_target_pairs={{0,1},{1,0},{2,3},{3,2},{4,5},{5,4},{6,7},{7,6}} | collective-permute-start | bytes 6291464 | tf_op jit(solution)/shard_map/ppermute | solution.py:513
  283.7 18.3 %collective-permute-start.9 = (bf16[1024,1024]{1,0:T(8,128)(2,1)}, bf16[1024,1024]{1,0:T(8,128)(2,1)}, u32[]{:S(2)}, u32[]{:S(2)}) collective-permute-start(bf16[1024,1024]{1,0:T(8,128)(2,1)} %get-tuple-element.16), channel_id=1, source_target_pairs={{0,1},{1,0},{2,3},{3,2},{4,5},{5,4},{6,7},{7,6}} | collective-permute-start | bytes 6291464 | tf_op jit(solution)/shard_map/ppermute | solution.py:513
  296.8 112.6 %collective-permute-start.6 = (bf16[1024,2048]{1,0:T(8,128)(2,1)}, bf16[1024,2048]{1,0:T(8,128)(2,1)}, u32[]{:S(2)}, u32[]{:S(2)}) collective-permute-start(bf16[1024,2048]{1,0:T(8,128)(2,1)} %side.1), channel_id=1, source_target_pairs={{0,1},{1,0},{2,3},{3,2},{4,5},{5,4},{6,7},{7,6}} | collective-permute-start | bytes 12582920 | tf_op jit(solution)/shard_map/ppermute | solution.py:513
  296.8 5.1 %copy-start = (f32[1024,1024]{1,0:T(8,128)S(1)}, f32[1024,1024]{1,0:T(8,128)}, u32[]{:S(2)}) copy-start(f32[1024,1024]{1,0:T(8,128)} %get-tuple-element.15) | copy-start | bytes 12582916
  302.0 107.4 %collective-permute-start.8 = (bf16[1024,1024]{1,0:T(8,128)(2,1)}, bf16[1024,1024]{1,0:T(8,128)(2,1)S(1)}, u32[]{:S(2)}, u32[]{:S(2)}) collective-permute-start(bf16[1024,1024]{1,0:T(8,128)(2,1)} %add_convert_fusion.2), channel_id=1, source_target_pairs={{0,2},{1,3},{2,0},{3,1},{4,6},{5,7},{6,4},{7,5}} | collective-permute-start | bytes 6291464 | tf_op jit(solution)/shard_map/ppermute | solution.py:513
  305.8 103.6 %collective-permute-start.10 = (bf16[1024,1024]{1,0:T(8,128)(2,1)}, bf16[1024,1024]{1,0:T(8,128)(2,1)}, u32[]{:S(2)}, u32[]{:S(2)}) collective-permute-start(bf16[1024,1024]{1,0:T(8,128)(2,1)} %add_convert_fusion.1), channel_id=1, source_target_pairs={{0,2},{1,3},{2,0},{3,1},{4,6},{5,7},{6,4},{7,5}} | collective-permute-start | bytes 6291464 | tf_op jit(solution)/shard_map/ppermute | solution.py:513
